TPU v7x, 512 devices: a whole 4x8x8 slice. The times are simulated.
512 devices in a mesh: dp: 8 (over y_hi, core), ep: 64 (over x, y_lo, z).
Axes of the slice: x: 4, y: 8 (y_hi: 4, y_lo: 2; y = y_hi * 2 + y_lo), z: 8, core: 2. Of those that a mesh axis runs over, the one named last changes fastest.
Arguments:
- hidden_in: bfloat16 [12288, 4096], P(('dp', 'ep')), may hold values from -6 to 6
- expert_ids: int32 [12288, 2], P(('dp', 'ep')), may hold values from 0 to 63, all different within a row; in each aligned block of 24 rows (0 to 23, 24 to 47, ...) at most 2 rows name the same one
- route_logits: float32 [12288, 64], P(('dp', 'ep')), may hold values from -10 to 10
- first_weight: bfloat16 [64, 4096, 1024], P('ep', None, 'dp'), may hold values from -0.09375 to 0.09375
- second_weight: bfloat16 [64, 1024, 4096], P('ep', None, 'dp'), may hold values from -0.1875 to 0.1875
- queries: bfloat16 [12288, 2048], P(('dp', 'ep')), may hold values from -140 to 140
- span_keys: bfloat16 [12288, 2048], P(('dp', 'ep')), may hold values from -7 to 7
- span_values: bfloat16 [12288, 2048], P(('dp', 'ep')), may hold values from -6 to 6
- cache_keys: bfloat16 [512, 72, 2048], P(('dp', 'ep')), may hold values from -6 to 6
- cache_values: bfloat16 [512, 72, 2048], P(('dp', 'ep')), may hold values from -6 to 6
- valid_frames: int32 [512], P(('dp', 'ep')), may hold values from 1 to 3
Outputs:
- mixed: bfloat16 [12288, 4096], P(('dp', 'ep'))
- attended: bfloat16 [12288, 2048], P(('dp', 'ep'))
Inputs may be any that keep to these rules, and one draw needn't show every extreme that they name: `expert_ids`: each token names two different experts. In the rows of one device (24 rows) no expert is named more than 2 times, a bound that some block reaches.
All inputs are finite; a program needn't handle non-finite values.
Results may differ from a plain program's by a relative error of at most 0.0057.
Values may be sent and summed in bfloat16 or wider, within the bound.
No kernel may reach another device: no remote copies, remote signals or barrier semaphores. Data moves between devices by JAX's collectives and lax.ppermute only.
A program may use at most 128 MiB of HBM per device.

v0:
```python
import math

import jax
import jax.numpy as jnp
from jax import lax
from jax.sharding import PartitionSpec as P

HEADS = 16
HEAD_DIM = 128
FRAME_TOK = 24


def activate(pre):
    return jax.nn.gelu(pre, approximate=True).astype(jnp.bfloat16)


def expert_slots(expert_ids):
    flat_ids = expert_ids.reshape(-1)
    assigned = flat_ids.shape[0]
    row_ids = lax.broadcasted_iota(jnp.int32, (assigned, assigned), 0)
    col_ids = lax.broadcasted_iota(jnp.int32, (assigned, assigned), 1)
    same_expert = (flat_ids[:, None] == flat_ids[None, :]) & (col_ids < row_ids)
    return jnp.sum(same_expert.astype(jnp.int32), axis=1).reshape(expert_ids.shape)


def attend(queries, span_keys, span_values, cache_keys, cache_values, valid_count):
    token_count = queries.shape[0]
    cache_len = cache_keys.shape[0]
    key_rows = jnp.concatenate([cache_keys, span_keys], axis=0)
    value_rows = jnp.concatenate([cache_values, span_values], axis=0)
    query_heads = queries.reshape(token_count, HEADS, HEAD_DIM)
    key_heads = key_rows.reshape(-1, HEADS, HEAD_DIM)
    value_heads = value_rows.reshape(-1, HEADS, HEAD_DIM)
    scores = jnp.einsum(
        "thd,khd->htk", query_heads, key_heads, preferred_element_type=jnp.float32
    ) * (1.0 / math.sqrt(HEAD_DIM))
    position = lax.broadcasted_iota(jnp.int32, (key_rows.shape[0],), 0)
    usable = (position >= cache_len) | (position // FRAME_TOK < valid_count)
    scores = jnp.where(usable[None, None, :], scores, -1e30)
    row_max = jnp.max(scores, axis=2, keepdims=True)
    weights = jnp.exp(scores - row_max)
    weights = (weights / jnp.sum(weights, axis=2, keepdims=True)).astype(jnp.bfloat16)
    result = jnp.einsum("htk,khd->thd", weights, value_heads, preferred_element_type=jnp.float32)
    return result.astype(jnp.bfloat16).reshape(token_count, HEADS * HEAD_DIM)


def shards(
    hidden_in,
    expert_ids,
    route_logits,
    first_weight,
    second_weight,
    queries,
    span_keys,
    span_values,
    cache_keys,
    cache_values,
    valid_frames,
):
    tokens, model_width = hidden_in.shape
    experts = lax.axis_size("ep")
    capacity = max(2, 8 * tokens // (3 * experts))
    slots = expert_slots(expert_ids)
    places = expert_ids * capacity + slots
    place_ids = lax.broadcasted_iota(jnp.int32, (tokens, experts * capacity), 1)
    picks = [places[:, column : column + 1] == place_ids for column in range(2)]
    chooser = (picks[0] | picks[1]).astype(jnp.bfloat16)
    dispatch = lax.dot_general(
        chooser, hidden_in, (((0,), (0,)), ((), ())), preferred_element_type=jnp.float32
    )
    dispatch = dispatch.astype(jnp.bfloat16).reshape(experts, capacity, model_width)
    expert_cols = lax.broadcasted_iota(jnp.int32, route_logits.shape, 1)
    chosen = jnp.stack(
        [
            jnp.sum(
                jnp.where(expert_cols == expert_ids[:, column : column + 1], route_logits, 0.0),
                axis=1,
            )
            for column in range(2)
        ],
        axis=1,
    )
    gates = jax.nn.softmax(chosen, axis=1)
    first_local = first_weight[0]
    second_local = second_weight[0]
    received = lax.all_to_all(dispatch, "ep", split_axis=0, concat_axis=0, tiled=True)
    sources, item_count, _ = received.shape
    expert_rows = received.reshape(sources * item_count, model_width)
    hidden = activate(
        jnp.dot(
            expert_rows,
            lax.all_gather(first_local, "dp", axis=1, tiled=True),
            preferred_element_type=jnp.float32,
        )
    )
    result = jnp.dot(
        hidden,
        lax.all_gather(second_local, "dp", axis=1, tiled=True),
        preferred_element_type=jnp.float32,
    ).astype(jnp.bfloat16)
    outputs = result.reshape(sources, item_count, model_width)
    returned = lax.all_to_all(outputs, "ep", split_axis=0, concat_axis=0, tiled=True)
    attended = attend(
        queries, span_keys, span_values, cache_keys[0], cache_values[0], valid_frames[0]
    )
    flat_back = returned.reshape(experts * capacity, model_width)
    running = jnp.zeros((tokens, model_width), jnp.float32)
    for column in range(2):
        picked = jnp.dot(
            picks[column].astype(jnp.bfloat16), flat_back, preferred_element_type=jnp.float32
        )
        running = running + gates[:, column : column + 1] * picked
    mixed = running.astype(jnp.bfloat16)
    return (mixed, attended)


def solution(mesh):
    placed = (
        P(("dp", "ep"), None),
        P(("dp", "ep"), None),
        P(("dp", "ep"), None),
        P("ep", None, "dp"),
        P("ep", None, "dp"),
        P(("dp", "ep"), None),
        P(("dp", "ep"), None),
        P(("dp", "ep"), None),
        P(("dp", "ep"), None, None),
        P(("dp", "ep"), None, None),
        P(("dp", "ep")),
    )
    return jax.shard_map(
        shards,
        mesh=mesh,
        in_specs=placed,
        out_specs=(P(("dp", "ep"), None), P(("dp", "ep"), None)),
        check_vma=False,
    )
```

profile of v0, /device:TPU:2, one launch (start us, length us, event | category | flops | bytes accessed | tf_op | source)
XLA Modules:
  0.0 263.9 jit_solution(3099905430017032602)
XLA Ops:
  7.2 0.0 copy-start
  7.2 0.0 all-gather.7.cloned.1.call-start
  7.2 0.7 all-gather.7.cloned.1.call-update
  7.9 0.0 all-gather.5.cloned.1.call-start
  8.0 0.7 all-gather.5.cloned.1.call-update
  8.7 0.8 copy.35
  9.4 0.1 eq.61
  9.5 0.2 convert_reduce_fusion
  9.7 0.1 reshape.64
  9.8 0.1 copy.36
  9.9 0.7 multiply_add_fusion
  10.6 0.5 convolution_convert_fusion
  11.1 0.7 reshape.65
  11.9 52.7 %all_to_all.10 = bf16[64,2,4096]{2,1,0:T(2,128)(2,1)S(1)} all-to-all(bf16[64,2,4096]{2,1,0:T(2,128)(2,1)S(1)} %reshape.65), channel_id=1, replica_groups=mesh['dp'=8,'ep'=64] {'ep'}, dimensions={0} | all-to-all | bytes 2097152 | tf_op jit(solution)/shard_map/all_to_all | solution.py:86
  64.5 0.4 reshape.66
  64.9 0.0 copy-start.1
  65.0 0.0 copy-start.4
  65.0 45.3 %all-gather.7.cloned.1.call-done = bf16[1,1024,4096]{2,1,0:T(8,128)(2,1)} async-done(((bf16[1,1024,512]{2,1,0:T(8,128)(2,1)}), bf16[1,1024,4096]{2,1,0:T(8,128)(2,1)}) %all-gather.7.cloned.1.call-update) | async-done | bytes 8388624 | tf_op jit(solution)/shard_map/all_gather | solution.py:98
  110.3 95.3 %all-gather.5.cloned.1.call-done = bf16[1,4096,1024]{2,1,0:T(8,128)(2,1)} async-done(((bf16[1,4096,128]{2,1,0:T(8,128)(2,1)}), bf16[1,4096,1024]{2,1,0:T(8,128)(2,1)}) %all-gather.5.cloned.1.call-update) | async-done | bytes 8388624 | tf_op jit(solution)/shard_map/all_gather | solution.py:92
  205.7 8.3 %fusion.5 = bf16[128,4096]{1,0:T(8,128)(2,1)S(1)} fusion(bf16[1,1024,4096]{2,1,0:T(8,128)(2,1)} %all-gather.7.cloned.1.call-done, bf16[128,4096]{1,0:T(8,128)(2,1)S(1)} %reshape.66, bf16[1,4096,1024]{2,1,0:T(8,128)(2,1)} %all-gather.5.cloned.1.call-done), kind=kOutput, calls=%fused_computation.5 | convolution fusion | flops 2149187584 | bytes 18874368 | tf_op jit(solution)/shard_map/dot_general | solution.py:96
  214.0 1.5 reshape.67
  215.5 10.9 %all-to-all-start.1 = ((bf16[64,2,4096]{2,1,0:T(2,128)(2,1)}), bf16[64,2,4096]{2,1,0:T(2,128)(2,1)S(1)}, u32[]{:S(2)}, u32[]{:S(2)}) async-start(bf16[64,2,4096]{2,1,0:T(2,128)(2,1)} %reshape.67), calls=%async_computation.1 | async-start | bytes 2097152 | tf_op jit(solution)/shard_map/all_to_all | solution.py:102
  226.5 0.1 copy.37
  226.6 0.1 copy.39
  227.5 0.5 fusion.70
  227.9 0.3 fusion.14
  228.2 0.7 copy.62
  228.9 0.2 select_reduce_fusion
  229.2 26.1 %all-to-all-done.1 = bf16[64,2,4096]{2,1,0:T(2,128)(2,1)S(1)} async-done(((bf16[64,2,4096]{2,1,0:T(2,128)(2,1)}), bf16[64,2,4096]{2,1,0:T(2,128)(2,1)S(1)}, u32[]{:S(2)}, u32[]{:S(2)}) %all-to-all-start.1) | async-done | bytes 1048608 | tf_op jit(solution)/shard_map/all_to_all | solution.py:102
  255.3 0.4 reshape.68
  255.7 0.3 convolution_multiply_fusion.1
  256.0 1.0 fusion.9
  (24 shorter events, 0.2 us)
Async XLA Ops:
  7.2 3.4 %copy-start = (bf16[24,4096]{1,0:T(8,128)(2,1)S(1)}, bf16[24,4096]{1,0:T(8,128)(2,1)}, u32[]{:S(2)}) copy-start(bf16[24,4096]{1,0:T(8,128)(2,1)} %param.11) | copy-start | bytes 589828
  7.2 103.1 %all-gather.7.cloned.1.call-start = ((), (), s32[]{:S(2)}) async-start(), calls=%async_computation.3 | async-start | bytes 9437184 | tf_op jit(solution)/shard_map/all_gather | solution.py:98
  7.9 197.7 %all-gather.5.cloned.1.call-start = ((), (), s32[]{:S(2)}) async-start(), calls=%async_computation.2 | async-start | bytes 9437184 | tf_op jit(solution)/shard_map/all_gather | solution.py:92
  64.9 161.5 %copy-start.1 = (bf16[1,72,2048]{2,1,0:T(8,128)(2,1)S(1)}, bf16[1,72,2048]{2,1,0:T(8,128)(2,1)}, u32[]{:S(2)}) copy-start(bf16[1,72,2048]{2,1,0:T(8,128)(2,1)} %param.20) | copy-start | bytes 884740
  65.0 161.6 %copy-start.2 = (bf16[1,72,2048]{2,1,0:T(8,128)(2,1)S(1)}, bf16[1,72,2048]{2,1,0:T(8,128)(2,1)}, u32[]{:S(2)}) copy-start(bf16[1,72,2048]{2,1,0:T(8,128)(2,1)} %param.19) | copy-start | bytes 884740
  65.0 162.4 %copy-start.3 = (bf16[24,2048]{1,0:T(8,128)(2,1)S(1)}, bf16[24,2048]{1,0:T(8,128)(2,1)}, u32[]{:S(2)}) copy-start(bf16[24,2048]{1,0:T(8,128)(2,1)} %param.18) | copy-start | bytes 294916
  65.0 162.4 %copy-start.4 = (bf16[24,2048]{1,0:T(8,128)(2,1)S(1)}, bf16[24,2048]{1,0:T(8,128)(2,1)}, u32[]{:S(2)}) copy-start(bf16[24,2048]{1,0:T(8,128)(2,1)} %param.17) | copy-start | bytes 294916
  65.0 162.5 %copy-start.7 = (bf16[24,2048]{1,0:T(8,128)(2,1)S(1)}, bf16[24,2048]{1,0:T(8,128)(2,1)}, u32[]{:S(2)}) copy-start(bf16[24,2048]{1,0:T(8,128)(2,1)} %param.16) | copy-start | bytes 294916
  214.0 14.9 %copy-start.6 = (s32[24,2]{0,1:T(2,128)S(1)}, s32[24,2]{0,1:T(2,128)}, u32[]{:S(2)}) copy-start(s32[24,2]{0,1:T(2,128)} %param.12) | copy-start | bytes 580
  214.0 14.9 %copy-start.5 = (f32[24,64]{1,0:T(8,128)S(1)}, f32[24,64]{1,0:T(8,128)}, u32[]{:S(2)}) copy-start(f32[24,64]{1,0:T(8,128)} %param.13) | copy-start | bytes 18436
  215.5 39.8 %all-to-all-start.1 = ((bf16[64,2,4096]{2,1,0:T(2,128)(2,1)}), bf16[64,2,4096]{2,1,0:T(2,128)(2,1)S(1)}, u32[]{:S(2)}, u32[]{:S(2)}) async-start(bf16[64,2,4096]{2,1,0:T(2,128)(2,1)} %reshape.67), calls=%async_computation.1 | async-start | bytes 2097152 | tf_op jit(solution)/shard_map/all_to_all | solution.py:102
Sparse Core Ops, SparseCore 0:
  10.1 100.1 all-gather.6
  112.4 93.1 all-gather.4
where the time goes:
time: 264 us
  waiting for transfers between devices  168 us (64%)
  blocking collectives  52.7 us (20%)
  between operations  14.9 us (6%)
  starting transfers between devices  11 us (4%)
  matrix products  10.9 us (4%)
  local copies, waits for them, and re-layouts  5.07 us (2%)
    all_gather x1, waiting for transfers between devices, shards(): lax.all_gather(first_local, 'dp', axis=1, tiled=True)  95.3 us
    all_to_all x1, blocking collectives, shards(): lax.all_to_all(dispatch, 'ep', split_axis=0, concat_axis=0, tiled=True)  52.7 us
    all_gather x1, waiting for transfers between devices, shards(): lax.all_gather(second_local, 'dp', axis=1, tiled=True)  45.3 us
    all_to_all x1, waiting for transfers between devices, shards(): lax.all_to_all(outputs, 'ep', split_axis=0, concat_axis=0, tiled=True)  26.1 us
    all_to_all x1, starting transfers between devices, shards(): lax.all_to_all(outputs, 'ep', split_axis=0, concat_axis=0, tiled=True)  10.9 us
    dot_general x1, matrix products, shards(): jnp.dot(hidden, lax.all_gather(second_local, 'dp', axis=1, tiled=True), p...  8.33 us
  transfers between devices with their start and end apart: 3, of which 3 were waited for; matrix products, arithmetic and copies ran while one was open for 2% of the time, Pallas kernels for 0%

commit v1 on v0

--- a/solution.py
+++ b/solution.py
@@ -5,9 +5,22 @@
 from jax import lax
 from jax.sharding import PartitionSpec as P
 
+
 HEADS = 16
 HEAD_DIM = 128
 FRAME_TOK = 24
+
+WEIGHT_MATE = (1, 0, 3, 2)
+ROW_MATE = (3, 2, 1, 0)
+
+
+def ring_swap(mate):
+    return [(2 * ring + core, 2 * mate[ring] + core) for ring in range(4) for core in range(2)]
+
+
+WEIGHT_SWAP = ring_swap(WEIGHT_MATE)
+ROW_SWAP = ring_swap(ROW_MATE)
+CORE_SWAP = [(place, place ^ 1) for place in range(8)]
 
 
 def activate(pre):
@@ -44,6 +57,25 @@
     return result.astype(jnp.bfloat16).reshape(token_count, HEADS * HEAD_DIM)
 
 
+def in_order(swapped, first, second):
+    return [jnp.where(swapped, second, first), jnp.where(swapped, first, second)]
+
+
+def pair_order(ring, core, blocks):
+    own = jnp.concatenate(in_order(core == 1, blocks[0], blocks[1]), axis=1)
+    mate = jnp.concatenate(in_order(core == 1, blocks[2], blocks[3]), axis=1)
+    return jnp.concatenate(in_order(ring % 2 == 1, own, mate), axis=1)
+
+
+def swap(block, pairs):
+    return lax.ppermute(block, "dp", pairs)
+
+
+def both_cores(block):
+    mate = swap(block, WEIGHT_SWAP)
+    return [block, swap(block, CORE_SWAP), mate, swap(mate, CORE_SWAP)]
+
+
 def shards(
     hidden_in,
     expert_ids,
@@ -59,16 +91,15 @@
 ):
     tokens, model_width = hidden_in.shape
     experts = lax.axis_size("ep")
-    capacity = max(2, 8 * tokens // (3 * experts))
+    place = lax.axis_index("dp")
+    ring, core = place // 2, place % 2
+    upper = ring // 2
+
+    first_parts = both_cores(first_weight[0])
+    second_parts = both_cores(second_weight[0])
+
     slots = expert_slots(expert_ids)
-    places = expert_ids * capacity + slots
-    place_ids = lax.broadcasted_iota(jnp.int32, (tokens, experts * capacity), 1)
-    picks = [places[:, column : column + 1] == place_ids for column in range(2)]
-    chooser = (picks[0] | picks[1]).astype(jnp.bfloat16)
-    dispatch = lax.dot_general(
-        chooser, hidden_in, (((0,), (0,)), ((), ())), preferred_element_type=jnp.float32
-    )
-    dispatch = dispatch.astype(jnp.bfloat16).reshape(experts, capacity, model_width)
+    places = expert_ids * 4 + upper * 2 + slots
     expert_cols = lax.broadcasted_iota(jnp.int32, route_logits.shape, 1)
     chosen = jnp.stack(
         [
@@ -81,36 +112,59 @@
         axis=1,
     )
     gates = jax.nn.softmax(chosen, axis=1)
-    first_local = first_weight[0]
-    second_local = second_weight[0]
+    notes = jnp.concatenate([places.astype(jnp.float32), gates], axis=1)
+    both_notes = jnp.concatenate([notes, swap(notes, ROW_SWAP)], axis=0)
+    both_places = both_notes[:, :2].astype(jnp.int32)
+    both_gates = both_notes[:, 2:]
+    both_hidden = jnp.concatenate([hidden_in, swap(hidden_in, ROW_SWAP)], axis=0)
+    place_ids = lax.broadcasted_iota(jnp.int32, (2 * tokens, experts * 4), 1)
+    picks = [both_places[:, column : column + 1] == place_ids for column in range(2)]
+    chooser = (picks[0] | picks[1]).astype(jnp.bfloat16)
+
+    dispatch = lax.dot_general(
+        chooser, both_hidden, (((0,), (0,)), ((), ())), preferred_element_type=jnp.float32
+    )
+    dispatch = dispatch.astype(jnp.bfloat16).reshape(experts, 4, model_width)
     received = lax.all_to_all(dispatch, "ep", split_axis=0, concat_axis=0, tiled=True)
-    sources, item_count, _ = received.shape
-    expert_rows = received.reshape(sources * item_count, model_width)
-    hidden = activate(
-        jnp.dot(
-            expert_rows,
-            lax.all_gather(first_local, "dp", axis=1, tiled=True),
-            preferred_element_type=jnp.float32,
-        )
+    expert_rows = received.reshape(experts * 4, model_width)
+
+    act = pair_order(
+        ring,
+        core,
+        [
+            activate(jnp.dot(expert_rows, part, preferred_element_type=jnp.float32))
+            for part in first_parts
+        ],
     )
-    result = jnp.dot(
-        hidden,
-        lax.all_gather(second_local, "dp", axis=1, tiled=True),
-        preferred_element_type=jnp.float32,
-    ).astype(jnp.bfloat16)
-    outputs = result.reshape(sources, item_count, model_width)
-    returned = lax.all_to_all(outputs, "ep", split_axis=0, concat_axis=0, tiled=True)
+    other_act = swap(act, ROW_SWAP)
+    all_act = jnp.concatenate(in_order(upper == 1, act, other_act), axis=1)
+
+    outputs = jnp.concatenate(
+        [
+            jnp.dot(all_act, part, preferred_element_type=jnp.float32).astype(jnp.bfloat16)
+            for part in second_parts
+        ],
+        axis=1,
+    )
+    returned = lax.all_to_all(
+        outputs.reshape(experts, 4, -1), "ep", split_axis=0, concat_axis=0, tiled=True
+    )
+    flat_back = returned.reshape(experts * 4, -1)
+
     attended = attend(
         queries, span_keys, span_values, cache_keys[0], cache_values[0], valid_frames[0]
     )
-    flat_back = returned.reshape(experts * capacity, model_width)
-    running = jnp.zeros((tokens, model_width), jnp.float32)
+
+    running = jnp.zeros((2 * tokens, flat_back.shape[1]), jnp.float32)
     for column in range(2):
         picked = jnp.dot(
             picks[column].astype(jnp.bfloat16), flat_back, preferred_element_type=jnp.float32
         )
-        running = running + gates[:, column : column + 1] * picked
+        running = running + both_gates[:, column : column + 1] * picked
     mixed = running.astype(jnp.bfloat16)
+    mixed = pair_order(ring, core, jnp.split(mixed, 4, axis=1))
+    other_mixed = swap(mixed[tokens:], ROW_SWAP)
+    mixed = jnp.concatenate(in_order(upper == 1, mixed[:tokens], other_mixed), axis=1)
     return (mixed, attended)
 
 

time: 264 us -> 209 us (0.79)
  the two profiles are of different devices: /device:TPU:2 before, /device:TPU:10 now
where the time goes in v1:
time: 209 us; the launch traced here: 208 us
  waiting for transfers between devices  118 us (56%)
  starting transfers between devices  60.2 us (29%)
  matrix products  15.7 us (8%)
  local copies, waits for them, and re-layouts  9.03 us (4%)
  other arithmetic  2.99 us (1%)
    ppermute x10, waiting for transfers between devices, swap(): return lax.ppermute(block, 'dp', pairs)  90.3 us
    ppermute x10, starting transfers between devices, swap(): return lax.ppermute(block, 'dp', pairs)  31.5 us
    all_to_all x1, waiting for transfers between devices, shards(): lax.all_to_all(outputs.reshape(experts, 4, -1), 'ep', split_axis=0, conca...  27.5 us
    all_to_all x1, starting transfers between devices, shards(): lax.all_to_all(dispatch, 'ep', split_axis=0, concat_axis=0, tiled=True)  15.1 us
    all_to_all x1, starting transfers between devices, shards(): lax.all_to_all(outputs.reshape(experts, 4, -1), 'ep', split_axis=0, conca...  13.6 us
    dot_general x4, matrix products, shards(): jnp.dot(expert_rows, part, preferred_element_type=jnp.float32)  7.08 us
    dot_general x4, matrix products, shards(): jnp.dot(all_act, part, preferred_element_type=jnp.float32)  5.48 us
  transfers between devices with their start and end apart: 12, of which 5 were waited for; matrix products, arithmetic and copies ran while one was open for 8% of the time, Pallas kernels for 0%

profile of v1, /device:TPU:10, one launch (start us, length us, event | category | flops | bytes accessed | tf_op | source)
XLA Modules:
  0.0 207.5 jit_solution(2986595793742103601)
XLA Ops:
  0.7 0.8 copy.54
  1.5 0.8 slice_bitcast_fusion.5
  2.7 0.9 select_reduce_fusion
  4.3 5.3 %collective-permute-start = (f32[24,4]{0,1:T(4,128)S(1)}, f32[24,4]{0,1:T(4,128)S(1)}, u32[]{:S(2)}, u32[]{:S(2)}) collective-permute-start(f32[24,4]{0,1:T(4,128)S(1)} %pad_maximum_fusion.9), channel_id=1, source_target_pairs={{0,384},{64,448},{128,256},{192,320},{256,128},{320,192},{384,0},{... | collective-permute-start | bytes 1160 | tf_op jit(solution)/shard_map/ppermute | solution.py:71
  9.6 2.7 %collective-permute-start.1 = (bf16[24,4096]{1,0:T(8,128)(2,1)}, bf16[24,4096]{1,0:T(8,128)(2,1)S(1)}, u32[]{:S(2)}, u32[]{:S(2)}) collective-permute-start(bf16[24,4096]{1,0:T(8,128)(2,1)} %param.11), channel_id=1, source_target_pairs={{0,384},{64,448},{128,256},{192,320},{256,128},{320,192},{384,0},{... | collective-permute-start | bytes 589832 | tf_op jit(solution)/shard_map/ppermute | solution.py:71
  12.4 12.0 %collective-permute-done.1 = bf16[24,4096]{1,0:T(8,128)(2,1)S(1)} collective-permute-done((bf16[24,4096]{1,0:T(8,128)(2,1)}, bf16[24,4096]{1,0:T(8,128)(2,1)S(1)}, u32[]{:S(2)}, u32[]{:S(2)}) %collective-permute-start.1) | collective-permute-done | bytes 196640 | tf_op jit(solution)/shard_map/ppermute | solution.py:71
  24.4 1.7 convolution_convert_fusion
  26.1 2.2 %reshape.65 = bf16[64,4,4096]{2,1,0:T(4,128)(2,1)} reshape(bf16[256,4096]{1,0:T(8,128)(2,1)S(1)} %convolution_convert_fusion) | data formatting | bytes 4194304 | tf_op jit(solution)/shard_map/reshape | solution.py:127
  28.3 15.1 %all-to-all-start = ((bf16[64,4,4096]{2,1,0:T(4,128)(2,1)}), bf16[64,4,4096]{2,1,0:T(4,128)(2,1)}, u32[]{:S(2)}, u32[]{:S(2)}) async-start(bf16[64,4,4096]{2,1,0:T(4,128)(2,1)} %reshape.65), calls=%async_computation | async-start | bytes 4194304 | tf_op jit(solution)/shard_map/all_to_all | solution.py:128
  43.5 3.9 %collective-permute-start.2 = (bf16[4096,128]{1,0:T(8,128)(2,1)S(1)}, bf16[4096,128]{1,0:T(8,128)(2,1)}, u32[]{:S(2)}, u32[]{:S(2)}) collective-permute-start(bf16[4096,128]{1,0:T(8,128)(2,1)S(1)} %bitcast.82), channel_id=1, source_target_pairs={{0,128},{64,192},{128,0},{192,64},{256,384},{320,448},{384,256},{4... | collective-permute-start | bytes 3145736 | tf_op jit(solution)/shard_map/ppermute | solution.py:71
  47.4 1.9 collective-permute-start.4
  49.4 42.5 %collective-permute-done.2 = bf16[4096,128]{1,0:T(8,128)(2,1)} collective-permute-done((bf16[4096,128]{1,0:T(8,128)(2,1)S(1)}, bf16[4096,128]{1,0:T(8,128)(2,1)}, u32[]{:S(2)}, u32[]{:S(2)}) %collective-permute-start.2) | collective-permute-done | bytes 1048608 | tf_op jit(solution)/shard_map/ppermute | solution.py:71
  91.9 1.9 collective-permute-start.3
  93.8 2.4 %collective-permute-start.6 = (bf16[1024,512]{1,0:T(8,128)(2,1)}, bf16[1024,512]{1,0:T(8,128)(2,1)}, u32[]{:S(2)}, u32[]{:S(2)}) collective-permute-start(bf16[1024,512]{1,0:T(8,128)(2,1)} %bitcast.8), channel_id=1, source_target_pairs={{0,64},{64,0},{128,192},{192,128},{256,320},{320,256},{384,448},{4... | collective-permute-start | bytes 3145736 | tf_op jit(solution)/shard_map/ppermute | solution.py:71
  96.2 5.4 %collective-permute-start.7 = (bf16[1024,512]{1,0:T(8,128)(2,1)}, bf16[1024,512]{1,0:T(8,128)(2,1)}, u32[]{:S(2)}, u32[]{:S(2)}) collective-permute-start(bf16[1024,512]{1,0:T(8,128)(2,1)} %bitcast.8), channel_id=1, source_target_pairs={{0,128},{64,192},{128,0},{192,64},{256,384},{320,448},{384,256},{4... | collective-permute-start | bytes 3145736 | tf_op jit(solution)/shard_map/ppermute | solution.py:71
  101.6 2.5 %reshape.66 = bf16[256,4096]{1,0:T(8,128)(2,1)S(1)} reshape(bf16[64,4,4096]{2,1,0:T(4,128)(2,1)} %all-to-all-done) | data formatting | bytes 4194304 | tf_op jit(solution)/shard_map/reshape | solution.py:129
  104.2 0.9 fusion.46
  105.1 2.1 %broadcast_select_fusion.9 = (bf16[256,128]{0,1:T(8,128)(2,1)S(1)}, bf16[256,128]{0,1:T(8,128)(2,1)S(1)}) fusion(bf16[256,128]{0,1:T(8,128)(2,1)S(1)} %fusion.46, pred[]{:T(512)S(6)} %eq.75, bf16[256,4096]{1,0:T(8,128)(2,1)S(1)} %reshape.66, bf16[4096,128]{1,0:T(8,128)(2,1)} %collective-permute-done.4), kind=kOutput, calls=%fused_computation.87 | convolution fusion | flops 268795904 | bytes 3342337 | tf_op jit(solution)/shard_map/dot_general | solution.py:135
  107.2 2.0 fusion.88
  109.2 2.1 %broadcast_select_fusion.11 = (bf16[256,128]{0,1:T(8,128)(2,1)S(1)}, bf16[256,128]{0,1:T(8,128)(2,1)S(1)}) fusion(pred[]{:T(512)S(6)} %eq.75, f32[256,128]{0,1:T(8,128)S(1)} %fusion.88, bf16[256,4096]{1,0:T(8,128)(2,1)S(1)} %reshape.66, bf16[4096,128]{1,0:T(8,128)(2,1)} %collective-permute-done.3), kind=kOutput, calls=%fused_computation.89 | convolution fusion | flops 269090816 | bytes 3407873 | tf_op jit(solution)/shard_map/dot_general | solution.py:135
  111.4 1.9 collective-permute-start.5
  113.3 31.2 %collective-permute-done.7 = bf16[1024,512]{1,0:T(8,128)(2,1)} collective-permute-done((bf16[1024,512]{1,0:T(8,128)(2,1)}, bf16[1024,512]{1,0:T(8,128)(2,1)}, u32[]{:S(2)}, u32[]{:S(2)}) %collective-permute-start.7) | collective-permute-done | bytes 1048608 | tf_op jit(solution)/shard_map/ppermute | solution.py:71
  144.6 1.9 collective-permute-start.8
  146.6 1.7 convolution_convert_fusion.4
  148.3 1.7 convolution_convert_fusion.2
  150.0 1.7 convolution_convert_fusion.3
  152.3 1.2 reshape.67
  153.5 13.6 %all-to-all-start.1 = ((bf16[64,4,2048]{2,1,0:T(4,128)(2,1)}), bf16[64,4,2048]{2,1,0:T(4,128)(2,1)S(1)}, u32[]{:S(2)}, u32[]{:S(2)}) async-start(bf16[64,4,2048]{2,1,0:T(4,128)(2,1)} %reshape.67), calls=%async_computation.1 | async-start | bytes 2097152 | tf_op jit(solution)/shard_map/all_to_all | solution.py:149
  168.6 27.5 %all-to-all-done.1 = bf16[64,4,2048]{2,1,0:T(4,128)(2,1)S(1)} async-done(((bf16[64,4,2048]{2,1,0:T(4,128)(2,1)}), bf16[64,4,2048]{2,1,0:T(4,128)(2,1)S(1)}, u32[]{:S(2)}, u32[]{:S(2)}) %all-to-all-start.1) | async-done | bytes 1048608 | tf_op jit(solution)/shard_map/all_to_all | solution.py:149
  197.1 4.1 %collective-permute-start.9 = (bf16[24,2048]{1,0:T(8,128)(2,1)S(1)}, bf16[24,2048]{1,0:T(8,128)(2,1)S(1)}, u32[]{:S(2)}, u32[]{:S(2)}) collective-permute-start(bf16[24,2048]{1,0:T(8,128)(2,1)S(1)} %fusion.47), channel_id=1, source_target_pairs={{0,384},{64,448},{128,256},{192,320},{256,128},{320,192},{384,0},{... | collective-permute-start | bytes 294920 | tf_op jit(solution)/shard_map/ppermute | solution.py:71
  202.2 4.6 %collective-permute-done.9 = bf16[24,2048]{1,0:T(8,128)(2,1)S(1)} collective-permute-done((bf16[24,2048]{1,0:T(8,128)(2,1)S(1)}, bf16[24,2048]{1,0:T(8,128)(2,1)S(1)}, u32[]{:S(2)}, u32[]{:S(2)}) %collective-permute-start.9) | collective-permute-done | bytes 98336 | tf_op jit(solution)/shard_map/ppermute | solution.py:71
  206.8 0.7 pad_maximum_fusion.3
  (54 shorter events, 4.8 us)
Async XLA Ops:
  0.6 167.4 %copy-start = (bf16[24,2048]{1,0:T(8,128)(2,1)S(1)}, bf16[24,2048]{1,0:T(8,128)(2,1)}, u32[]{:S(2)}) copy-start(bf16[24,2048]{1,0:T(8,128)(2,1)} %param.17) | copy-start | bytes 294916
  4.3 8.0 %collective-permute-start = (f32[24,4]{0,1:T(4,128)S(1)}, f32[24,4]{0,1:T(4,128)S(1)}, u32[]{:S(2)}, u32[]{:S(2)}) collective-permute-start(f32[24,4]{0,1:T(4,128)S(1)} %pad_maximum_fusion.9), channel_id=1, source_target_pairs={{0,384},{64,448},{128,256},{192,320},{256,128},{320,192},{384,0},{... | collective-permute-start | bytes 1160 | tf_op jit(solution)/shard_map/ppermute | solution.py:71
  9.6 14.8 %collective-permute-start.1 = (bf16[24,4096]{1,0:T(8,128)(2,1)}, bf16[24,4096]{1,0:T(8,128)(2,1)S(1)}, u32[]{:S(2)}, u32[]{:S(2)}) collective-permute-start(bf16[24,4096]{1,0:T(8,128)(2,1)} %param.11), channel_id=1, source_target_pairs={{0,384},{64,448},{128,256},{192,320},{256,128},{320,192},{384,0},{... | collective-permute-start | bytes 589832 | tf_op jit(solution)/shard_map/ppermute | solution.py:71
  28.3 15.1 %copy-start.1 = (bf16[1,4096,128]{2,1,0:T(8,128)(2,1)S(1)}, bf16[1,4096,128]{2,1,0:T(8,128)(2,1)}, u32[]{:S(2)}) copy-start(bf16[1,4096,128]{2,1,0:T(8,128)(2,1)} %param.14) | copy-start | bytes 3145732
  28.3 73.3 %all-to-all-start = ((bf16[64,4,4096]{2,1,0:T(4,128)(2,1)}), bf16[64,4,4096]{2,1,0:T(4,128)(2,1)}, u32[]{:S(2)}, u32[]{:S(2)}) async-start(bf16[64,4,4096]{2,1,0:T(4,128)(2,1)} %reshape.65), calls=%async_computation | async-start | bytes 4194304 | tf_op jit(solution)/shard_map/all_to_all | solution.py:128
  43.5 48.4 %collective-permute-start.2 = (bf16[4096,128]{1,0:T(8,128)(2,1)S(1)}, bf16[4096,128]{1,0:T(8,128)(2,1)}, u32[]{:S(2)}, u32[]{:S(2)}) collective-permute-start(bf16[4096,128]{1,0:T(8,128)(2,1)S(1)} %bitcast.82), channel_id=1, source_target_pairs={{0,128},{64,192},{128,0},{192,64},{256,384},{320,448},{384,256},{4... | collective-permute-start | bytes 3145736 | tf_op jit(solution)/shard_map/ppermute | solution.py:71
  47.4 57.6 %collective-permute-start.4 = (bf16[4096,128]{1,0:T(8,128)(2,1)S(1)}, bf16[4096,128]{1,0:T(8,128)(2,1)}, u32[]{:S(2)}, u32[]{:S(2)}) collective-permute-start(bf16[4096,128]{1,0:T(8,128)(2,1)S(1)} %bitcast.83), channel_id=1, source_target_pairs={{0,64},{64,0},{128,192},{192,128},{256,320},{320,256},{384,448},{4... | collective-permute-start | bytes 3145736 | tf_op jit(solution)/shard_map/ppermute | solution.py:71
  91.9 17.4 %collective-permute-start.3 = (bf16[4096,128]{1,0:T(8,128)(2,1)}, bf16[4096,128]{1,0:T(8,128)(2,1)}, u32[]{:S(2)}, u32[]{:S(2)}) collective-permute-start(bf16[4096,128]{1,0:T(8,128)(2,1)} %collective-permute-done.2), channel_id=1, source_target_pairs={{0,64},{64,0},{128,192},{192,128},{256,320},{320,256},{384,448},{4... | collective-permute-start | bytes 3145736 | tf_op jit(solution)/shard_map/ppermute | solution.py:71
  93.8 56.2 %collective-permute-start.6 = (bf16[1024,512]{1,0:T(8,128)(2,1)}, bf16[1024,512]{1,0:T(8,128)(2,1)}, u32[]{:S(2)}, u32[]{:S(2)}) collective-permute-start(bf16[1024,512]{1,0:T(8,128)(2,1)} %bitcast.8), channel_id=1, source_target_pairs={{0,64},{64,0},{128,192},{192,128},{256,320},{320,256},{384,448},{4... | collective-permute-start | bytes 3145736 | tf_op jit(solution)/shard_map/ppermute | solution.py:71
  96.2 48.4 %collective-permute-start.7 = (bf16[1024,512]{1,0:T(8,128)(2,1)}, bf16[1024,512]{1,0:T(8,128)(2,1)}, u32[]{:S(2)}, u32[]{:S(2)}) collective-permute-start(bf16[1024,512]{1,0:T(8,128)(2,1)} %bitcast.8), channel_id=1, source_target_pairs={{0,128},{64,192},{128,0},{192,64},{256,384},{320,448},{384,256},{4... | collective-permute-start | bytes 3145736 | tf_op jit(solution)/shard_map/ppermute | solution.py:71
  111.4 35.1 %collective-permute-start.5 = (bf16[256,512]{0,1:T(8,128)(2,1)S(1)}, bf16[256,512]{0,1:T(8,128)(2,1)S(1)}, u32[]{:S(2)}, u32[]{:S(2)}) collective-permute-start(bf16[256,512]{0,1:T(8,128)(2,1)S(1)} %pad_maximum_fusion.2), channel_id=1, source_target_pairs={{0,384},{64,448},{128,256},{192,320},{256,128},{320,192},{384,0},{... | collective-permute-start | bytes 786440 | tf_op jit(solution)/shard_map/ppermute | solution.py:71
  144.6 7.1 %collective-permute-start.8 = (bf16[1024,512]{1,0:T(8,128)(2,1)}, bf16[1024,512]{1,0:T(8,128)(2,1)S(1)}, u32[]{:S(2)}, u32[]{:S(2)}) collective-permute-start(bf16[1024,512]{1,0:T(8,128)(2,1)} %collective-permute-done.7), channel_id=1, source_target_pairs={{0,64},{64,0},{128,192},{192,128},{256,320},{320,256},{384,448},{4... | collective-permute-start | bytes 3145736 | tf_op jit(solution)/shard_map/ppermute | solution.py:71
  152.3 14.8 %copy-start.2 = (bf16[1,72,2048]{2,1,0:T(8,128)(2,1)S(1)}, bf16[1,72,2048]{2,1,0:T(8,128)(2,1)}, u32[]{:S(2)}) copy-start(bf16[1,72,2048]{2,1,0:T(8,128)(2,1)} %param.19) | copy-start | bytes 884740
  153.5 14.4 %copy-start.3 = (bf16[1,72,2048]{2,1,0:T(8,128)(2,1)S(1)}, bf16[1,72,2048]{2,1,0:T(8,128)(2,1)}, u32[]{:S(2)}) copy-start(bf16[1,72,2048]{2,1,0:T(8,128)(2,1)} %param.20) | copy-start | bytes 884740
  153.5 14.6 %copy-start.4 = (bf16[24,2048]{1,0:T(8,128)(2,1)S(1)}, bf16[24,2048]{1,0:T(8,128)(2,1)}, u32[]{:S(2)}) copy-start(bf16[24,2048]{1,0:T(8,128)(2,1)} %param.18) | copy-start | bytes 294916
  153.5 14.6 %copy-start.5 = (bf16[24,2048]{1,0:T(8,128)(2,1)S(1)}, bf16[24,2048]{1,0:T(8,128)(2,1)}, u32[]{:S(2)}) copy-start(bf16[24,2048]{1,0:T(8,128)(2,1)} %param.16) | copy-start | bytes 294916
  153.5 42.6 %all-to-all-start.1 = ((bf16[64,4,2048]{2,1,0:T(4,128)(2,1)}), bf16[64,4,2048]{2,1,0:T(4,128)(2,1)S(1)}, u32[]{:S(2)}, u32[]{:S(2)}) async-start(bf16[64,4,2048]{2,1,0:T(4,128)(2,1)} %reshape.67), calls=%async_computation.1 | async-start | bytes 2097152 | tf_op jit(solution)/shard_map/all_to_all | solution.py:149
  197.1 9.7 %collective-permute-start.9 = (bf16[24,2048]{1,0:T(8,128)(2,1)S(1)}, bf16[24,2048]{1,0:T(8,128)(2,1)S(1)}, u32[]{:S(2)}, u32[]{:S(2)}) collective-permute-start(bf16[24,2048]{1,0:T(8,128)(2,1)S(1)} %fusion.47), channel_id=1, source_target_pairs={{0,384},{64,448},{128,256},{192,320},{256,128},{320,192},{384,0},{... | collective-permute-start | bytes 294920 | tf_op jit(solution)/shard_map/ppermute | solution.py:71

commit v2 on v0

--- a/solution.py
+++ b/solution.py
@@ -3,11 +3,17 @@
 import jax
 import jax.numpy as jnp
 from jax import lax
+from jax.experimental import pallas as pl
+from jax.experimental.pallas import tpu as pltpu
 from jax.sharding import PartitionSpec as P
+
 
 HEADS = 16
 HEAD_DIM = 128
 FRAME_TOK = 24
+
+CORE_FLIP, FIRST_FLIP, ROW_FLIP, SECOND_FLIP = 1, 2, 4, 6
+ACT_BLOCK = 256
 
 
 def activate(pre):
@@ -44,6 +50,158 @@
     return result.astype(jnp.bfloat16).reshape(token_count, HEADS * HEAD_DIM)
 
 
+def swap(block, flip):
+    return lax.ppermute(block, "dp", [(place, place ^ flip) for place in range(8)])
+
+
+def four_parts(block, flip, pieces):
+    mate = jnp.concatenate(
+        [swap(piece, flip) for piece in jnp.split(block, pieces, axis=0)],
+        axis=0,
+    )
+    return [block, swap(block, CORE_FLIP), mate, swap(mate, CORE_FLIP)]
+
+
+def dispatch_kernel(choose_ref, own_ref, mate_ref, out_ref):
+    choose = choose_ref[...]
+    half = choose.shape[1] // 2
+    rows = jnp.dot(choose[:, :half], own_ref[...], preferred_element_type=jnp.float32)
+    rows += jnp.dot(choose[:, half:], mate_ref[...], preferred_element_type=jnp.float32)
+    out_ref[...] = rows.astype(jnp.bfloat16).reshape(out_ref.shape)
+
+
+def dispatch_rows(choose, own, mate, items):
+    count, width = choose.shape[0], own.shape[1]
+    tokens, step = own.shape[0], 1024
+    return pl.pallas_call(
+        dispatch_kernel,
+        grid=(width // step,),
+        in_specs=[pl.BlockSpec(choose.shape, lambda i: (0, 0))]
+        + [pl.BlockSpec((tokens, step), lambda i: (0, i))] * 2,
+        out_specs=pl.BlockSpec((items, count // items, step), lambda i: (0, 0, i)),
+        out_shape=jax.ShapeDtypeStruct((items, count // items, width), jnp.bfloat16),
+        name="dispatch_rows",
+    )(choose, own, mate)
+
+
+def first_kernel(place_ref, rows_ref, left_ref, right_ref, act_ref, sums):
+    step = pl.program_id(0)
+
+    @pl.when(step == 0)
+    def _():
+        sums[...] = jnp.zeros_like(sums)
+
+    rows = rows_ref[...].reshape(sums.shape[0], -1)
+    wide = jnp.concatenate([left_ref[...], right_ref[...]], axis=1)
+    sums[...] += jnp.dot(rows, wide, preferred_element_type=jnp.float32)
+
+    @pl.when(step == pl.num_programs(0) - 1)
+    def _():
+        odd = place_ref[0] % 2 == 1
+        half = ACT_BLOCK // 2
+        act = activate(sums[...])
+        left, right = act[:, :half], act[:, half:]
+        act_ref[:, :half] = jnp.where(odd, right, left)
+        act_ref[:, half:] = jnp.where(odd, left, right)
+
+
+def first_stage(place, rows, left, right):
+    items, slots, depth = rows.shape
+    count, wide, step = items * slots, left.shape[1], 1024
+    return pl.pallas_call(
+        first_kernel,
+        grid_spec=pltpu.PrefetchScalarGridSpec(
+            num_scalar_prefetch=1,
+            grid=(depth // step,),
+            in_specs=[pl.BlockSpec((items, slots, step), lambda i, p: (0, 0, i))]
+            + [pl.BlockSpec((step, wide), lambda i, p: (i, 0))] * 2,
+            out_specs=pl.BlockSpec((count, ACT_BLOCK), lambda i, p: (0, 0)),
+            scratch_shapes=[pltpu.VMEM((count, ACT_BLOCK), jnp.float32)],
+        ),
+        out_shape=jax.ShapeDtypeStruct((count, ACT_BLOCK), jnp.bfloat16),
+        name="first_stage",
+    )(place, rows, left, right)
+
+
+def near_kernel(place_ref, even_ref, odd_ref, *refs):
+    part_refs, sums_ref = refs[:4], refs[4]
+    step = pl.program_id(0)
+    wide = part_refs[0].shape[1]
+    act = jnp.where(step == 0, even_ref[...], odd_ref[...])
+
+    @pl.when(step == 0)
+    def _():
+        for index, part_ref in enumerate(part_refs):
+            sums_ref[:, index * wide : (index + 1) * wide] = jnp.dot(
+                act, part_ref[...], preferred_element_type=jnp.float32
+            )
+
+    @pl.when(step > 0)
+    def _():
+        for index, part_ref in enumerate(part_refs):
+            sums_ref[:, index * wide : (index + 1) * wide] += jnp.dot(
+                act, part_ref[...], preferred_element_type=jnp.float32
+            )
+
+
+def far_kernel(place_ref, even_ref, odd_ref, *refs):
+    part_refs, before_ref, out_ref, sums = refs[:4], refs[4], refs[5], refs[6]
+    step = pl.program_id(0)
+    wide = part_refs[0].shape[1]
+    act = jnp.where(step == 0, even_ref[...], odd_ref[...])
+
+    @pl.when(step == 0)
+    def _():
+        for index, part_ref in enumerate(part_refs):
+            lanes = slice(index * wide, (index + 1) * wide)
+            sums[:, lanes] = before_ref[:, lanes] + jnp.dot(
+                act, part_ref[...], preferred_element_type=jnp.float32
+            )
+
+    @pl.when(step > 0)
+    def _():
+        for index, part_ref in enumerate(part_refs):
+            lanes = slice(index * wide, (index + 1) * wide)
+            total = sums[:, lanes] + jnp.dot(
+                act, part_ref[...], preferred_element_type=jnp.float32
+            )
+            out_ref[:, :, lanes] = total.astype(jnp.bfloat16).reshape(out_ref.shape[:2] + (wide,))
+
+
+def second_stage(place, acts, parts, before=None, items=None):
+    count = acts[0].shape[0]
+    wide = parts[0].shape[1]
+    width = 4 * wide
+    near = before is None
+    first_block = 0 if near else 2
+    whole = pl.BlockSpec((count, width), lambda i, p: (0, 0))
+    in_specs = [pl.BlockSpec((count, ACT_BLOCK), lambda i, p: (0, 0))] * 2 + [
+        pl.BlockSpec((ACT_BLOCK, wide), lambda i, p: ((p[0] // 2) ^ (i + first_block), 0))
+    ] * 4
+    if near:
+        return pl.pallas_call(
+            near_kernel,
+            grid_spec=pltpu.PrefetchScalarGridSpec(
+                num_scalar_prefetch=1, grid=(2,), in_specs=in_specs, out_specs=whole
+            ),
+            out_shape=jax.ShapeDtypeStruct((count, width), jnp.float32),
+            name="second_near",
+        )(place, *acts, *parts)
+    shape = (items, count // items, width)
+    return pl.pallas_call(
+        far_kernel,
+        grid_spec=pltpu.PrefetchScalarGridSpec(
+            num_scalar_prefetch=1,
+            grid=(2,),
+            in_specs=in_specs + [whole],
+            out_specs=pl.BlockSpec(shape, lambda i, p: (0, 0, 0)),
+            scratch_shapes=[pltpu.VMEM((count, width), jnp.float32)],
+        ),
+        out_shape=jax.ShapeDtypeStruct(shape, jnp.bfloat16),
+        name="second_far",
+    )(place, *acts, *parts, before)
+
+
 def shards(
     hidden_in,
     expert_ids,
@@ -59,16 +217,38 @@
 ):
     tokens, model_width = hidden_in.shape
     experts = lax.axis_size("ep")
-    capacity = max(2, 8 * tokens // (3 * experts))
-    slots = expert_slots(expert_ids)
-    places = expert_ids * capacity + slots
-    place_ids = lax.broadcasted_iota(jnp.int32, (tokens, experts * capacity), 1)
+    place = lax.axis_index("dp")
+    place_list = place.reshape(1).astype(jnp.int32)
+
+    first_parts = four_parts(first_weight[0], FIRST_FLIP, 1)
+    second_parts = four_parts(second_weight[0], SECOND_FLIP, 1)
+
+    tail = jnp.pad(expert_ids.astype(jnp.bfloat16), ((0, 0), (0, 126)))
+    mate_rows = swap(jnp.concatenate([hidden_in, tail], axis=1), ROW_FLIP)
+    ids_mate = mate_rows[:, model_width : model_width + 2].astype(jnp.int32)
+    upper = place // 4
+    places = jnp.concatenate(
+        [
+            expert_ids * 4 + 2 * upper + expert_slots(expert_ids),
+            ids_mate * 4 + 2 * (1 - upper) + expert_slots(ids_mate),
+        ],
+        axis=0,
+    )
+    place_ids = lax.broadcasted_iota(jnp.int32, (2 * tokens, experts * 4), 1)
     picks = [places[:, column : column + 1] == place_ids for column in range(2)]
-    chooser = (picks[0] | picks[1]).astype(jnp.bfloat16)
-    dispatch = lax.dot_general(
-        chooser, hidden_in, (((0,), (0,)), ((), ())), preferred_element_type=jnp.float32
-    )
-    dispatch = dispatch.astype(jnp.bfloat16).reshape(experts, capacity, model_width)
+    place_rows = lax.broadcasted_iota(jnp.int32, (experts * 4, 2 * tokens), 0)
+    choose = (places[:, 0][None, :] == place_rows) | (places[:, 1][None, :] == place_rows)
+
+    dispatch = dispatch_rows(choose.astype(jnp.bfloat16), hidden_in, mate_rows, experts)
+    received = lax.all_to_all(dispatch, "ep", split_axis=0, concat_axis=0, tiled=True)
+
+    near, far = [], []
+    for index in range(2):
+        left, right = first_parts[2 * index : 2 * index + 2]
+        act = first_stage(place_list, received, left, right)
+        near.append(act)
+        far.append(swap(act, ROW_FLIP))
+
     expert_cols = lax.broadcasted_iota(jnp.int32, route_logits.shape, 1)
     chosen = jnp.stack(
         [
@@ -81,36 +261,35 @@
         axis=1,
     )
     gates = jax.nn.softmax(chosen, axis=1)
-    first_local = first_weight[0]
-    second_local = second_weight[0]
-    received = lax.all_to_all(dispatch, "ep", split_axis=0, concat_axis=0, tiled=True)
-    sources, item_count, _ = received.shape
-    expert_rows = received.reshape(sources * item_count, model_width)
-    hidden = activate(
-        jnp.dot(
-            expert_rows,
-            lax.all_gather(first_local, "dp", axis=1, tiled=True),
-            preferred_element_type=jnp.float32,
-        )
-    )
-    result = jnp.dot(
-        hidden,
-        lax.all_gather(second_local, "dp", axis=1, tiled=True),
-        preferred_element_type=jnp.float32,
-    ).astype(jnp.bfloat16)
-    outputs = result.reshape(sources, item_count, model_width)
+    both_gates = jnp.concatenate([gates, swap(gates, ROW_FLIP)], axis=0)
+
+    sums = second_stage(place_list, near, second_parts)
+    outputs = second_stage(place_list, far, second_parts, sums, experts)
+    width = outputs.shape[2]
     returned = lax.all_to_all(outputs, "ep", split_axis=0, concat_axis=0, tiled=True)
+    flat_back = returned.reshape(experts * 4, width)
+
     attended = attend(
         queries, span_keys, span_values, cache_keys[0], cache_values[0], valid_frames[0]
     )
-    flat_back = returned.reshape(experts * capacity, model_width)
-    running = jnp.zeros((tokens, model_width), jnp.float32)
+
+    running = jnp.zeros((2 * tokens, width), jnp.float32)
     for column in range(2):
         picked = jnp.dot(
             picks[column].astype(jnp.bfloat16), flat_back, preferred_element_type=jnp.float32
         )
-        running = running + gates[:, column : column + 1] * picked
-    mixed = running.astype(jnp.bfloat16)
+        running = running + both_gates[:, column : column + 1] * picked
+    halves = running.astype(jnp.bfloat16)
+    arrived = swap(halves[tokens:], ROW_FLIP)
+    flips = (0, CORE_FLIP, SECOND_FLIP, SECOND_FLIP ^ CORE_FLIP)
+    blocks = [None] * 8
+    for half, flip in ((halves[:tokens], 0), (arrived, ROW_FLIP)):
+        for index, block in enumerate(jnp.split(half, 4, axis=1)):
+            blocks[flips[index] ^ flip] = block
+    for bit in (1, 2, 4):
+        turned = (place & bit) != 0
+        blocks = [jnp.where(turned, blocks[index ^ bit], blocks[index]) for index in range(8)]
+    mixed = jnp.concatenate(blocks, axis=1)
     return (mixed, attended)
 
 

time: 264 us -> 206 us (0.78)
  the two profiles are of different devices: /device:TPU:2 before, /device:TPU:10 now
where the time goes in v2:
time: 206 us; the launch traced here: 205 us
  waiting for transfers between devices  101 us (49%)
  starting transfers between devices  70.8 us (34%)
  Pallas kernels  20.4 us (10%)
  local copies, waits for them, and re-layouts  5.43 us (3%)
  other arithmetic  3.33 us (2%)
    ppermute x11, waiting for transfers between devices, swap(): lax.ppermute(block, 'dp', [(place, place ^ flip) for place in range(8)])  86.6 us
    ppermute x11, starting transfers between devices, swap(): lax.ppermute(block, 'dp', [(place, place ^ flip) for place in range(8)])  44.1 us
    all_to_all x1, starting transfers between devices, shards(): lax.all_to_all(dispatch, 'ep', split_axis=0, concat_axis=0, tiled=True)  14.9 us
    all_to_all x1, waiting for transfers between devices, shards(): lax.all_to_all(outputs, 'ep', split_axis=0, concat_axis=0, tiled=True)  14.9 us
    all_to_all x1, starting transfers between devices, shards(): lax.all_to_all(outputs, 'ep', split_axis=0, concat_axis=0, tiled=True)  11.8 us
    pallas_call x2, Pallas kernels, first_stage(): pl.pallas_call(first_kernel, grid_spec=pltpu.PrefetchScalarGridSpec(num_s...  8.34 us
    pallas_call x1, Pallas kernels, dispatch_rows(): pl.pallas_call(dispatch_kernel, grid=(width // step,), in_specs=[pl.Block...  4.35 us
  transfers between devices with their start and end apart: 13, of which 6 were waited for; matrix products, arithmetic and copies ran while one was open for 2% of the time, Pallas kernels for 6%

profile of v2, /device:TPU:10, one launch (start us, length us, event | category | flops | bytes accessed | tf_op | source)
XLA Modules:
  0.0 204.7 jit_solution(17612712451162093341)
XLA Ops:
  0.7 0.8 multiply_add_fusion
  1.5 0.9 fusion.15
  2.5 6.8 %collective-permute-start.1 = (bf16[24,4224]{1,0:T(8,128)(2,1)S(1)}, bf16[24,4224]{1,0:T(8,128)(2,1)S(1)}, u32[]{:S(2)}, u32[]{:S(2)}) collective-permute-start(bf16[24,4224]{1,0:T(8,128)(2,1)S(1)} %fusion.15), channel_id=1, source_target_pairs={{0,256},{64,320},{128,384},{192,448},{256,0},{320,64},{384,128},{4... | collective-permute-start | bytes 608264 | tf_op jit(solution)/shard_map/ppermute | solution.py:54
  9.3 0.8 copy.57
  10.6 7.1 %collective-permute-done.1.mate_ref = bf16[24,4224]{1,0:T(8,128)(2,1)S(1)} collective-permute-done((bf16[24,4224]{1,0:T(8,128)(2,1)S(1)}, bf16[24,4224]{1,0:T(8,128)(2,1)S(1)}, u32[]{:S(2)}, u32[]{:S(2)}) %collective-permute-start.1) | collective-permute-done | bytes 202784 | tf_op jit(solution)/shard_map/ppermute | solution.py:54
  18.3 0.7 fusion.17.choose_ref
  19.0 4.3 %dispatch_rows.1 = bf16[64,4,4096]{2,1,0:T(4,128)(2,1)} custom-call(bf16[256,48]{1,0:T(8,128)(2,1)} %fusion.17.choose_ref, bf16[24,4096]{1,0:T(8,128)(2,1)} %own_ref.1, bf16[24,4224]{1,0:T(8,128)(2,1)} %copy-done.6), custom_call_target="tpu_custom_call" | custom-call | tf_op jit(solution)/shard_map/dispatch_rows/pallas_call | solution.py:76
  23.3 14.9 %all-to-all-start = ((bf16[64,4,4096]{2,1,0:T(4,128)(2,1)}), bf16[64,4,4096]{2,1,0:T(4,128)(2,1)S(1)}, u32[]{:S(2)}, u32[]{:S(2)}) async-start(bf16[64,4,4096]{2,1,0:T(4,128)(2,1)} %dispatch_rows.1), calls=%async_computation | async-start | bytes 4194304 | tf_op jit(solution)/shard_map/all_to_all | solution.py:243
  38.3 5.2 %collective-permute-start.4 = (bf16[4096,128]{1,0:T(8,128)(2,1)}, bf16[4096,128]{1,0:T(8,128)(2,1)S(1)}, u32[]{:S(2)}, u32[]{:S(2)}) collective-permute-start(bf16[4096,128]{1,0:T(8,128)(2,1)} %bitcast.71), channel_id=1, source_target_pairs={{0,128},{64,192},{128,0},{192,64},{256,384},{320,448},{384,256},{4... | collective-permute-start | bytes 3145736 | tf_op jit(solution)/shard_map/ppermute | solution.py:54
  43.5 5.6 %collective-permute-start.8 = (bf16[1024,512]{1,0:T(8,128)(2,1)S(1)}, bf16[1024,512]{1,0:T(8,128)(2,1)}, u32[]{:S(2)}, u32[]{:S(2)}) collective-permute-start(bf16[1024,512]{1,0:T(8,128)(2,1)S(1)} %bitcast.67), channel_id=1, source_target_pairs={{0,384},{64,448},{128,256},{192,320},{256,128},{320,192},{384,0},{... | collective-permute-start | bytes 3145736 | tf_op jit(solution)/shard_map/ppermute | solution.py:54
  49.1 60.0 %collective-permute-done.4.left_ref = bf16[4096,128]{1,0:T(8,128)(2,1)S(1)} collective-permute-done((bf16[4096,128]{1,0:T(8,128)(2,1)}, bf16[4096,128]{1,0:T(8,128)(2,1)S(1)}, u32[]{:S(2)}, u32[]{:S(2)}) %collective-permute-start.4) | collective-permute-done | bytes 1048608 | tf_op jit(solution)/shard_map/ppermute | solution.py:54
  109.1 1.9 collective-permute-start.5
  111.0 2.4 %collective-permute-start.2 = (bf16[4096,128]{1,0:T(8,128)(2,1)}, bf16[4096,128]{1,0:T(8,128)(2,1)}, u32[]{:S(2)}, u32[]{:S(2)}) collective-permute-start(bf16[4096,128]{1,0:T(8,128)(2,1)} %bitcast.72), channel_id=1, source_target_pairs={{0,64},{64,0},{128,192},{192,128},{256,320},{320,256},{384,448},{4... | collective-permute-start | bytes 3145736 | tf_op jit(solution)/shard_map/ppermute | solution.py:54
  113.4 1.9 collective-permute-start.7
  115.4 2.4 %collective-permute-start.9 = (bf16[1024,512]{1,0:T(8,128)(2,1)}, bf16[1024,512]{1,0:T(8,128)(2,1)}, u32[]{:S(2)}, u32[]{:S(2)}) collective-permute-start(bf16[1024,512]{1,0:T(8,128)(2,1)} %collective-permute-done.8.refs_2_), channel_id=1, source_target_pairs={{0,64},{64,0},{128,192},{192,128},{256,320},{320,256},{384,448},{4... | collective-permute-start | bytes 3145736 | tf_op jit(solution)/shard_map/ppermute | solution.py:54
  117.8 1.3 copy-done.1
  119.2 4.2 %first_stage.3.odd_ref = bf16[256,256]{1,0:T(8,128)(2,1)} custom-call(s32[1]{0:T(128)} %bitcast.6.place_ref, bf16[64,4,4096]{2,1,0:T(4,128)(2,1)} %copy-done.1, bf16[4096,128]{1,0:T(8,128)(2,1)} %copy-done.3, bf16[4096,128]{1,0:T(8,128)(2,1)} %collective-permute-done.5.right_ref), custom_call_target="tpu_custom_call" | custom-call | tf_op jit(solution)/shard_map/first_stage/pallas_call | solution.py:111
  123.3 5.8 %collective-permute-start.6 = (bf16[256,256]{1,0:T(8,128)(2,1)}, bf16[256,256]{1,0:T(8,128)(2,1)S(1)}, u32[]{:S(2)}, u32[]{:S(2)}) collective-permute-start(bf16[256,256]{1,0:T(8,128)(2,1)} %first_stage.3.odd_ref), channel_id=1, source_target_pairs={{0,256},{64,320},{128,384},{192,448},{256,0},{320,64},{384,128},{4... | collective-permute-start | bytes 393224 | tf_op jit(solution)/shard_map/ppermute | solution.py:54
  129.1 4.2 %first_stage.2.even_ref = bf16[256,256]{1,0:T(8,128)(2,1)} custom-call(s32[1]{0:T(128)} %bitcast.6.place_ref, bf16[64,4,4096]{2,1,0:T(4,128)(2,1)} %copy-done.1, bf16[4096,128]{1,0:T(8,128)(2,1)} %bitcast.73, bf16[4096,128]{1,0:T(8,128)(2,1)} %collective-permute-done.2.right_ref), custom_call_target="tpu_custom_call" | custom-call | tf_op jit(solution)/shard_map/first_stage/pallas_call | solution.py:111
  133.3 3.9 %collective-permute-start.3 = (bf16[256,256]{1,0:T(8,128)(2,1)}, bf16[256,256]{1,0:T(8,128)(2,1)S(1)}, u32[]{:S(2)}, u32[]{:S(2)}) collective-permute-start(bf16[256,256]{1,0:T(8,128)(2,1)} %first_stage.2.even_ref), channel_id=1, source_target_pairs={{0,256},{64,320},{128,384},{192,448},{256,0},{320,64},{384,128},{4... | collective-permute-start | bytes 393224 | tf_op jit(solution)/shard_map/ppermute | solution.py:54
  137.3 3.7 %second_near.1.refs_4_ = f32[256,2048]{1,0:T(8,128)} custom-call(s32[1]{0:T(128)} %bitcast.6.place_ref, bf16[256,256]{1,0:T(8,128)(2,1)} %first_stage.2.even_ref, bf16[256,256]{1,0:T(8,128)(2,1)} %first_stage.3.odd_ref, bf16[1024,512]{1,0:T(8,128)(2,1)} %bitcast.65, bf16[1024,512]{1,0:T(8,128)(2,1)} %collective-permute-done.7.refs_1_, ...), custom_call_target="tpu_custom_call" | custom-call | tf_op jit(solution)/shard_map/second_near/pallas_call | solution.py:182
  140.9 5.4 %collective-permute-done.3.even_ref = bf16[256,256]{1,0:T(8,128)(2,1)S(1)} collective-permute-done((bf16[256,256]{1,0:T(8,128)(2,1)}, bf16[256,256]{1,0:T(8,128)(2,1)S(1)}, u32[]{:S(2)}, u32[]{:S(2)}) %collective-permute-start.3) | collective-permute-done | bytes 131104 | tf_op jit(solution)/shard_map/ppermute | solution.py:54
  146.3 0.7 copy-done.8
  147.0 4.1 %second_far.1 = bf16[64,4,2048]{2,1,0:T(4,128)(2,1)} custom-call(s32[1]{0:T(128)} %bitcast.6.place_ref, bf16[256,256]{1,0:T(8,128)(2,1)} %copy-done.8, bf16[256,256]{1,0:T(8,128)(2,1)} %copy-done.7, bf16[1024,512]{1,0:T(8,128)(2,1)} %bitcast.66, bf16[1024,512]{1,0:T(8,128)(2,1)} %collective-permute-done.7.refs_1_, ...), custom_call_target="tpu_custom_call" | custom-call | tf_op jit(solution)/shard_map/second_far/pallas_call | solution.py:191
  151.1 11.8 %all-to-all-start.1 = ((bf16[64,4,2048]{2,1,0:T(4,128)(2,1)}), bf16[64,4,2048]{2,1,0:T(4,128)(2,1)S(1)}, u32[]{:S(2)}, u32[]{:S(2)}) async-start(bf16[64,4,2048]{2,1,0:T(4,128)(2,1)} %second_far.1), calls=%async_computation.1 | async-start | bytes 2097152 | tf_op jit(solution)/shard_map/all_to_all | solution.py:269
  163.2 4.0 %collective-permute-start = (f32[24,2]{0,1:T(2,128)S(1)}, f32[24,2]{0,1:T(2,128)S(1)}, u32[]{:S(2)}, u32[]{:S(2)}) collective-permute-start(f32[24,2]{0,1:T(2,128)S(1)} %broadcast_divide_fusion), channel_id=1, source_target_pairs={{0,256},{64,320},{128,384},{192,448},{256,0},{320,64},{384,128},{4... | collective-permute-start | bytes 584 | tf_op jit(solution)/shard_map/ppermute | solution.py:54
  168.7 7.7 %collective-permute-done = f32[24,2]{0,1:T(2,128)S(1)} collective-permute-done((f32[24,2]{0,1:T(2,128)S(1)}, f32[24,2]{0,1:T(2,128)S(1)}, u32[]{:S(2)}, u32[]{:S(2)}) %collective-permute-start) | collective-permute-done | bytes 224 | tf_op jit(solution)/shard_map/ppermute | solution.py:54
  176.5 14.9 %all-to-all-done.1 = bf16[64,4,2048]{2,1,0:T(4,128)(2,1)S(1)} async-done(((bf16[64,4,2048]{2,1,0:T(4,128)(2,1)}), bf16[64,4,2048]{2,1,0:T(4,128)(2,1)S(1)}, u32[]{:S(2)}, u32[]{:S(2)}) %all-to-all-start.1) | async-done | bytes 1048608 | tf_op jit(solution)/shard_map/all_to_all | solution.py:269
  192.3 4.0 %collective-permute-start.10 = (bf16[24,2048]{1,0:T(8,128)(2,1)S(1)}, bf16[24,2048]{1,0:T(8,128)(2,1)S(1)}, u32[]{:S(2)}, u32[]{:S(2)}) collective-permute-start(bf16[24,2048]{1,0:T(8,128)(2,1)S(1)} %slice.40), channel_id=1, source_target_pairs={{0,256},{64,320},{128,384},{192,448},{256,0},{320,64},{384,128},{4... | collective-permute-start | bytes 294920 | tf_op jit(solution)/shard_map/ppermute | solution.py:54
  196.7 0.7 copy.88
  197.3 6.4 %collective-permute-done.10 = bf16[24,2048]{1,0:T(8,128)(2,1)S(1)} collective-permute-done((bf16[24,2048]{1,0:T(8,128)(2,1)S(1)}, bf16[24,2048]{1,0:T(8,128)(2,1)S(1)}, u32[]{:S(2)}, u32[]{:S(2)}) %collective-permute-start.10) | collective-permute-done | bytes 98336 | tf_op jit(solution)/shard_map/ppermute | solution.py:54
  204.0 0.7 copy-done.12
  (75 shorter events, 3.8 us)
Async XLA Ops:
  0.6 167.4 %copy-start = (bf16[24,2048]{1,0:T(8,128)(2,1)S(1)}, bf16[24,2048]{1,0:T(8,128)(2,1)}, u32[]{:S(2)}) copy-start(bf16[24,2048]{1,0:T(8,128)(2,1)} %param.17) | copy-start | bytes 294916
  2.5 15.3 %collective-permute-start.1 = (bf16[24,4224]{1,0:T(8,128)(2,1)S(1)}, bf16[24,4224]{1,0:T(8,128)(2,1)S(1)}, u32[]{:S(2)}, u32[]{:S(2)}) collective-permute-start(bf16[24,4224]{1,0:T(8,128)(2,1)S(1)} %fusion.15), channel_id=1, source_target_pairs={{0,256},{64,320},{128,384},{192,448},{256,0},{320,64},{384,128},{4... | collective-permute-start | bytes 608264 | tf_op jit(solution)/shard_map/ppermute | solution.py:54
  17.8 1.2 copy-start.6
  23.3 20.1 %copy-start.2 = (bf16[1,1024,512]{2,1,0:T(8,128)(2,1)S(1)}, bf16[1,1024,512]{2,1,0:T(8,128)(2,1)}, u32[]{:S(2)}) copy-start(bf16[1,1024,512]{2,1,0:T(8,128)(2,1)} %param.15) | copy-start | bytes 3145732
  23.3 94.5 %all-to-all-start = ((bf16[64,4,4096]{2,1,0:T(4,128)(2,1)}), bf16[64,4,4096]{2,1,0:T(4,128)(2,1)S(1)}, u32[]{:S(2)}, u32[]{:S(2)}) async-start(bf16[64,4,4096]{2,1,0:T(4,128)(2,1)} %dispatch_rows.1), calls=%async_computation | async-start | bytes 4194304 | tf_op jit(solution)/shard_map/all_to_all | solution.py:243
  38.3 70.8 %collective-permute-start.4 = (bf16[4096,128]{1,0:T(8,128)(2,1)}, bf16[4096,128]{1,0:T(8,128)(2,1)S(1)}, u32[]{:S(2)}, u32[]{:S(2)}) collective-permute-start(bf16[4096,128]{1,0:T(8,128)(2,1)} %bitcast.71), channel_id=1, source_target_pairs={{0,128},{64,192},{128,0},{192,64},{256,384},{320,448},{384,256},{4... | collective-permute-start | bytes 3145736 | tf_op jit(solution)/shard_map/ppermute | solution.py:54
  43.5 71.9 %collective-permute-start.8 = (bf16[1024,512]{1,0:T(8,128)(2,1)S(1)}, bf16[1024,512]{1,0:T(8,128)(2,1)}, u32[]{:S(2)}, u32[]{:S(2)}) collective-permute-start(bf16[1024,512]{1,0:T(8,128)(2,1)S(1)} %bitcast.67), channel_id=1, source_target_pairs={{0,384},{64,448},{128,256},{192,320},{256,128},{320,192},{384,0},{... | collective-permute-start | bytes 3145736 | tf_op jit(solution)/shard_map/ppermute | solution.py:54
  109.1 8.7 %copy-start.3 = (bf16[4096,128]{1,0:T(8,128)(2,1)}, bf16[4096,128]{1,0:T(8,128)(2,1)S(1)}, u32[]{:S(2)}) copy-start(bf16[4096,128]{1,0:T(8,128)(2,1)S(1)} %collective-permute-done.4.left_ref) | copy-start | bytes 3145732
  109.1 8.7 %collective-permute-start.5 = (bf16[4096,128]{1,0:T(8,128)(2,1)S(1)}, bf16[4096,128]{1,0:T(8,128)(2,1)}, u32[]{:S(2)}, u32[]{:S(2)}) collective-permute-start(bf16[4096,128]{1,0:T(8,128)(2,1)S(1)} %collective-permute-done.4.left_ref), channel_id=1, source_target_pairs={{0,64},{64,0},{128,192},{192,128},{256,320},{320,256},{384,448},{4... | collective-permute-start | bytes 3145736 | tf_op jit(solution)/shard_map/ppermute | solution.py:54
  111.0 18.1 %collective-permute-start.2 = (bf16[4096,128]{1,0:T(8,128)(2,1)}, bf16[4096,128]{1,0:T(8,128)(2,1)}, u32[]{:S(2)}, u32[]{:S(2)}) collective-permute-start(bf16[4096,128]{1,0:T(8,128)(2,1)} %bitcast.72), channel_id=1, source_target_pairs={{0,64},{64,0},{128,192},{192,128},{256,320},{320,256},{384,448},{4... | collective-permute-start | bytes 3145736 | tf_op jit(solution)/shard_map/ppermute | solution.py:54
  113.4 23.8 %collective-permute-start.7 = (bf16[1024,512]{1,0:T(8,128)(2,1)S(1)}, bf16[1024,512]{1,0:T(8,128)(2,1)}, u32[]{:S(2)}, u32[]{:S(2)}) collective-permute-start(bf16[1024,512]{1,0:T(8,128)(2,1)S(1)} %bitcast.68), channel_id=1, source_target_pairs={{0,64},{64,0},{128,192},{192,128},{256,320},{320,256},{384,448},{4... | collective-permute-start | bytes 3145736 | tf_op jit(solution)/shard_map/ppermute | solution.py:54
  115.4 21.9 %collective-permute-start.9 = (bf16[1024,512]{1,0:T(8,128)(2,1)}, bf16[1024,512]{1,0:T(8,128)(2,1)}, u32[]{:S(2)}, u32[]{:S(2)}) collective-permute-start(bf16[1024,512]{1,0:T(8,128)(2,1)} %collective-permute-done.8.refs_2_), channel_id=1, source_target_pairs={{0,64},{64,0},{128,192},{192,128},{256,320},{320,256},{384,448},{4... | collective-permute-start | bytes 3145736 | tf_op jit(solution)/shard_map/ppermute | solution.py:54
  117.8 1.3 copy-start.1
  123.3 17.6 %collective-permute-start.6 = (bf16[256,256]{1,0:T(8,128)(2,1)}, bf16[256,256]{1,0:T(8,128)(2,1)S(1)}, u32[]{:S(2)}, u32[]{:S(2)}) collective-permute-start(bf16[256,256]{1,0:T(8,128)(2,1)} %first_stage.3.odd_ref), channel_id=1, source_target_pairs={{0,256},{64,320},{128,384},{192,448},{256,0},{320,64},{384,128},{4... | collective-permute-start | bytes 393224 | tf_op jit(solution)/shard_map/ppermute | solution.py:54
  133.3 13.0 %collective-permute-start.3 = (bf16[256,256]{1,0:T(8,128)(2,1)}, bf16[256,256]{1,0:T(8,128)(2,1)S(1)}, u32[]{:S(2)}, u32[]{:S(2)}) collective-permute-start(bf16[256,256]{1,0:T(8,128)(2,1)} %first_stage.2.even_ref), channel_id=1, source_target_pairs={{0,256},{64,320},{128,384},{192,448},{256,0},{320,64},{384,128},{4... | collective-permute-start | bytes 393224 | tf_op jit(solution)/shard_map/ppermute | solution.py:54
  140.9 5.4 %copy-start.7 = (bf16[256,256]{1,0:T(8,128)(2,1)}, bf16[256,256]{1,0:T(8,128)(2,1)S(1)}, u32[]{:S(2)}) copy-start(bf16[256,256]{1,0:T(8,128)(2,1)S(1)} %collective-permute-done.6.odd_ref) | copy-start | bytes 393220
  146.3 0.7 copy-start.8
  151.1 11.8 %copy-start.11 = (s32[24,2]{0,1:T(2,128)S(1)}, s32[24,2]{0,1:T(2,128)}, u32[]{:S(2)}) copy-start(s32[24,2]{0,1:T(2,128)} %param.12) | copy-start | bytes 580
  151.1 11.8 %copy-start.10 = (f32[24,64]{1,0:T(8,128)S(1)}, f32[24,64]{1,0:T(8,128)}, u32[]{:S(2)}) copy-start(f32[24,64]{1,0:T(8,128)} %param.13) | copy-start | bytes 18436
  151.1 16.1 %copy-start.4 = (bf16[1,72,2048]{2,1,0:T(8,128)(2,1)S(1)}, bf16[1,72,2048]{2,1,0:T(8,128)(2,1)}, u32[]{:S(2)}) copy-start(bf16[1,72,2048]{2,1,0:T(8,128)(2,1)} %param.19) | copy-start | bytes 884740
  151.1 17.0 %copy-start.9 = (bf16[24,2048]{1,0:T(8,128)(2,1)S(1)}, bf16[24,2048]{1,0:T(8,128)(2,1)}, u32[]{:S(2)}) copy-start(bf16[24,2048]{1,0:T(8,128)(2,1)} %param.18) | copy-start | bytes 294916
  151.1 17.0 %copy-start.13 = (bf16[24,2048]{1,0:T(8,128)(2,1)S(1)}, bf16[24,2048]{1,0:T(8,128)(2,1)}, u32[]{:S(2)}) copy-start(bf16[24,2048]{1,0:T(8,128)(2,1)} %param.16) | copy-start | bytes 294916
  151.1 17.5 %copy-start.5 = (bf16[1,72,2048]{2,1,0:T(8,128)(2,1)S(1)}, bf16[1,72,2048]{2,1,0:T(8,128)(2,1)}, u32[]{:S(2)}) copy-start(bf16[1,72,2048]{2,1,0:T(8,128)(2,1)} %param.20) | copy-start | bytes 884740
  151.1 40.3 %all-to-all-start.1 = ((bf16[64,4,2048]{2,1,0:T(4,128)(2,1)}), bf16[64,4,2048]{2,1,0:T(4,128)(2,1)S(1)}, u32[]{:S(2)}, u32[]{:S(2)}) async-start(bf16[64,4,2048]{2,1,0:T(4,128)(2,1)} %second_far.1), calls=%async_computation.1 | async-start | bytes 2097152 | tf_op jit(solution)/shard_map/all_to_all | solution.py:269
  163.2 13.3 %collective-permute-start = (f32[24,2]{0,1:T(2,128)S(1)}, f32[24,2]{0,1:T(2,128)S(1)}, u32[]{:S(2)}, u32[]{:S(2)}) collective-permute-start(f32[24,2]{0,1:T(2,128)S(1)} %broadcast_divide_fusion), channel_id=1, source_target_pairs={{0,256},{64,320},{128,384},{192,448},{256,0},{320,64},{384,128},{4... | collective-permute-start | bytes 584 | tf_op jit(solution)/shard_map/ppermute | solution.py:54
  192.3 11.4 %collective-permute-start.10 = (bf16[24,2048]{1,0:T(8,128)(2,1)S(1)}, bf16[24,2048]{1,0:T(8,128)(2,1)S(1)}, u32[]{:S(2)}, u32[]{:S(2)}) collective-permute-start(bf16[24,2048]{1,0:T(8,128)(2,1)S(1)} %slice.40), channel_id=1, source_target_pairs={{0,256},{64,320},{128,384},{192,448},{256,0},{320,64},{384,128},{4... | collective-permute-start | bytes 294920 | tf_op jit(solution)/shard_map/ppermute | solution.py:54
  204.0 0.7 copy-start.12

commit v3 on v2

--- a/solution.py
+++ b/solution.py
@@ -13,6 +13,7 @@
 FRAME_TOK = 24
 
 CORE_FLIP, FIRST_FLIP, ROW_FLIP, SECOND_FLIP = 1, 2, 4, 6
+SIDE_FLIP = 8
 ACT_BLOCK = 256
 
 
@@ -54,6 +55,10 @@
     return lax.ppermute(block, "dp", [(place, place ^ flip) for place in range(8)])
 
 
+def swap_far(block, places, flip):
+    return lax.ppermute(block, ("dp", "ep"), [(i, i ^ flip) for i in range(places)])
+
+
 def four_parts(block, flip, pieces):
     mate = jnp.concatenate(
         [swap(piece, flip) for piece in jnp.split(block, pieces, axis=0)],
@@ -62,26 +67,32 @@
     return [block, swap(block, CORE_FLIP), mate, swap(mate, CORE_FLIP)]
 
 
-def dispatch_kernel(choose_ref, own_ref, mate_ref, out_ref):
-    choose = choose_ref[...]
-    half = choose.shape[1] // 2
-    rows = jnp.dot(choose[:, :half], own_ref[...], preferred_element_type=jnp.float32)
-    rows += jnp.dot(choose[:, half:], mate_ref[...], preferred_element_type=jnp.float32)
-    out_ref[...] = rows.astype(jnp.bfloat16).reshape(out_ref.shape)
-
-
-def dispatch_rows(choose, own, mate, items):
-    count, width = choose.shape[0], own.shape[1]
-    tokens, step = own.shape[0], 1024
+def dispatch_kernel(choose_ref, *refs):
+    token_refs, out_ref = refs[:-1], refs[-1]
+    tokens = token_refs[0].shape[0]
+    rows = None
+    for index, token_ref in enumerate(token_refs):
+        part = jnp.dot(
+            choose_ref[:, index * tokens : (index + 1) * tokens],
+            token_ref[...],
+            preferred_element_type=jnp.float32,
+        )
+        rows = part if rows is None else rows + part
+    out_ref[...] = rows.astype(jnp.bfloat16)
+
+
+def dispatch_rows(choose, streams):
+    tokens, width = streams[0].shape
+    count, step = choose.shape[0], 1024
     return pl.pallas_call(
         dispatch_kernel,
         grid=(width // step,),
         in_specs=[pl.BlockSpec(choose.shape, lambda i: (0, 0))]
-        + [pl.BlockSpec((tokens, step), lambda i: (0, i))] * 2,
-        out_specs=pl.BlockSpec((items, count // items, step), lambda i: (0, 0, i)),
-        out_shape=jax.ShapeDtypeStruct((items, count // items, width), jnp.bfloat16),
+        + [pl.BlockSpec((tokens, step), lambda i: (0, i))] * len(streams),
+        out_specs=pl.BlockSpec((count, step), lambda i: (0, i)),
+        out_shape=jax.ShapeDtypeStruct((count, width), jnp.bfloat16),
         name="dispatch_rows",
-    )(choose, own, mate)
+    )(choose, *streams)
 
 
 def first_kernel(place_ref, rows_ref, left_ref, right_ref, act_ref, sums):
@@ -91,7 +102,7 @@
     def _():
         sums[...] = jnp.zeros_like(sums)
 
-    rows = rows_ref[...].reshape(sums.shape[0], -1)
+    rows = rows_ref[...]
     wide = jnp.concatenate([left_ref[...], right_ref[...]], axis=1)
     sums[...] += jnp.dot(rows, wide, preferred_element_type=jnp.float32)
 
@@ -106,14 +117,14 @@
 
 
 def first_stage(place, rows, left, right):
-    items, slots, depth = rows.shape
-    count, wide, step = items * slots, left.shape[1], 1024
+    count, depth = rows.shape
+    wide, step = left.shape[1], 1024
     return pl.pallas_call(
         first_kernel,
         grid_spec=pltpu.PrefetchScalarGridSpec(
             num_scalar_prefetch=1,
             grid=(depth // step,),
-            in_specs=[pl.BlockSpec((items, slots, step), lambda i, p: (0, 0, i))]
+            in_specs=[pl.BlockSpec((count, step), lambda i, p: (0, i))]
             + [pl.BlockSpec((step, wide), lambda i, p: (i, 0))] * 2,
             out_specs=pl.BlockSpec((count, ACT_BLOCK), lambda i, p: (0, 0)),
             scratch_shapes=[pltpu.VMEM((count, ACT_BLOCK), jnp.float32)],
@@ -165,10 +176,13 @@
             total = sums[:, lanes] + jnp.dot(
                 act, part_ref[...], preferred_element_type=jnp.float32
             )
-            out_ref[:, :, lanes] = total.astype(jnp.bfloat16).reshape(out_ref.shape[:2] + (wide,))
-
-
-def second_stage(place, acts, parts, before=None, items=None):
+            outer, sides, inner, slots, _ = out_ref.shape
+            total = total.reshape(outer, inner, sides * slots, wide).astype(jnp.bfloat16)
+            for side in range(sides):
+                out_ref[:, side, :, :, lanes] = total[:, :, side * slots : (side + 1) * slots, :]
+
+
+def second_stage(place, acts, parts, before=None, form=None):
     count = acts[0].shape[0]
     wide = parts[0].shape[1]
     width = 4 * wide
@@ -187,14 +201,14 @@
             out_shape=jax.ShapeDtypeStruct((count, width), jnp.float32),
             name="second_near",
         )(place, *acts, *parts)
-    shape = (items, count // items, width)
+    shape = form + (width,)
     return pl.pallas_call(
         far_kernel,
         grid_spec=pltpu.PrefetchScalarGridSpec(
             num_scalar_prefetch=1,
             grid=(2,),
             in_specs=in_specs + [whole],
-            out_specs=pl.BlockSpec(shape, lambda i, p: (0, 0, 0)),
+            out_specs=pl.BlockSpec(shape, lambda i, p: (0,) * len(shape)),
             scratch_shapes=[pltpu.VMEM((count, width), jnp.float32)],
         ),
         out_shape=jax.ShapeDtypeStruct(shape, jnp.bfloat16),
@@ -224,23 +238,42 @@
     second_parts = four_parts(second_weight[0], SECOND_FLIP, 1)
 
     tail = jnp.pad(expert_ids.astype(jnp.bfloat16), ((0, 0), (0, 126)))
-    mate_rows = swap(jnp.concatenate([hidden_in, tail], axis=1), ROW_FLIP)
-    ids_mate = mate_rows[:, model_width : model_width + 2].astype(jnp.int32)
+    rows = jnp.concatenate([hidden_in, tail], axis=1)
+    devices = lax.axis_size("dp") * experts
+    row_flip = ROW_FLIP * experts
+    mates = [swap_far(rows, devices, flip) for flip in (row_flip, SIDE_FLIP, row_flip ^ SIDE_FLIP)]
+    all_ids = [expert_ids] + [
+        mate[:, model_width : model_width + 2].astype(jnp.int32) for mate in mates
+    ]
+    all_slots = [expert_slots(ids) for ids in all_ids]
     upper = place // 4
+    side = (lax.axis_index("ep") // SIDE_FLIP) % 2
+    send_places = []
+    for index, (ids, slots) in enumerate(zip(all_ids, all_slots)):
+        source_side, stream = side ^ (index // 2), upper ^ (index % 2)
+        column = (ids // (2 * SIDE_FLIP)) * SIDE_FLIP + ids % SIDE_FLIP
+        sent = (ids // SIDE_FLIP) % 2 == side
+        send_places.append(jnp.where(sent, column * 8 + source_side * 4 + stream * 2 + slots, -1))
+    send_places = jnp.concatenate(send_places, axis=0)
+    send_rows = lax.broadcasted_iota(jnp.int32, (experts * 4, 4 * tokens), 0)
+    choose = (send_places[:, 0][None, :] == send_rows) | (send_places[:, 1][None, :] == send_rows)
     places = jnp.concatenate(
-        [
-            expert_ids * 4 + 2 * upper + expert_slots(expert_ids),
-            ids_mate * 4 + 2 * (1 - upper) + expert_slots(ids_mate),
-        ],
+        [all_ids[0] * 4 + 2 * upper + all_slots[0], all_ids[1] * 4 + 2 * (1 - upper) + all_slots[1]],
         axis=0,
     )
     place_ids = lax.broadcasted_iota(jnp.int32, (2 * tokens, experts * 4), 1)
     picks = [places[:, column : column + 1] == place_ids for column in range(2)]
-    place_rows = lax.broadcasted_iota(jnp.int32, (experts * 4, 2 * tokens), 0)
-    choose = (places[:, 0][None, :] == place_rows) | (places[:, 1][None, :] == place_rows)
-
-    dispatch = dispatch_rows(choose.astype(jnp.bfloat16), hidden_in, mate_rows, experts)
-    received = lax.all_to_all(dispatch, "ep", split_axis=0, concat_axis=0, tiled=True)
+
+    dispatch = dispatch_rows(choose.astype(jnp.bfloat16), [hidden_in] + mates)
+    sides = [[e for e in range(experts) if e // SIDE_FLIP % 2 == side] for side in range(2)]
+    received = lax.all_to_all(
+        dispatch.reshape(experts // 2, 8, model_width),
+        "ep",
+        split_axis=0,
+        concat_axis=0,
+        tiled=True,
+        axis_index_groups=sides,
+    ).reshape(experts * 4, model_width)
 
     near, far = [], []
     for index in range(2):
@@ -264,8 +297,10 @@
     both_gates = jnp.concatenate([gates, swap(gates, ROW_FLIP)], axis=0)
 
     sums = second_stage(place_list, near, second_parts)
-    outputs = second_stage(place_list, far, second_parts, sums, experts)
-    width = outputs.shape[2]
+    form = (experts // (2 * SIDE_FLIP), 2, SIDE_FLIP, 4)
+    outputs = second_stage(place_list, far, second_parts, sums, form)
+    width = outputs.shape[-1]
+    outputs = outputs.reshape(experts, 4, width)
     returned = lax.all_to_all(outputs, "ep", split_axis=0, concat_axis=0, tiled=True)
     flat_back = returned.reshape(experts * 4, width)
 

time: 206 us -> 195 us (0.947)
  waiting for transfers between devices: 101 us -> 82.1 us
  starting transfers between devices: 70.8 us -> 77.2 us
    ppermute x11 -> x10, waiting for transfers between devices: 86.6 us -> 56 us  [swap(): lax.ppermute(block, 'dp', [(place, place ^ flip) for place in range(8)])]
    ppermute x0 -> x3, starting transfers between devices: none -> 12.2 us  [swap_far(): lax.ppermute(block, ('dp', 'ep'), [(i, i ^ flip) for i in range(places)])]
    ppermute x0 -> x3, waiting for transfers between devices: none -> 11.8 us  [swap_far(): lax.ppermute(block, ('dp', 'ep'), [(i, i ^ flip) for i in range(places)])]
    ppermute x11 -> x10, starting transfers between devices: 44.1 us -> 36.5 us  [swap(): lax.ppermute(block, 'dp', [(place, place ^ flip) for place in range(8)])]
    all_to_all x1, starting transfers between devices: 11.8 us -> 14.9 us  [shards(): lax.all_to_all(outputs, 'ep', split_axis=0, concat_axis=0, tiled=True)]
  transfers between devices with their start and end apart: 13 -> 15, of which waited for: 6 -> 7; matrix products, arithmetic and copies ran while one was open for 2% -> 2% of each run, Pallas kernels for 6% -> 6%
where the time goes in v3:
time: 195 us; the launch traced here: 194 us
  waiting for transfers between devices  82.1 us (42%)
  starting transfers between devices  77.2 us (40%)
  Pallas kernels  21.2 us (11%)
  local copies, waits for them, and re-layouts  6.15 us (3%)
  other arithmetic  3.9 us (2%)
    ppermute x10, waiting for transfers between devices, swap(): lax.ppermute(block, 'dp', [(place, place ^ flip) for place in range(8)])  56 us
    ppermute x10, starting transfers between devices, swap(): lax.ppermute(block, 'dp', [(place, place ^ flip) for place in range(8)])  36.5 us
    all_to_all x1, starting transfers between devices, shards(): lax.all_to_all(outputs, 'ep', split_axis=0, concat_axis=0, tiled=True)  14.9 us
    all_to_all x1, waiting for transfers between devices, shards(): lax.all_to_all(outputs, 'ep', split_axis=0, concat_axis=0, tiled=True)  14.3 us
    all_to_all x1, starting transfers between devices, shards(): lax.all_to_all(dispatch.reshape(experts // 2, 8, model_width), 'ep', spli...  13.6 us
    ppermute x3, starting transfers between devices, swap_far(): lax.ppermute(block, ('dp', 'ep'), [(i, i ^ flip) for i in range(places)])  12.2 us
    ppermute x3, waiting for transfers between devices, swap_far(): lax.ppermute(block, ('dp', 'ep'), [(i, i ^ flip) for i in range(places)])  11.8 us
    pallas_call x2, Pallas kernels, first_stage(): pl.pallas_call(first_kernel, grid_spec=pltpu.PrefetchScalarGridSpec(num_s...  8.35 us
  transfers between devices with their start and end apart: 15, of which 7 were waited for; matrix products, arithmetic and copies ran while one was open for 2% of the time, Pallas kernels for 6%

profile of v3, /device:TPU:10, one launch (start us, length us, event | category | flops | bytes accessed | tf_op | source)
XLA Modules:
  0.0 194.0 jit_solution(7897320492427655770)
XLA Ops:
  0.7 0.8 multiply_add_fusion
  1.5 0.9 fusion.15
  2.5 6.8 %collective-permute-start.1 = (bf16[24,4224]{1,0:T(8,128)(2,1)S(1)}, bf16[24,4224]{1,0:T(8,128)(2,1)S(1)}, u32[]{:S(2)}, u32[]{:S(2)}) collective-permute-start(bf16[24,4224]{1,0:T(8,128)(2,1)S(1)} %fusion.15), channel_id=1, source_target_pairs={{0,256},{1,257},{2,258},{3,259},{4,260},{5,261},{6,262},{7,263},{8... | collective-permute-start | bytes 608264 | tf_op jit(solution)/shard_map/ppermute | solution.py:59
  9.3 3.3 %collective-permute-start.2 = (bf16[24,4224]{1,0:T(8,128)(2,1)S(1)}, bf16[24,4224]{1,0:T(8,128)(2,1)S(1)}, u32[]{:S(2)}, u32[]{:S(2)}) collective-permute-start(bf16[24,4224]{1,0:T(8,128)(2,1)S(1)} %fusion.15), channel_id=1, source_target_pairs={{0,8},{1,9},{2,10},{3,11},{4,12},{5,13},{6,14},{7,15},{8,0},{9,1},... | collective-permute-start | bytes 608264 | tf_op jit(solution)/shard_map/ppermute | solution.py:59
  12.6 2.1 %collective-permute-start.3 = (bf16[24,4224]{1,0:T(8,128)(2,1)S(1)}, bf16[24,4224]{1,0:T(8,128)(2,1)S(1)}, u32[]{:S(2)}, u32[]{:S(2)}) collective-permute-start(bf16[24,4224]{1,0:T(8,128)(2,1)S(1)} %fusion.15), channel_id=1, source_target_pairs={{0,264},{1,265},{2,266},{3,267},{4,268},{5,269},{6,270},{7,271},{8... | collective-permute-start | bytes 608264 | tf_op jit(solution)/shard_map/ppermute | solution.py:59
  14.7 0.8 copy.82
  16.1 4.7 %collective-permute-done.1.refs_1_ = bf16[24,4224]{1,0:T(8,128)(2,1)S(1)} collective-permute-done((bf16[24,4224]{1,0:T(8,128)(2,1)S(1)}, bf16[24,4224]{1,0:T(8,128)(2,1)S(1)}, u32[]{:S(2)}, u32[]{:S(2)}) %collective-permute-start.1) | collective-permute-done | bytes 202784 | tf_op jit(solution)/shard_map/ppermute | solution.py:59
  21.4 7.0 %collective-permute-done.2.refs_2_ = bf16[24,4224]{1,0:T(8,128)(2,1)S(1)} collective-permute-done((bf16[24,4224]{1,0:T(8,128)(2,1)S(1)}, bf16[24,4224]{1,0:T(8,128)(2,1)S(1)}, u32[]{:S(2)}, u32[]{:S(2)}) %collective-permute-start.2) | collective-permute-done | bytes 202784 | tf_op jit(solution)/shard_map/ppermute | solution.py:59
  30.2 5.1 %dispatch_rows.1 = bf16[256,4096]{1,0:T(8,128)(2,1)} custom-call(bf16[256,96]{1,0:T(8,128)(2,1)} %fusion.17.choose_ref, bf16[24,4096]{1,0:T(8,128)(2,1)} %refs_0_.1, bf16[24,4224]{1,0:T(8,128)(2,1)} %copy-done.6, bf16[24,4224]{1,0:T(8,128)(2,1)} %copy-done.7, bf16[24,4224]{1,0:T(8,128)(2,1)} %copy-done.8), custom_call_target="tpu_custom_call" | custom-call | tf_op jit(solution)/shard_map/dispatch_rows/pallas_call | solution.py:87
  35.4 13.6 %all-to-all-start = ((bf16[32,8,4096]{2,1,0:T(8,128)(2,1)}), bf16[32,8,4096]{2,1,0:T(8,128)(2,1)S(1)}, u32[]{:S(2)}, u32[]{:S(2)}) async-start(bf16[32,8,4096]{2,1,0:T(8,128)(2,1)} %bitcast.74), calls=%async_computation | async-start | bytes 4194304 | tf_op jit(solution)/shard_map/all_to_all | solution.py:269
  49.0 1.9 collective-permute-start.6
  50.9 6.5 %collective-permute-start.10 = (bf16[1024,512]{1,0:T(8,128)(2,1)S(1)}, bf16[1024,512]{1,0:T(8,128)(2,1)}, u32[]{:S(2)}, u32[]{:S(2)}) collective-permute-start(bf16[1024,512]{1,0:T(8,128)(2,1)S(1)} %bitcast.78), channel_id=1, source_target_pairs={{0,384},{64,448},{128,256},{192,320},{256,128},{320,192},{384,0},{... | collective-permute-start | bytes 3145736 | tf_op jit(solution)/shard_map/ppermute | solution.py:55
  57.4 38.5 %collective-permute-done.6.left_ref = bf16[4096,128]{1,0:T(8,128)(2,1)S(1)} collective-permute-done((bf16[4096,128]{1,0:T(8,128)(2,1)}, bf16[4096,128]{1,0:T(8,128)(2,1)S(1)}, u32[]{:S(2)}, u32[]{:S(2)}) %collective-permute-start.6) | collective-permute-done | bytes 1048608 | tf_op jit(solution)/shard_map/ppermute | solution.py:55
  96.0 1.9 collective-permute-start.7
  97.9 2.4 %collective-permute-start.4 = (bf16[4096,128]{1,0:T(8,128)(2,1)}, bf16[4096,128]{1,0:T(8,128)(2,1)}, u32[]{:S(2)}, u32[]{:S(2)}) collective-permute-start(bf16[4096,128]{1,0:T(8,128)(2,1)} %bitcast.83), channel_id=1, source_target_pairs={{0,64},{64,0},{128,192},{192,128},{256,320},{320,256},{384,448},{4... | collective-permute-start | bytes 3145736 | tf_op jit(solution)/shard_map/ppermute | solution.py:55
  100.3 1.9 collective-permute-start.9
  102.2 2.4 %collective-permute-start.11 = (bf16[1024,512]{1,0:T(8,128)(2,1)}, bf16[1024,512]{1,0:T(8,128)(2,1)}, u32[]{:S(2)}, u32[]{:S(2)}) collective-permute-start(bf16[1024,512]{1,0:T(8,128)(2,1)} %collective-permute-done.10.refs_2_), channel_id=1, source_target_pairs={{0,64},{64,0},{128,192},{192,128},{256,320},{320,256},{384,448},{4... | collective-permute-start | bytes 3145736 | tf_op jit(solution)/shard_map/ppermute | solution.py:55
  104.7 1.3 copy-done.1
  106.0 4.2 %first_stage.3.odd_ref = bf16[256,256]{1,0:T(8,128)(2,1)} custom-call(s32[1]{0:T(128)} %bitcast.6.place_ref, bf16[256,4096]{1,0:T(8,128)(2,1)} %bitcast.72, bf16[4096,128]{1,0:T(8,128)(2,1)} %copy-done.3, bf16[4096,128]{1,0:T(8,128)(2,1)} %collective-permute-done.7.right_ref), custom_call_target="tpu_custom_call" | custom-call | tf_op jit(solution)/shard_map/first_stage/pallas_call | solution.py:122
  110.2 6.3 %collective-permute-start.8 = (bf16[256,256]{1,0:T(8,128)(2,1)}, bf16[256,256]{1,0:T(8,128)(2,1)S(1)}, u32[]{:S(2)}, u32[]{:S(2)}) collective-permute-start(bf16[256,256]{1,0:T(8,128)(2,1)} %first_stage.3.odd_ref), channel_id=1, source_target_pairs={{0,256},{64,320},{128,384},{192,448},{256,0},{320,64},{384,128},{4... | collective-permute-start | bytes 393224 | tf_op jit(solution)/shard_map/ppermute | solution.py:55
  116.5 4.2 %first_stage.2.even_ref = bf16[256,256]{1,0:T(8,128)(2,1)} custom-call(s32[1]{0:T(128)} %bitcast.6.place_ref, bf16[256,4096]{1,0:T(8,128)(2,1)} %bitcast.73, bf16[4096,128]{1,0:T(8,128)(2,1)} %bitcast.84, bf16[4096,128]{1,0:T(8,128)(2,1)} %collective-permute-done.4.right_ref), custom_call_target="tpu_custom_call" | custom-call | tf_op jit(solution)/shard_map/first_stage/pallas_call | solution.py:122
  120.7 3.4 %collective-permute-start.5 = (bf16[256,256]{1,0:T(8,128)(2,1)}, bf16[256,256]{1,0:T(8,128)(2,1)S(1)}, u32[]{:S(2)}, u32[]{:S(2)}) collective-permute-start(bf16[256,256]{1,0:T(8,128)(2,1)} %first_stage.2.even_ref), channel_id=1, source_target_pairs={{0,256},{64,320},{128,384},{192,448},{256,0},{320,64},{384,128},{4... | collective-permute-start | bytes 393224 | tf_op jit(solution)/shard_map/ppermute | solution.py:55
  124.1 3.7 %second_near.1.refs_4_ = f32[256,2048]{1,0:T(8,128)} custom-call(s32[1]{0:T(128)} %bitcast.6.place_ref, bf16[256,256]{1,0:T(8,128)(2,1)} %first_stage.2.even_ref, bf16[256,256]{1,0:T(8,128)(2,1)} %first_stage.3.odd_ref, bf16[1024,512]{1,0:T(8,128)(2,1)} %bitcast.76, bf16[1024,512]{1,0:T(8,128)(2,1)} %collective-permute-done.9.refs_1_, ...), custom_call_target="tpu_custom_call" | custom-call | tf_op jit(solution)/shard_map/second_near/pallas_call | solution.py:196
  127.8 4.1 %collective-permute-done.5.even_ref = bf16[256,256]{1,0:T(8,128)(2,1)S(1)} collective-permute-done((bf16[256,256]{1,0:T(8,128)(2,1)}, bf16[256,256]{1,0:T(8,128)(2,1)S(1)}, u32[]{:S(2)}, u32[]{:S(2)}) %collective-permute-start.5) | collective-permute-done | bytes 131104 | tf_op jit(solution)/shard_map/ppermute | solution.py:55
  132.6 4.1 %second_far.1 = bf16[4,2,8,4,2048]{4,3,2,1,0:T(4,128)(2,1)} custom-call(s32[1]{0:T(128)} %bitcast.6.place_ref, bf16[256,256]{1,0:T(8,128)(2,1)} %copy-done.10, bf16[256,256]{1,0:T(8,128)(2,1)} %copy-done.9, bf16[1024,512]{1,0:T(8,128)(2,1)} %bitcast.77, bf16[1024,512]{1,0:T(8,128)(2,1)} %collective-permute-done.9.refs_1_, ...), custom_call_target="tpu_custom_call" | custom-call | tf_op jit(solution)/shard_map/second_far/pallas_call | solution.py:205
  136.7 14.9 %all-to-all-start.1 = ((bf16[64,4,2048]{2,1,0:T(4,128)(2,1)}), bf16[64,4,2048]{2,1,0:T(4,128)(2,1)S(1)}, u32[]{:S(2)}, u32[]{:S(2)}) async-start(bf16[64,4,2048]{2,1,0:T(4,128)(2,1)} %bitcast.75), calls=%async_computation.1 | async-start | bytes 2097152 | tf_op jit(solution)/shard_map/all_to_all | solution.py:304
  151.9 5.3 %collective-permute-start = (f32[24,2]{0,1:T(2,128)S(1)}, f32[24,2]{0,1:T(2,128)S(1)}, u32[]{:S(2)}, u32[]{:S(2)}) collective-permute-start(f32[24,2]{0,1:T(2,128)S(1)} %broadcast_divide_fusion), channel_id=1, source_target_pairs={{0,256},{64,320},{128,384},{192,448},{256,0},{320,64},{384,128},{4... | collective-permute-start | bytes 584 | tf_op jit(solution)/shard_map/ppermute | solution.py:55
  158.8 6.7 %collective-permute-done = f32[24,2]{0,1:T(2,128)S(1)} collective-permute-done((f32[24,2]{0,1:T(2,128)S(1)}, f32[24,2]{0,1:T(2,128)S(1)}, u32[]{:S(2)}, u32[]{:S(2)}) %collective-permute-start) | collective-permute-done | bytes 224 | tf_op jit(solution)/shard_map/ppermute | solution.py:55
  165.8 14.3 %all-to-all-done.1 = bf16[64,4,2048]{2,1,0:T(4,128)(2,1)S(1)} async-done(((bf16[64,4,2048]{2,1,0:T(4,128)(2,1)}), bf16[64,4,2048]{2,1,0:T(4,128)(2,1)S(1)}, u32[]{:S(2)}, u32[]{:S(2)}) %all-to-all-start.1) | async-done | bytes 1048608 | tf_op jit(solution)/shard_map/all_to_all | solution.py:304
  181.1 4.4 %collective-permute-start.12 = (bf16[24,2048]{1,0:T(8,128)(2,1)S(1)}, bf16[24,2048]{1,0:T(8,128)(2,1)S(1)}, u32[]{:S(2)}, u32[]{:S(2)}) collective-permute-start(bf16[24,2048]{1,0:T(8,128)(2,1)S(1)} %slice.56), channel_id=1, source_target_pairs={{0,256},{64,320},{128,384},{192,448},{256,0},{320,64},{384,128},{4... | collective-permute-start | bytes 294920 | tf_op jit(solution)/shard_map/ppermute | solution.py:55
  186.5 6.6 %collective-permute-done.12 = bf16[24,2048]{1,0:T(8,128)(2,1)S(1)} collective-permute-done((bf16[24,2048]{1,0:T(8,128)(2,1)S(1)}, bf16[24,2048]{1,0:T(8,128)(2,1)S(1)}, u32[]{:S(2)}, u32[]{:S(2)}) %collective-permute-start.12) | collective-permute-done | bytes 98336 | tf_op jit(solution)/shard_map/ppermute | solution.py:55
  193.3 0.7 copy-done.14
  (99 shorter events, 7.1 us)
Async XLA Ops:
  0.6 157.5 %copy-start = (bf16[24,2048]{1,0:T(8,128)(2,1)S(1)}, bf16[24,2048]{1,0:T(8,128)(2,1)}, u32[]{:S(2)}) copy-start(bf16[24,2048]{1,0:T(8,128)(2,1)} %param.17) | copy-start | bytes 294916
  2.5 18.4 %collective-permute-start.1 = (bf16[24,4224]{1,0:T(8,128)(2,1)S(1)}, bf16[24,4224]{1,0:T(8,128)(2,1)S(1)}, u32[]{:S(2)}, u32[]{:S(2)}) collective-permute-start(bf16[24,4224]{1,0:T(8,128)(2,1)S(1)} %fusion.15), channel_id=1, source_target_pairs={{0,256},{1,257},{2,258},{3,259},{4,260},{5,261},{6,262},{7,263},{8... | collective-permute-start | bytes 608264 | tf_op jit(solution)/shard_map/ppermute | solution.py:59
  9.3 19.1 %collective-permute-start.2 = (bf16[24,4224]{1,0:T(8,128)(2,1)S(1)}, bf16[24,4224]{1,0:T(8,128)(2,1)S(1)}, u32[]{:S(2)}, u32[]{:S(2)}) collective-permute-start(bf16[24,4224]{1,0:T(8,128)(2,1)S(1)} %fusion.15), channel_id=1, source_target_pairs={{0,8},{1,9},{2,10},{3,11},{4,12},{5,13},{6,14},{7,15},{8,0},{9,1},... | collective-permute-start | bytes 608264 | tf_op jit(solution)/shard_map/ppermute | solution.py:59
  12.6 16.4 %collective-permute-start.3 = (bf16[24,4224]{1,0:T(8,128)(2,1)S(1)}, bf16[24,4224]{1,0:T(8,128)(2,1)S(1)}, u32[]{:S(2)}, u32[]{:S(2)}) collective-permute-start(bf16[24,4224]{1,0:T(8,128)(2,1)S(1)} %fusion.15), channel_id=1, source_target_pairs={{0,264},{1,265},{2,266},{3,267},{4,268},{5,269},{6,270},{7,271},{8... | collective-permute-start | bytes 608264 | tf_op jit(solution)/shard_map/ppermute | solution.py:59
  20.8 9.4 %copy-start.6 = (bf16[24,4224]{1,0:T(8,128)(2,1)}, bf16[24,4224]{1,0:T(8,128)(2,1)S(1)}, u32[]{:S(2)}) copy-start(bf16[24,4224]{1,0:T(8,128)(2,1)S(1)} %collective-permute-done.1.refs_1_) | copy-start | bytes 608260
  28.4 1.8 copy-start.7
  29.0 1.3 copy-start.8
  35.3 15.5 %copy-start.2 = (bf16[1,1024,512]{2,1,0:T(8,128)(2,1)S(1)}, bf16[1,1024,512]{2,1,0:T(8,128)(2,1)}, u32[]{:S(2)}) copy-start(bf16[1,1024,512]{2,1,0:T(8,128)(2,1)} %param.15) | copy-start | bytes 3145732
  35.4 69.3 %all-to-all-start = ((bf16[32,8,4096]{2,1,0:T(8,128)(2,1)}), bf16[32,8,4096]{2,1,0:T(8,128)(2,1)S(1)}, u32[]{:S(2)}, u32[]{:S(2)}) async-start(bf16[32,8,4096]{2,1,0:T(8,128)(2,1)} %bitcast.74), calls=%async_computation | async-start | bytes 4194304 | tf_op jit(solution)/shard_map/all_to_all | solution.py:269
  49.0 47.0 %collective-permute-start.6 = (bf16[4096,128]{1,0:T(8,128)(2,1)}, bf16[4096,128]{1,0:T(8,128)(2,1)S(1)}, u32[]{:S(2)}, u32[]{:S(2)}) collective-permute-start(bf16[4096,128]{1,0:T(8,128)(2,1)} %bitcast.82), channel_id=1, source_target_pairs={{0,128},{64,192},{128,0},{192,64},{256,384},{320,448},{384,256},{4... | collective-permute-start | bytes 3145736 | tf_op jit(solution)/shard_map/ppermute | solution.py:55
  50.9 51.3 %collective-permute-start.10 = (bf16[1024,512]{1,0:T(8,128)(2,1)S(1)}, bf16[1024,512]{1,0:T(8,128)(2,1)}, u32[]{:S(2)}, u32[]{:S(2)}) collective-permute-start(bf16[1024,512]{1,0:T(8,128)(2,1)S(1)} %bitcast.78), channel_id=1, source_target_pairs={{0,384},{64,448},{128,256},{192,320},{256,128},{320,192},{384,0},{... | collective-permute-start | bytes 3145736 | tf_op jit(solution)/shard_map/ppermute | solution.py:55
  96.0 8.7 %copy-start.3 = (bf16[4096,128]{1,0:T(8,128)(2,1)}, bf16[4096,128]{1,0:T(8,128)(2,1)S(1)}, u32[]{:S(2)}) copy-start(bf16[4096,128]{1,0:T(8,128)(2,1)S(1)} %collective-permute-done.6.left_ref) | copy-start | bytes 3145732
  96.0 8.7 %collective-permute-start.7 = (bf16[4096,128]{1,0:T(8,128)(2,1)S(1)}, bf16[4096,128]{1,0:T(8,128)(2,1)}, u32[]{:S(2)}, u32[]{:S(2)}) collective-permute-start(bf16[4096,128]{1,0:T(8,128)(2,1)S(1)} %collective-permute-done.6.left_ref), channel_id=1, source_target_pairs={{0,64},{64,0},{128,192},{192,128},{256,320},{320,256},{384,448},{4... | collective-permute-start | bytes 3145736 | tf_op jit(solution)/shard_map/ppermute | solution.py:55
  97.9 18.6 %collective-permute-start.4 = (bf16[4096,128]{1,0:T(8,128)(2,1)}, bf16[4096,128]{1,0:T(8,128)(2,1)}, u32[]{:S(2)}, u32[]{:S(2)}) collective-permute-start(bf16[4096,128]{1,0:T(8,128)(2,1)} %bitcast.83), channel_id=1, source_target_pairs={{0,64},{64,0},{128,192},{192,128},{256,320},{320,256},{384,448},{4... | collective-permute-start | bytes 3145736 | tf_op jit(solution)/shard_map/ppermute | solution.py:55
  100.3 23.8 %collective-permute-start.9 = (bf16[1024,512]{1,0:T(8,128)(2,1)S(1)}, bf16[1024,512]{1,0:T(8,128)(2,1)}, u32[]{:S(2)}, u32[]{:S(2)}) collective-permute-start(bf16[1024,512]{1,0:T(8,128)(2,1)S(1)} %bitcast.79), channel_id=1, source_target_pairs={{0,64},{64,0},{128,192},{192,128},{256,320},{320,256},{384,448},{4... | collective-permute-start | bytes 3145736 | tf_op jit(solution)/shard_map/ppermute | solution.py:55
  102.2 21.9 %collective-permute-start.11 = (bf16[1024,512]{1,0:T(8,128)(2,1)}, bf16[1024,512]{1,0:T(8,128)(2,1)}, u32[]{:S(2)}, u32[]{:S(2)}) collective-permute-start(bf16[1024,512]{1,0:T(8,128)(2,1)} %collective-permute-done.10.refs_2_), channel_id=1, source_target_pairs={{0,64},{64,0},{128,192},{192,128},{256,320},{320,256},{384,448},{4... | collective-permute-start | bytes 3145736 | tf_op jit(solution)/shard_map/ppermute | solution.py:55
  104.7 1.3 copy-start.1
  110.2 17.6 %collective-permute-start.8 = (bf16[256,256]{1,0:T(8,128)(2,1)}, bf16[256,256]{1,0:T(8,128)(2,1)S(1)}, u32[]{:S(2)}, u32[]{:S(2)}) collective-permute-start(bf16[256,256]{1,0:T(8,128)(2,1)} %first_stage.3.odd_ref), channel_id=1, source_target_pairs={{0,256},{64,320},{128,384},{192,448},{256,0},{320,64},{384,128},{4... | collective-permute-start | bytes 393224 | tf_op jit(solution)/shard_map/ppermute | solution.py:55
  120.7 11.2 %collective-permute-start.5 = (bf16[256,256]{1,0:T(8,128)(2,1)}, bf16[256,256]{1,0:T(8,128)(2,1)S(1)}, u32[]{:S(2)}, u32[]{:S(2)}) collective-permute-start(bf16[256,256]{1,0:T(8,128)(2,1)} %first_stage.2.even_ref), channel_id=1, source_target_pairs={{0,256},{64,320},{128,384},{192,448},{256,0},{320,64},{384,128},{4... | collective-permute-start | bytes 393224 | tf_op jit(solution)/shard_map/ppermute | solution.py:55
  127.8 4.1 %copy-start.9 = (bf16[256,256]{1,0:T(8,128)(2,1)}, bf16[256,256]{1,0:T(8,128)(2,1)S(1)}, u32[]{:S(2)}) copy-start(bf16[256,256]{1,0:T(8,128)(2,1)S(1)} %collective-permute-done.8.odd_ref) | copy-start | bytes 393220
  131.9 0.7 copy-start.10
  136.7 15.0 %copy-start.13 = (s32[24,2]{0,1:T(2,128)S(1)}, s32[24,2]{0,1:T(2,128)}, u32[]{:S(2)}) copy-start(s32[24,2]{0,1:T(2,128)} %param.12) | copy-start | bytes 580
  136.7 15.0 %copy-start.12 = (f32[24,64]{1,0:T(8,128)S(1)}, f32[24,64]{1,0:T(8,128)}, u32[]{:S(2)}) copy-start(f32[24,64]{1,0:T(8,128)} %param.13) | copy-start | bytes 18436
  136.7 20.6 %copy-start.4 = (bf16[1,72,2048]{2,1,0:T(8,128)(2,1)S(1)}, bf16[1,72,2048]{2,1,0:T(8,128)(2,1)}, u32[]{:S(2)}) copy-start(bf16[1,72,2048]{2,1,0:T(8,128)(2,1)} %param.19) | copy-start | bytes 884740
  136.7 21.5 %copy-start.11 = (bf16[24,2048]{1,0:T(8,128)(2,1)S(1)}, bf16[24,2048]{1,0:T(8,128)(2,1)}, u32[]{:S(2)}) copy-start(bf16[24,2048]{1,0:T(8,128)(2,1)} %param.18) | copy-start | bytes 294916
  136.7 21.5 %copy-start.15 = (bf16[24,2048]{1,0:T(8,128)(2,1)S(1)}, bf16[24,2048]{1,0:T(8,128)(2,1)}, u32[]{:S(2)}) copy-start(bf16[24,2048]{1,0:T(8,128)(2,1)} %param.16) | copy-start | bytes 294916
  136.7 22.0 %copy-start.5 = (bf16[1,72,2048]{2,1,0:T(8,128)(2,1)S(1)}, bf16[1,72,2048]{2,1,0:T(8,128)(2,1)}, u32[]{:S(2)}) copy-start(bf16[1,72,2048]{2,1,0:T(8,128)(2,1)} %param.20) | copy-start | bytes 884740
  136.7 43.4 %all-to-all-start.1 = ((bf16[64,4,2048]{2,1,0:T(4,128)(2,1)}), bf16[64,4,2048]{2,1,0:T(4,128)(2,1)S(1)}, u32[]{:S(2)}, u32[]{:S(2)}) async-start(bf16[64,4,2048]{2,1,0:T(4,128)(2,1)} %bitcast.75), calls=%async_computation.1 | async-start | bytes 2097152 | tf_op jit(solution)/shard_map/all_to_all | solution.py:304
  151.9 13.6 %collective-permute-start = (f32[24,2]{0,1:T(2,128)S(1)}, f32[24,2]{0,1:T(2,128)S(1)}, u32[]{:S(2)}, u32[]{:S(2)}) collective-permute-start(f32[24,2]{0,1:T(2,128)S(1)} %broadcast_divide_fusion), channel_id=1, source_target_pairs={{0,256},{64,320},{128,384},{192,448},{256,0},{320,64},{384,128},{4... | collective-permute-start | bytes 584 | tf_op jit(solution)/shard_map/ppermute | solution.py:55
  181.1 11.9 %collective-permute-start.12 = (bf16[24,2048]{1,0:T(8,128)(2,1)S(1)}, bf16[24,2048]{1,0:T(8,128)(2,1)S(1)}, u32[]{:S(2)}, u32[]{:S(2)}) collective-permute-start(bf16[24,2048]{1,0:T(8,128)(2,1)S(1)} %slice.56), channel_id=1, source_target_pairs={{0,256},{64,320},{128,384},{192,448},{256,0},{320,64},{384,128},{4... | collective-permute-start | bytes 294920 | tf_op jit(solution)/shard_map/ppermute | solution.py:55
  193.3 0.7 copy-start.14

commit v4 on v0

--- a/solution.py
+++ b/solution.py
@@ -3,11 +3,17 @@
 import jax
 import jax.numpy as jnp
 from jax import lax
+from jax.experimental import pallas as pl
+from jax.experimental.pallas import tpu as pltpu
 from jax.sharding import PartitionSpec as P
+
 
 HEADS = 16
 HEAD_DIM = 128
 FRAME_TOK = 24
+
+CORE_FLIP, FIRST_FLIP, ROW_FLIP, SECOND_FLIP = 1, 2, 4, 6
+ACT_BLOCK = 256
 
 
 def activate(pre):
@@ -44,6 +50,94 @@
     return result.astype(jnp.bfloat16).reshape(token_count, HEADS * HEAD_DIM)
 
 
+def swap(block, flip):
+    return lax.ppermute(block, "dp", [(place, place ^ flip) for place in range(8)])
+
+
+def four_parts(block, flip, pieces):
+    mate = jnp.concatenate(
+        [swap(piece, flip) for piece in jnp.split(block, pieces, axis=0)],
+        axis=0,
+    )
+    return [block, swap(block, CORE_FLIP), mate, swap(mate, CORE_FLIP)]
+
+
+def in_vmem(kernel, shape, dtype, place, *operands, to_hbm=False):
+    operands = [pltpu.with_memory_space_constraint(operand, pltpu.VMEM) for operand in operands]
+    specs = [pl.BlockSpec(memory_space=pltpu.VMEM)] * len(operands)
+    if place is not None:
+        operands, specs = [place] + operands, [pl.BlockSpec(memory_space=pltpu.SMEM)] + specs
+    return pl.pallas_call(
+        kernel,
+        in_specs=specs,
+        out_specs=pl.BlockSpec(memory_space=pltpu.VMEM),
+        out_shape=jax.ShapeDtypeStruct(shape, dtype) if to_hbm else pltpu.VMEM(shape, dtype),
+        compiler_params=pltpu.CompilerParams(vmem_limit_bytes=8 << 20),
+    )(*operands)
+
+
+def dispatch_kernel(choose_ref, *refs):
+    token_refs, out_ref = refs[:-1], refs[-1]
+    tokens, width = token_refs[0].shape[0], out_ref.shape[-1]
+    step = 512
+    for at in range(0, width, step):
+        lanes = slice(at, at + step)
+        rows = None
+        for index, token_ref in enumerate(token_refs):
+            part = jnp.dot(
+                choose_ref[:, index * tokens : (index + 1) * tokens],
+                token_ref[:, lanes],
+                preferred_element_type=jnp.float32,
+            )
+            rows = part if rows is None else rows + part
+        out_ref[..., lanes] = rows.astype(jnp.bfloat16).reshape(out_ref.shape[:-1] + (step,))
+
+
+def first_kernel(place_ref, rows_ref, left_ref, right_ref, act_ref):
+    depth, half, step = left_ref.shape[0], left_ref.shape[1], 1024
+    total = None
+    for at in range(0, depth, step):
+        lanes = slice(at, at + step)
+        rows = rows_ref[..., lanes].reshape(act_ref.shape[0], step)
+        wide = jnp.concatenate([left_ref[lanes, :], right_ref[lanes, :]], axis=1)
+        part = jnp.dot(rows, wide, preferred_element_type=jnp.float32)
+        total = part if total is None else total + part
+    act = activate(total)
+    odd = place_ref[0] % 2 == 1
+    left, right = act[:, :half], act[:, half:]
+    act_ref[:, :half] = jnp.where(odd, right, left)
+    act_ref[:, half:] = jnp.where(odd, left, right)
+
+
+def second_dot(place_ref, even_ref, odd_ref, part_ref, first_block):
+    ring = place_ref[0] // 2
+    base = ((ring ^ first_block) // 2) * (2 * ACT_BLOCK)
+    base = pl.multiple_of(base, 2 * ACT_BLOCK)
+    turned = ring % 2 == 1
+    even, odd = even_ref[...], odd_ref[...]
+    act = jnp.concatenate([jnp.where(turned, odd, even), jnp.where(turned, even, odd)], axis=1)
+    return jnp.dot(
+        act, part_ref[pl.ds(base, 2 * ACT_BLOCK), :], preferred_element_type=jnp.float32
+    )
+
+
+def near_kernel(place_ref, even_ref, odd_ref, *refs):
+    part_refs, sums_ref = refs[:4], refs[4]
+    wide = part_refs[0].shape[1]
+    for index, part_ref in enumerate(part_refs):
+        lanes = slice(index * wide, (index + 1) * wide)
+        sums_ref[:, lanes] = second_dot(place_ref, even_ref, odd_ref, part_ref, 0)
+
+
+def far_kernel(place_ref, even_ref, odd_ref, *refs):
+    part_refs, before_ref, out_ref = refs[:4], refs[4], refs[5]
+    wide = part_refs[0].shape[1]
+    for index, part_ref in enumerate(part_refs):
+        lanes = slice(index * wide, (index + 1) * wide)
+        total = before_ref[:, lanes] + second_dot(place_ref, even_ref, odd_ref, part_ref, 2)
+        out_ref[..., lanes] = total.astype(jnp.bfloat16).reshape(out_ref.shape[:-1] + (wide,))
+
+
 def shards(
     hidden_in,
     expert_ids,
@@ -59,16 +153,49 @@
 ):
     tokens, model_width = hidden_in.shape
     experts = lax.axis_size("ep")
-    capacity = max(2, 8 * tokens // (3 * experts))
-    slots = expert_slots(expert_ids)
-    places = expert_ids * capacity + slots
-    place_ids = lax.broadcasted_iota(jnp.int32, (tokens, experts * capacity), 1)
+    place = lax.axis_index("dp")
+    place_list = place.reshape(1).astype(jnp.int32)
+
+    first_parts = four_parts(first_weight[0], FIRST_FLIP, 1)
+    second_parts = four_parts(second_weight[0], SECOND_FLIP, 1)
+
+    tail = jnp.pad(expert_ids.astype(jnp.bfloat16), ((0, 0), (0, 126)))
+    mate_rows = swap(jnp.concatenate([hidden_in, tail], axis=1), ROW_FLIP)
+    ids_mate = mate_rows[:, model_width : model_width + 2].astype(jnp.int32)
+    upper = place // 4
+    places = jnp.concatenate(
+        [
+            expert_ids * 4 + 2 * upper + expert_slots(expert_ids),
+            ids_mate * 4 + 2 * (1 - upper) + expert_slots(ids_mate),
+        ],
+        axis=0,
+    )
+    place_ids = lax.broadcasted_iota(jnp.int32, (2 * tokens, experts * 4), 1)
     picks = [places[:, column : column + 1] == place_ids for column in range(2)]
-    chooser = (picks[0] | picks[1]).astype(jnp.bfloat16)
-    dispatch = lax.dot_general(
-        chooser, hidden_in, (((0,), (0,)), ((), ())), preferred_element_type=jnp.float32
-    )
-    dispatch = dispatch.astype(jnp.bfloat16).reshape(experts, capacity, model_width)
+    place_rows = lax.broadcasted_iota(jnp.int32, (experts * 4, 2 * tokens), 0)
+    choose = (places[:, 0][None, :] == place_rows) | (places[:, 1][None, :] == place_rows)
+
+    dispatch = in_vmem(
+        dispatch_kernel,
+        (experts, 4, model_width),
+        jnp.bfloat16,
+        None,
+        choose.astype(jnp.bfloat16),
+        hidden_in,
+        mate_rows,
+        to_hbm=True,
+    )
+    received = lax.all_to_all(dispatch, "ep", split_axis=0, concat_axis=0, tiled=True)
+
+    near, far = [], []
+    for index in range(2):
+        left, right = first_parts[2 * index : 2 * index + 2]
+        act = in_vmem(
+            first_kernel, (experts * 4, ACT_BLOCK), jnp.bfloat16, place_list, received, left, right
+        )
+        near.append(act)
+        far.append(swap(act, ROW_FLIP))
+
     expert_cols = lax.broadcasted_iota(jnp.int32, route_logits.shape, 1)
     chosen = jnp.stack(
         [
@@ -81,36 +208,44 @@
         axis=1,
     )
     gates = jax.nn.softmax(chosen, axis=1)
-    first_local = first_weight[0]
-    second_local = second_weight[0]
-    received = lax.all_to_all(dispatch, "ep", split_axis=0, concat_axis=0, tiled=True)
-    sources, item_count, _ = received.shape
-    expert_rows = received.reshape(sources * item_count, model_width)
-    hidden = activate(
-        jnp.dot(
-            expert_rows,
-            lax.all_gather(first_local, "dp", axis=1, tiled=True),
-            preferred_element_type=jnp.float32,
-        )
-    )
-    result = jnp.dot(
-        hidden,
-        lax.all_gather(second_local, "dp", axis=1, tiled=True),
-        preferred_element_type=jnp.float32,
-    ).astype(jnp.bfloat16)
-    outputs = result.reshape(sources, item_count, model_width)
+    both_gates = jnp.concatenate([gates, swap(gates, ROW_FLIP)], axis=0)
+
+    width = 4 * second_parts[0].shape[1]
+    sums = in_vmem(near_kernel, (experts * 4, width), jnp.float32, place_list, *near, *second_parts)
+    outputs = in_vmem(
+        far_kernel,
+        (experts, 4) + (width,),
+        jnp.bfloat16,
+        place_list,
+        *far,
+        *second_parts,
+        sums,
+        to_hbm=True,
+    )
     returned = lax.all_to_all(outputs, "ep", split_axis=0, concat_axis=0, tiled=True)
+    flat_back = returned.reshape(experts * 4, width)
+
     attended = attend(
         queries, span_keys, span_values, cache_keys[0], cache_values[0], valid_frames[0]
     )
-    flat_back = returned.reshape(experts * capacity, model_width)
-    running = jnp.zeros((tokens, model_width), jnp.float32)
+
+    running = jnp.zeros((2 * tokens, width), jnp.float32)
     for column in range(2):
         picked = jnp.dot(
             picks[column].astype(jnp.bfloat16), flat_back, preferred_element_type=jnp.float32
         )
-        running = running + gates[:, column : column + 1] * picked
-    mixed = running.astype(jnp.bfloat16)
+        running = running + both_gates[:, column : column + 1] * picked
+    halves = running.astype(jnp.bfloat16)
+    arrived = swap(halves[tokens:], ROW_FLIP)
+    flips = (0, CORE_FLIP, SECOND_FLIP, SECOND_FLIP ^ CORE_FLIP)
+    blocks = [None] * 8
+    for half, flip in ((halves[:tokens], 0), (arrived, ROW_FLIP)):
+        for index, block in enumerate(jnp.split(half, 4, axis=1)):
+            blocks[flips[index] ^ flip] = block
+    for bit in (1, 2, 4):
+        turned = (place & bit) != 0
+        blocks = [jnp.where(turned, blocks[index ^ bit], blocks[index]) for index in range(8)]
+    mixed = jnp.concatenate(blocks, axis=1)
     return (mixed, attended)
 
 

time: 264 us -> 201 us (0.76)
  the two profiles are of different devices: /device:TPU:2 before, /device:TPU:10 now
where the time goes in v4:
time: 201 us; the launch traced here: 200 us
  waiting for transfers between devices  103 us (51%)
  starting transfers between devices  70.8 us (35%)
  Pallas kernels  10.2 us (5%)
  local copies, waits for them, and re-layouts  10.1 us (5%)
  other arithmetic  2.7 us (1%)
    ppermute x11, waiting for transfers between devices, swap(): lax.ppermute(block, 'dp', [(place, place ^ flip) for place in range(8)])  87.8 us
    ppermute x11, starting transfers between devices, swap(): lax.ppermute(block, 'dp', [(place, place ^ flip) for place in range(8)])  44.1 us
    all_to_all x1, starting transfers between devices, shards(): lax.all_to_all(dispatch, 'ep', split_axis=0, concat_axis=0, tiled=True)  14.9 us
    all_to_all x1, waiting for transfers between devices, shards(): lax.all_to_all(outputs, 'ep', split_axis=0, concat_axis=0, tiled=True)  14.9 us
    all_to_all x1, starting transfers between devices, shards(): lax.all_to_all(outputs, 'ep', split_axis=0, concat_axis=0, tiled=True)  11.8 us
    pallas_call x5, Pallas kernels, in_vmem(): pl.pallas_call(kernel, in_specs=specs, out_specs=pl.BlockSpec(memory_spac...  10.2 us
    unnamed x35, local copies, waits for them, and re-layouts  8.27 us
  transfers between devices with their start and end apart: 13, of which 6 were waited for; matrix products, arithmetic and copies ran while one was open for 2% of the time, Pallas kernels for 3%

profile of v4, /device:TPU:10, one launch (start us, length us, event | category | flops | bytes accessed | tf_op | source)
XLA Modules:
  0.0 199.7 jit_solution(17827476923767068601)
XLA Ops:
  0.7 0.8 multiply_add_fusion
  1.5 0.9 fusion.15
  2.5 6.8 %collective-permute-start.1 = (bf16[24,4224]{1,0:T(8,128)(2,1)S(1)}, bf16[24,4224]{1,0:T(8,128)(2,1)S(1)}, u32[]{:S(2)}, u32[]{:S(2)}) collective-permute-start(bf16[24,4224]{1,0:T(8,128)(2,1)S(1)} %fusion.15), channel_id=1, source_target_pairs={{0,256},{64,320},{128,384},{192,448},{256,0},{320,64},{384,128},{4... | collective-permute-start | bytes 608264 | tf_op jit(solution)/shard_map/ppermute | solution.py:54
  9.3 0.8 copy.57
  10.6 7.1 %collective-permute-done.1.refs_1_ = bf16[24,4224]{1,0:T(8,128)(2,1)S(1)} collective-permute-done((bf16[24,4224]{1,0:T(8,128)(2,1)S(1)}, bf16[24,4224]{1,0:T(8,128)(2,1)S(1)}, u32[]{:S(2)}, u32[]{:S(2)}) %collective-permute-start.1) | collective-permute-done | bytes 202784 | tf_op jit(solution)/shard_map/ppermute | solution.py:54
  18.4 0.9 copy-done.8
  19.3 1.3 shard_map.122
  20.6 1.3 copy-done.1
  21.9 14.9 %all-to-all-start = ((bf16[64,4,4096]{2,1,0:T(4,128)(2,1)}), bf16[64,4,4096]{2,1,0:T(4,128)(2,1)S(1)}, u32[]{:S(2)}, u32[]{:S(2)}) async-start(bf16[64,4,4096]{2,1,0:T(4,128)(2,1)} %copy-done.1), calls=%async_computation | async-start | bytes 4194304 | tf_op jit(solution)/shard_map/all_to_all | solution.py:188
  36.9 5.2 %collective-permute-start.4 = (bf16[4096,128]{1,0:T(8,128)(2,1)}, bf16[4096,128]{1,0:T(8,128)(2,1)S(1)}, u32[]{:S(2)}, u32[]{:S(2)}) collective-permute-start(bf16[4096,128]{1,0:T(8,128)(2,1)} %bitcast.69), channel_id=1, source_target_pairs={{0,128},{64,192},{128,0},{192,64},{256,384},{320,448},{384,256},{4... | collective-permute-start | bytes 3145736 | tf_op jit(solution)/shard_map/ppermute | solution.py:54
  42.1 5.6 %collective-permute-start.8 = (bf16[1024,512]{1,0:T(8,128)(2,1)S(1)}, bf16[1024,512]{1,0:T(8,128)(2,1)}, u32[]{:S(2)}, u32[]{:S(2)}) collective-permute-start(bf16[1024,512]{1,0:T(8,128)(2,1)S(1)} %bitcast.65), channel_id=1, source_target_pairs={{0,384},{64,448},{128,256},{192,320},{256,128},{320,192},{384,0},{... | collective-permute-start | bytes 3145736 | tf_op jit(solution)/shard_map/ppermute | solution.py:54
  47.7 60.0 %collective-permute-done.4.left_ref = bf16[4096,128]{1,0:T(8,128)(2,1)S(1)} collective-permute-done((bf16[4096,128]{1,0:T(8,128)(2,1)}, bf16[4096,128]{1,0:T(8,128)(2,1)S(1)}, u32[]{:S(2)}, u32[]{:S(2)}) %collective-permute-start.4) | collective-permute-done | bytes 1048608 | tf_op jit(solution)/shard_map/ppermute | solution.py:54
  107.7 1.9 collective-permute-start.5
  109.6 1.0 copy-done.4
  110.6 2.4 %collective-permute-start.2 = (bf16[4096,128]{1,0:T(8,128)(2,1)}, bf16[4096,128]{1,0:T(8,128)(2,1)}, u32[]{:S(2)}, u32[]{:S(2)}) collective-permute-start(bf16[4096,128]{1,0:T(8,128)(2,1)} %bitcast.70), channel_id=1, source_target_pairs={{0,64},{64,0},{128,192},{192,128},{256,320},{320,256},{384,448},{4... | collective-permute-start | bytes 3145736 | tf_op jit(solution)/shard_map/ppermute | solution.py:54
  113.0 1.9 collective-permute-start.7
  114.9 2.4 %collective-permute-start.9 = (bf16[1024,512]{1,0:T(8,128)(2,1)}, bf16[1024,512]{1,0:T(8,128)(2,1)}, u32[]{:S(2)}, u32[]{:S(2)}) collective-permute-start(bf16[1024,512]{1,0:T(8,128)(2,1)} %collective-permute-done.8.refs_2_), channel_id=1, source_target_pairs={{0,64},{64,0},{128,192},{192,128},{256,320},{320,256},{384,448},{4... | collective-permute-start | bytes 3145736 | tf_op jit(solution)/shard_map/ppermute | solution.py:54
  117.4 1.0 copy-done.6
  118.4 1.2 copy-done.5
  119.6 1.2 copy-done.7
  121.6 5.8 %collective-permute-start.6 = (bf16[256,256]{1,0:T(8,128)(2,1)S(1)}, bf16[256,256]{1,0:T(8,128)(2,1)S(1)}, u32[]{:S(2)}, u32[]{:S(2)}) collective-permute-start(bf16[256,256]{1,0:T(8,128)(2,1)S(1)} %shard_map.124.odd_ref), channel_id=1, source_target_pairs={{0,256},{64,320},{128,384},{192,448},{256,0},{320,64},{384,128},{4... | collective-permute-start | bytes 393224 | tf_op jit(solution)/shard_map/ppermute | solution.py:54
  127.4 2.0 %shard_map.123.even_ref = bf16[256,256]{1,0:T(8,128)(2,1)S(1)} custom-call(s32[1]{0:T(128)} %bitcast.6.place_ref, bf16[64,4,4096]{2,1,0:T(4,128)(2,1)S(1)} %all-to-all-done.rows_ref, bf16[4096,128]{1,0:T(8,128)(2,1)S(1)} %bitcast.71, bf16[4096,128]{1,0:T(8,128)(2,1)} %collective-permute-done.2.right_ref), custom_call_target="tpu_custom_call" | custom-call | tf_op jit(solution)/shard_map/pallas_call | solution.py:70
  129.5 3.9 %collective-permute-start.3 = (bf16[256,256]{1,0:T(8,128)(2,1)S(1)}, bf16[256,256]{1,0:T(8,128)(2,1)S(1)}, u32[]{:S(2)}, u32[]{:S(2)}) collective-permute-start(bf16[256,256]{1,0:T(8,128)(2,1)S(1)} %shard_map.123.even_ref), channel_id=1, source_target_pairs={{0,256},{64,320},{128,384},{192,448},{256,0},{320,64},{384,128},{4... | collective-permute-start | bytes 393224 | tf_op jit(solution)/shard_map/ppermute | solution.py:54
  133.4 2.6 %shard_map.125.refs_4_ = f32[256,2048]{1,0:T(8,128)S(1)} custom-call(s32[1]{0:T(128)} %bitcast.6.place_ref, bf16[256,256]{1,0:T(8,128)(2,1)S(1)} %shard_map.123.even_ref, bf16[256,256]{1,0:T(8,128)(2,1)S(1)} %shard_map.124.odd_ref, bf16[1024,512]{1,0:T(8,128)(2,1)S(1)} %bitcast.67, bf16[1024,512]{1,0:T(8,128)(2,1)} %collective-permute-done.7.refs_1_, ...), custom_call_target="tpu_custom_call" | custom-call | tf_op jit(solution)/shard_map/pallas_call | solution.py:70
  136.0 7.1 %collective-permute-done.3.even_ref = bf16[256,256]{1,0:T(8,128)(2,1)S(1)} collective-permute-done((bf16[256,256]{1,0:T(8,128)(2,1)S(1)}, bf16[256,256]{1,0:T(8,128)(2,1)S(1)}, u32[]{:S(2)}, u32[]{:S(2)}) %collective-permute-start.3) | collective-permute-done | bytes 131104 | tf_op jit(solution)/shard_map/ppermute | solution.py:54
  143.1 3.6 %shard_map.126 = bf16[64,4,2048]{2,1,0:T(4,128)(2,1)} custom-call(s32[1]{0:T(128)} %bitcast.6.place_ref, bf16[256,256]{1,0:T(8,128)(2,1)S(1)} %collective-permute-done.3.even_ref, bf16[256,256]{1,0:T(8,128)(2,1)S(1)} %collective-permute-done.6.odd_ref, bf16[1024,512]{1,0:T(8,128)(2,1)S(1)} %bitcast.68, bf16[1024,512]{1,0:T(8,128)(2,1)} %collective-permute-done.7.refs_1_, ...), custom_call_target="tpu_custom_call" | custom-call | tf_op jit(solution)/shard_map/pallas_call | solution.py:70
  146.8 11.8 %all-to-all-start.1 = ((bf16[64,4,2048]{2,1,0:T(4,128)(2,1)}), bf16[64,4,2048]{2,1,0:T(4,128)(2,1)S(1)}, u32[]{:S(2)}, u32[]{:S(2)}) async-start(bf16[64,4,2048]{2,1,0:T(4,128)(2,1)} %shard_map.126), calls=%async_computation.1 | async-start | bytes 2097152 | tf_op jit(solution)/shard_map/all_to_all | solution.py:225
  158.8 4.0 %collective-permute-start = (f32[24,2]{0,1:T(2,128)S(1)}, f32[24,2]{0,1:T(2,128)S(1)}, u32[]{:S(2)}, u32[]{:S(2)}) collective-permute-start(f32[24,2]{0,1:T(2,128)S(1)} %broadcast_divide_fusion), channel_id=1, source_target_pairs={{0,256},{64,320},{128,384},{192,448},{256,0},{320,64},{384,128},{4... | collective-permute-start | bytes 584 | tf_op jit(solution)/shard_map/ppermute | solution.py:54
  164.4 7.2 %collective-permute-done = f32[24,2]{0,1:T(2,128)S(1)} collective-permute-done((f32[24,2]{0,1:T(2,128)S(1)}, f32[24,2]{0,1:T(2,128)S(1)}, u32[]{:S(2)}, u32[]{:S(2)}) %collective-permute-start) | collective-permute-done | bytes 224 | tf_op jit(solution)/shard_map/ppermute | solution.py:54
  171.6 14.9 %all-to-all-done.1 = bf16[64,4,2048]{2,1,0:T(4,128)(2,1)S(1)} async-done(((bf16[64,4,2048]{2,1,0:T(4,128)(2,1)}), bf16[64,4,2048]{2,1,0:T(4,128)(2,1)S(1)}, u32[]{:S(2)}, u32[]{:S(2)}) %all-to-all-start.1) | async-done | bytes 1048608 | tf_op jit(solution)/shard_map/all_to_all | solution.py:225
  187.5 4.0 %collective-permute-start.10 = (bf16[24,2048]{1,0:T(8,128)(2,1)S(1)}, bf16[24,2048]{1,0:T(8,128)(2,1)S(1)}, u32[]{:S(2)}, u32[]{:S(2)}) collective-permute-start(bf16[24,2048]{1,0:T(8,128)(2,1)S(1)} %slice.40), channel_id=1, source_target_pairs={{0,256},{64,320},{128,384},{192,448},{256,0},{320,64},{384,128},{4... | collective-permute-start | bytes 294920 | tf_op jit(solution)/shard_map/ppermute | solution.py:54
  192.4 6.4 %collective-permute-done.10 = bf16[24,2048]{1,0:T(8,128)(2,1)S(1)} collective-permute-done((bf16[24,2048]{1,0:T(8,128)(2,1)S(1)}, bf16[24,2048]{1,0:T(8,128)(2,1)S(1)}, u32[]{:S(2)}, u32[]{:S(2)}) %collective-permute-start.10) | collective-permute-done | bytes 98336 | tf_op jit(solution)/shard_map/ppermute | solution.py:54
  (79 shorter events, 5.9 us)
Async XLA Ops:
  0.6 163.0 %copy-start = (bf16[24,2048]{1,0:T(8,128)(2,1)S(1)}, bf16[24,2048]{1,0:T(8,128)(2,1)}, u32[]{:S(2)}) copy-start(bf16[24,2048]{1,0:T(8,128)(2,1)} %param.17) | copy-start | bytes 294916
  2.5 15.3 %collective-permute-start.1 = (bf16[24,4224]{1,0:T(8,128)(2,1)S(1)}, bf16[24,4224]{1,0:T(8,128)(2,1)S(1)}, u32[]{:S(2)}, u32[]{:S(2)}) collective-permute-start(bf16[24,4224]{1,0:T(8,128)(2,1)S(1)} %fusion.15), channel_id=1, source_target_pairs={{0,256},{64,320},{128,384},{192,448},{256,0},{320,64},{384,128},{4... | collective-permute-start | bytes 608264 | tf_op jit(solution)/shard_map/ppermute | solution.py:54
  18.4 0.9 copy-start.8
  20.6 1.3 copy-start.1
  21.9 20.1 %copy-start.2 = (bf16[1,1024,512]{2,1,0:T(8,128)(2,1)S(1)}, bf16[1,1024,512]{2,1,0:T(8,128)(2,1)}, u32[]{:S(2)}) copy-start(bf16[1,1024,512]{2,1,0:T(8,128)(2,1)} %param.15) | copy-start | bytes 3145732
  21.9 96.5 %all-to-all-start = ((bf16[64,4,4096]{2,1,0:T(4,128)(2,1)}), bf16[64,4,4096]{2,1,0:T(4,128)(2,1)S(1)}, u32[]{:S(2)}, u32[]{:S(2)}) async-start(bf16[64,4,4096]{2,1,0:T(4,128)(2,1)} %copy-done.1), calls=%async_computation | async-start | bytes 4194304 | tf_op jit(solution)/shard_map/all_to_all | solution.py:188
  36.9 70.8 %collective-permute-start.4 = (bf16[4096,128]{1,0:T(8,128)(2,1)}, bf16[4096,128]{1,0:T(8,128)(2,1)S(1)}, u32[]{:S(2)}, u32[]{:S(2)}) collective-permute-start(bf16[4096,128]{1,0:T(8,128)(2,1)} %bitcast.69), channel_id=1, source_target_pairs={{0,128},{64,192},{128,0},{192,64},{256,384},{320,448},{384,256},{4... | collective-permute-start | bytes 3145736 | tf_op jit(solution)/shard_map/ppermute | solution.py:54
  42.1 72.8 %collective-permute-start.8 = (bf16[1024,512]{1,0:T(8,128)(2,1)S(1)}, bf16[1024,512]{1,0:T(8,128)(2,1)}, u32[]{:S(2)}, u32[]{:S(2)}) collective-permute-start(bf16[1024,512]{1,0:T(8,128)(2,1)S(1)} %bitcast.65), channel_id=1, source_target_pairs={{0,384},{64,448},{128,256},{192,320},{256,128},{320,192},{384,0},{... | collective-permute-start | bytes 3145736 | tf_op jit(solution)/shard_map/ppermute | solution.py:54
  107.7 9.7 %collective-permute-start.5 = (bf16[4096,128]{1,0:T(8,128)(2,1)S(1)}, bf16[4096,128]{1,0:T(8,128)(2,1)S(1)}, u32[]{:S(2)}, u32[]{:S(2)}) collective-permute-start(bf16[4096,128]{1,0:T(8,128)(2,1)S(1)} %collective-permute-done.4.left_ref), channel_id=1, source_target_pairs={{0,64},{64,0},{128,192},{192,128},{256,320},{320,256},{384,448},{4... | collective-permute-start | bytes 3145736 | tf_op jit(solution)/shard_map/ppermute | solution.py:54
  109.6 1.0 copy-start.4
  110.6 16.8 %collective-permute-start.2 = (bf16[4096,128]{1,0:T(8,128)(2,1)}, bf16[4096,128]{1,0:T(8,128)(2,1)}, u32[]{:S(2)}, u32[]{:S(2)}) collective-permute-start(bf16[4096,128]{1,0:T(8,128)(2,1)} %bitcast.70), channel_id=1, source_target_pairs={{0,64},{64,0},{128,192},{192,128},{256,320},{320,256},{384,448},{4... | collective-permute-start | bytes 3145736 | tf_op jit(solution)/shard_map/ppermute | solution.py:54
  113.0 20.4 %collective-permute-start.7 = (bf16[1024,512]{1,0:T(8,128)(2,1)S(1)}, bf16[1024,512]{1,0:T(8,128)(2,1)}, u32[]{:S(2)}, u32[]{:S(2)}) collective-permute-start(bf16[1024,512]{1,0:T(8,128)(2,1)S(1)} %bitcast.66), channel_id=1, source_target_pairs={{0,64},{64,0},{128,192},{192,128},{256,320},{320,256},{384,448},{4... | collective-permute-start | bytes 3145736 | tf_op jit(solution)/shard_map/ppermute | solution.py:54
  114.9 18.5 %collective-permute-start.9 = (bf16[1024,512]{1,0:T(8,128)(2,1)}, bf16[1024,512]{1,0:T(8,128)(2,1)}, u32[]{:S(2)}, u32[]{:S(2)}) collective-permute-start(bf16[1024,512]{1,0:T(8,128)(2,1)} %collective-permute-done.8.refs_2_), channel_id=1, source_target_pairs={{0,64},{64,0},{128,192},{192,128},{256,320},{320,256},{384,448},{4... | collective-permute-start | bytes 3145736 | tf_op jit(solution)/shard_map/ppermute | solution.py:54
  117.3 1.0 copy-start.6
  118.4 1.2 copy-start.5
  119.6 1.2 copy-start.7
  120.8 6.6 %copy-start.3 = (bf16[1,4096,128]{2,1,0:T(8,128)(2,1)S(1)}, bf16[1,4096,128]{2,1,0:T(8,128)(2,1)}, u32[]{:S(2)}) copy-start(bf16[1,4096,128]{2,1,0:T(8,128)(2,1)} %param.14) | copy-start | bytes 3145732
  121.6 14.4 %collective-permute-start.6 = (bf16[256,256]{1,0:T(8,128)(2,1)S(1)}, bf16[256,256]{1,0:T(8,128)(2,1)S(1)}, u32[]{:S(2)}, u32[]{:S(2)}) collective-permute-start(bf16[256,256]{1,0:T(8,128)(2,1)S(1)} %shard_map.124.odd_ref), channel_id=1, source_target_pairs={{0,256},{64,320},{128,384},{192,448},{256,0},{320,64},{384,128},{4... | collective-permute-start | bytes 393224 | tf_op jit(solution)/shard_map/ppermute | solution.py:54
  129.5 13.7 %collective-permute-start.3 = (bf16[256,256]{1,0:T(8,128)(2,1)S(1)}, bf16[256,256]{1,0:T(8,128)(2,1)S(1)}, u32[]{:S(2)}, u32[]{:S(2)}) collective-permute-start(bf16[256,256]{1,0:T(8,128)(2,1)S(1)} %shard_map.123.even_ref), channel_id=1, source_target_pairs={{0,256},{64,320},{128,384},{192,448},{256,0},{320,64},{384,128},{4... | collective-permute-start | bytes 393224 | tf_op jit(solution)/shard_map/ppermute | solution.py:54
  146.7 11.8 %copy-start.13 = (s32[24,2]{0,1:T(2,128)S(1)}, s32[24,2]{0,1:T(2,128)}, u32[]{:S(2)}) copy-start(s32[24,2]{0,1:T(2,128)} %param.12) | copy-start | bytes 580
  146.7 11.8 %copy-start.12 = (f32[24,64]{1,0:T(8,128)S(1)}, f32[24,64]{1,0:T(8,128)}, u32[]{:S(2)}) copy-start(f32[24,64]{1,0:T(8,128)} %param.13) | copy-start | bytes 18436
  146.7 16.1 %copy-start.9 = (bf16[1,72,2048]{2,1,0:T(8,128)(2,1)S(1)}, bf16[1,72,2048]{2,1,0:T(8,128)(2,1)}, u32[]{:S(2)}) copy-start(bf16[1,72,2048]{2,1,0:T(8,128)(2,1)} %param.19) | copy-start | bytes 884740
  146.7 17.0 %copy-start.11 = (bf16[24,2048]{1,0:T(8,128)(2,1)S(1)}, bf16[24,2048]{1,0:T(8,128)(2,1)}, u32[]{:S(2)}) copy-start(bf16[24,2048]{1,0:T(8,128)(2,1)} %param.18) | copy-start | bytes 294916
  146.7 17.0 %copy-start.15 = (bf16[24,2048]{1,0:T(8,128)(2,1)S(1)}, bf16[24,2048]{1,0:T(8,128)(2,1)}, u32[]{:S(2)}) copy-start(bf16[24,2048]{1,0:T(8,128)(2,1)} %param.16) | copy-start | bytes 294916
  146.7 17.5 %copy-start.10 = (bf16[1,72,2048]{2,1,0:T(8,128)(2,1)S(1)}, bf16[1,72,2048]{2,1,0:T(8,128)(2,1)}, u32[]{:S(2)}) copy-start(bf16[1,72,2048]{2,1,0:T(8,128)(2,1)} %param.20) | copy-start | bytes 884740
  146.8 39.7 %all-to-all-start.1 = ((bf16[64,4,2048]{2,1,0:T(4,128)(2,1)}), bf16[64,4,2048]{2,1,0:T(4,128)(2,1)S(1)}, u32[]{:S(2)}, u32[]{:S(2)}) async-start(bf16[64,4,2048]{2,1,0:T(4,128)(2,1)} %shard_map.126), calls=%async_computation.1 | async-start | bytes 2097152 | tf_op jit(solution)/shard_map/all_to_all | solution.py:225
  158.8 12.7 %collective-permute-start = (f32[24,2]{0,1:T(2,128)S(1)}, f32[24,2]{0,1:T(2,128)S(1)}, u32[]{:S(2)}, u32[]{:S(2)}) collective-permute-start(f32[24,2]{0,1:T(2,128)S(1)} %broadcast_divide_fusion), channel_id=1, source_target_pairs={{0,256},{64,320},{128,384},{192,448},{256,0},{320,64},{384,128},{4... | collective-permute-start | bytes 584 | tf_op jit(solution)/shard_map/ppermute | solution.py:54
  187.5 11.4 %collective-permute-start.10 = (bf16[24,2048]{1,0:T(8,128)(2,1)S(1)}, bf16[24,2048]{1,0:T(8,128)(2,1)S(1)}, u32[]{:S(2)}, u32[]{:S(2)}) collective-permute-start(bf16[24,2048]{1,0:T(8,128)(2,1)S(1)} %slice.40), channel_id=1, source_target_pairs={{0,256},{64,320},{128,384},{192,448},{256,0},{320,64},{384,128},{4... | collective-permute-start | bytes 294920 | tf_op jit(solution)/shard_map/ppermute | solution.py:54
  199.1 0.7 copy-start.14

commit v5 on v4

--- a/solution.py
+++ b/solution.py
@@ -109,32 +109,29 @@
     act_ref[:, half:] = jnp.where(odd, left, right)
 
 
-def second_dot(place_ref, even_ref, odd_ref, part_ref, first_block):
-    ring = place_ref[0] // 2
-    base = ((ring ^ first_block) // 2) * (2 * ACT_BLOCK)
-    base = pl.multiple_of(base, 2 * ACT_BLOCK)
-    turned = ring % 2 == 1
-    even, odd = even_ref[...], odd_ref[...]
-    act = jnp.concatenate([jnp.where(turned, odd, even), jnp.where(turned, even, odd)], axis=1)
+def ring_dot(place_ref, act_ref, part_ref, flip):
+    base = pl.multiple_of(((place_ref[0] // 2) ^ flip) * ACT_BLOCK, ACT_BLOCK)
     return jnp.dot(
-        act, part_ref[pl.ds(base, 2 * ACT_BLOCK), :], preferred_element_type=jnp.float32
-    )
-
-
-def near_kernel(place_ref, even_ref, odd_ref, *refs):
+        act_ref[...], part_ref[pl.ds(base, ACT_BLOCK), :], preferred_element_type=jnp.float32
+    )
+
+
+def near_kernel(place_ref, own_ref, mate_ref, far_ref, *refs):
     part_refs, sums_ref = refs[:4], refs[4]
     wide = part_refs[0].shape[1]
     for index, part_ref in enumerate(part_refs):
-        lanes = slice(index * wide, (index + 1) * wide)
-        sums_ref[:, lanes] = second_dot(place_ref, even_ref, odd_ref, part_ref, 0)
-
-
-def far_kernel(place_ref, even_ref, odd_ref, *refs):
+        total = ring_dot(place_ref, own_ref, part_ref, 0)
+        total += ring_dot(place_ref, mate_ref, part_ref, 1)
+        total += ring_dot(place_ref, far_ref, part_ref, 2)
+        sums_ref[:, index * wide : (index + 1) * wide] = total
+
+
+def far_kernel(place_ref, far_ref, *refs):
     part_refs, before_ref, out_ref = refs[:4], refs[4], refs[5]
     wide = part_refs[0].shape[1]
     for index, part_ref in enumerate(part_refs):
         lanes = slice(index * wide, (index + 1) * wide)
-        total = before_ref[:, lanes] + second_dot(place_ref, even_ref, odd_ref, part_ref, 2)
+        total = before_ref[:, lanes] + ring_dot(place_ref, far_ref, part_ref, 3)
         out_ref[..., lanes] = total.astype(jnp.bfloat16).reshape(out_ref.shape[:-1] + (wide,))
 
 
@@ -211,13 +208,15 @@
     both_gates = jnp.concatenate([gates, swap(gates, ROW_FLIP)], axis=0)
 
     width = 4 * second_parts[0].shape[1]
-    sums = in_vmem(near_kernel, (experts * 4, width), jnp.float32, place_list, *near, *second_parts)
+    sums = in_vmem(
+        near_kernel, (experts * 4, width), jnp.float32, place_list, *near, far[0], *second_parts
+    )
     outputs = in_vmem(
         far_kernel,
         (experts, 4) + (width,),
         jnp.bfloat16,
         place_list,
-        *far,
+        far[1],
         *second_parts,
         sums,
         to_hbm=True,

time: 201 us -> 198 us (0.985)
    unnamed x35 -> x31, local copies, waits for them, and re-layouts: 8.27 us -> 7.3 us
  transfers between devices with their start and end apart: 13 -> 13, of which waited for: 6 -> 7; matrix products, arithmetic and copies ran while one was open for 2% -> 2% of each run, Pallas kernels for 3% -> 3%
where the time goes in v5:
time: 198 us; the launch traced here: 197 us
  waiting for transfers between devices  101 us (51%)
  starting transfers between devices  70.3 us (36%)
  Pallas kernels  10.4 us (5%)
  local copies, waits for them, and re-layouts  9.16 us (5%)
  other arithmetic  2.7 us (1%)
    ppermute x11, waiting for transfers between devices, swap(): lax.ppermute(block, 'dp', [(place, place ^ flip) for place in range(8)])  86.1 us
    ppermute x11, starting transfers between devices, swap(): lax.ppermute(block, 'dp', [(place, place ^ flip) for place in range(8)])  43.6 us
    all_to_all x1, starting transfers between devices, shards(): lax.all_to_all(dispatch, 'ep', split_axis=0, concat_axis=0, tiled=True)  14.9 us
    all_to_all x1, waiting for transfers between devices, shards(): lax.all_to_all(outputs, 'ep', split_axis=0, concat_axis=0, tiled=True)  14.9 us
    all_to_all x1, starting transfers between devices, shards(): lax.all_to_all(outputs, 'ep', split_axis=0, concat_axis=0, tiled=True)  11.8 us
    pallas_call x5, Pallas kernels, in_vmem(): pl.pallas_call(kernel, in_specs=specs, out_specs=pl.BlockSpec(memory_spac...  10.4 us
    unnamed x31, local copies, waits for them, and re-layouts  7.3 us
  transfers between devices with their start and end apart: 13, of which 7 were waited for; matrix products, arithmetic and copies ran while one was open for 2% of the time, Pallas kernels for 3%

profile of v5, /device:TPU:10, one launch (start us, length us, event | category | flops | bytes accessed | tf_op | source)
XLA Modules:
  0.0 196.8 jit_solution(8120637225678364516)
XLA Ops:
  0.7 0.8 multiply_add_fusion
  1.5 0.9 fusion.15
  2.5 6.8 %collective-permute-start.1 = (bf16[24,4224]{1,0:T(8,128)(2,1)S(1)}, bf16[24,4224]{1,0:T(8,128)(2,1)S(1)}, u32[]{:S(2)}, u32[]{:S(2)}) collective-permute-start(bf16[24,4224]{1,0:T(8,128)(2,1)S(1)} %fusion.15), channel_id=1, source_target_pairs={{0,256},{64,320},{128,384},{192,448},{256,0},{320,64},{384,128},{4... | collective-permute-start | bytes 608264 | tf_op jit(solution)/shard_map/ppermute | solution.py:54
  9.3 0.8 copy.57
  10.6 7.1 %collective-permute-done.1.refs_1_ = bf16[24,4224]{1,0:T(8,128)(2,1)S(1)} collective-permute-done((bf16[24,4224]{1,0:T(8,128)(2,1)S(1)}, bf16[24,4224]{1,0:T(8,128)(2,1)S(1)}, u32[]{:S(2)}, u32[]{:S(2)}) %collective-permute-start.1) | collective-permute-done | bytes 202784 | tf_op jit(solution)/shard_map/ppermute | solution.py:54
  18.4 0.9 copy-done.6
  19.3 1.3 shard_map.122
  20.6 1.3 copy-done.1
  21.9 14.9 %all-to-all-start = ((bf16[64,4,4096]{2,1,0:T(4,128)(2,1)}), bf16[64,4,4096]{2,1,0:T(4,128)(2,1)S(1)}, u32[]{:S(2)}, u32[]{:S(2)}) async-start(bf16[64,4,4096]{2,1,0:T(4,128)(2,1)} %copy-done.1), calls=%async_computation | async-start | bytes 4194304 | tf_op jit(solution)/shard_map/all_to_all | solution.py:185
  36.9 5.2 %collective-permute-start.2 = (bf16[4096,128]{1,0:T(8,128)(2,1)}, bf16[4096,128]{1,0:T(8,128)(2,1)}, u32[]{:S(2)}, u32[]{:S(2)}) collective-permute-start(bf16[4096,128]{1,0:T(8,128)(2,1)} %bitcast.69), channel_id=1, source_target_pairs={{0,128},{64,192},{128,0},{192,64},{256,384},{320,448},{384,256},{4... | collective-permute-start | bytes 3145736 | tf_op jit(solution)/shard_map/ppermute | solution.py:54
  42.1 5.6 %collective-permute-start.6 = (bf16[1024,512]{1,0:T(8,128)(2,1)S(1)}, bf16[1024,512]{1,0:T(8,128)(2,1)}, u32[]{:S(2)}, u32[]{:S(2)}) collective-permute-start(bf16[1024,512]{1,0:T(8,128)(2,1)S(1)} %bitcast.65), channel_id=1, source_target_pairs={{0,384},{64,448},{128,256},{192,320},{256,128},{320,192},{384,0},{... | collective-permute-start | bytes 3145736 | tf_op jit(solution)/shard_map/ppermute | solution.py:54
  47.7 1.9 collective-permute-start.8
  49.6 58.1 %collective-permute-done.2.left_ref = bf16[4096,128]{1,0:T(8,128)(2,1)} collective-permute-done((bf16[4096,128]{1,0:T(8,128)(2,1)}, bf16[4096,128]{1,0:T(8,128)(2,1)}, u32[]{:S(2)}, u32[]{:S(2)}) %collective-permute-start.2) | collective-permute-done | bytes 1048608 | tf_op jit(solution)/shard_map/ppermute | solution.py:54
  107.8 1.9 collective-permute-start.3
  109.7 2.4 %collective-permute-start.5 = (bf16[1024,512]{1,0:T(8,128)(2,1)S(1)}, bf16[1024,512]{1,0:T(8,128)(2,1)}, u32[]{:S(2)}, u32[]{:S(2)}) collective-permute-start(bf16[1024,512]{1,0:T(8,128)(2,1)S(1)} %bitcast.66), channel_id=1, source_target_pairs={{0,64},{64,0},{128,192},{192,128},{256,320},{320,256},{384,448},{4... | collective-permute-start | bytes 3145736 | tf_op jit(solution)/shard_map/ppermute | solution.py:54
  112.1 1.9 collective-permute-start.7
  114.1 1.0 copy-done.4
  115.1 1.2 copy-done.3
  116.3 1.2 copy-done.5
  118.3 5.8 %collective-permute-start.9 = (bf16[256,256]{1,0:T(8,128)(2,1)S(1)}, bf16[256,256]{1,0:T(8,128)(2,1)S(1)}, u32[]{:S(2)}, u32[]{:S(2)}) collective-permute-start(bf16[256,256]{1,0:T(8,128)(2,1)S(1)} %shard_map.124.own_ref), channel_id=1, source_target_pairs={{0,256},{64,320},{128,384},{192,448},{256,0},{320,64},{384,128},{4... | collective-permute-start | bytes 393224 | tf_op jit(solution)/shard_map/ppermute | solution.py:54
  124.1 2.3 %shard_map.123.mate_ref = bf16[256,256]{1,0:T(8,128)(2,1)S(1)} custom-call(s32[1]{0:T(128)} %bitcast.6.place_ref, bf16[64,4,4096]{2,1,0:T(4,128)(2,1)S(1)} %all-to-all-done.rows_ref, bf16[4096,128]{1,0:T(8,128)(2,1)} %collective-permute-done.2.left_ref, bf16[4096,128]{1,0:T(8,128)(2,1)} %collective-permute-done.3.right_ref), custom_call_target="tpu_custom_call" | custom-call | tf_op jit(solution)/shard_map/pallas_call | solution.py:70
  126.4 3.9 %collective-permute-start.4 = (bf16[256,256]{1,0:T(8,128)(2,1)S(1)}, bf16[256,256]{1,0:T(8,128)(2,1)S(1)}, u32[]{:S(2)}, u32[]{:S(2)}) collective-permute-start(bf16[256,256]{1,0:T(8,128)(2,1)S(1)} %shard_map.123.mate_ref), channel_id=1, source_target_pairs={{0,256},{64,320},{128,384},{192,448},{256,0},{320,64},{384,128},{4... | collective-permute-start | bytes 393224 | tf_op jit(solution)/shard_map/ppermute | solution.py:54
  130.4 1.5 collective-permute-done.9.far_ref
  131.9 2.8 %shard_map.125.refs_4_ = f32[256,2048]{1,0:T(8,128)S(1)} custom-call(s32[1]{0:T(128)} %bitcast.6.place_ref, bf16[256,256]{1,0:T(8,128)(2,1)S(1)} %shard_map.124.own_ref, bf16[256,256]{1,0:T(8,128)(2,1)S(1)} %shard_map.123.mate_ref, bf16[256,256]{1,0:T(8,128)(2,1)S(1)} %collective-permute-done.9.far_ref, bf16[1024,512]{1,0:T(8,128)(2,1)S(1)} %bitcast.67, ...), custom_call_target="tpu_custom_call" | custom-call | tf_op jit(solution)/shard_map/pallas_call | solution.py:70
  134.7 5.8 %collective-permute-done.4.far_ref = bf16[256,256]{1,0:T(8,128)(2,1)S(1)} collective-permute-done((bf16[256,256]{1,0:T(8,128)(2,1)S(1)}, bf16[256,256]{1,0:T(8,128)(2,1)S(1)}, u32[]{:S(2)}, u32[]{:S(2)}) %collective-permute-start.4) | collective-permute-done | bytes 131104 | tf_op jit(solution)/shard_map/ppermute | solution.py:54
  140.6 3.3 %shard_map.126 = bf16[64,4,2048]{2,1,0:T(4,128)(2,1)} custom-call(s32[1]{0:T(128)} %bitcast.6.place_ref, bf16[256,256]{1,0:T(8,128)(2,1)S(1)} %collective-permute-done.4.far_ref, bf16[1024,512]{1,0:T(8,128)(2,1)S(1)} %bitcast.68, bf16[1024,512]{1,0:T(8,128)(2,1)} %collective-permute-done.5.refs_1_, bf16[1024,512]{1,0:T(8,128)(2,1)} %collective-permute-done.6.refs_2_, ...), custom_call_target="tpu_custom_call" | custom-call | tf_op jit(solution)/shard_map/pallas_call | solution.py:70
  143.9 11.8 %all-to-all-start.1 = ((bf16[64,4,2048]{2,1,0:T(4,128)(2,1)}), bf16[64,4,2048]{2,1,0:T(4,128)(2,1)S(1)}, u32[]{:S(2)}, u32[]{:S(2)}) async-start(bf16[64,4,2048]{2,1,0:T(4,128)(2,1)} %shard_map.126), calls=%async_computation.1 | async-start | bytes 2097152 | tf_op jit(solution)/shard_map/all_to_all | solution.py:224
  155.9 4.0 %collective-permute-start = (f32[24,2]{0,1:T(2,128)S(1)}, f32[24,2]{0,1:T(2,128)S(1)}, u32[]{:S(2)}, u32[]{:S(2)}) collective-permute-start(f32[24,2]{0,1:T(2,128)S(1)} %broadcast_divide_fusion), channel_id=1, source_target_pairs={{0,256},{64,320},{128,384},{192,448},{256,0},{320,64},{384,128},{4... | collective-permute-start | bytes 584 | tf_op jit(solution)/shard_map/ppermute | solution.py:54
  161.5 7.5 %collective-permute-done = f32[24,2]{0,1:T(2,128)S(1)} collective-permute-done((f32[24,2]{0,1:T(2,128)S(1)}, f32[24,2]{0,1:T(2,128)S(1)}, u32[]{:S(2)}, u32[]{:S(2)}) %collective-permute-start) | collective-permute-done | bytes 224 | tf_op jit(solution)/shard_map/ppermute | solution.py:54
  169.1 14.9 %all-to-all-done.1 = bf16[64,4,2048]{2,1,0:T(4,128)(2,1)S(1)} async-done(((bf16[64,4,2048]{2,1,0:T(4,128)(2,1)}), bf16[64,4,2048]{2,1,0:T(4,128)(2,1)S(1)}, u32[]{:S(2)}, u32[]{:S(2)}) %all-to-all-start.1) | async-done | bytes 1048608 | tf_op jit(solution)/shard_map/all_to_all | solution.py:224
  184.9 4.0 %collective-permute-start.10 = (bf16[24,2048]{1,0:T(8,128)(2,1)S(1)}, bf16[24,2048]{1,0:T(8,128)(2,1)S(1)}, u32[]{:S(2)}, u32[]{:S(2)}) collective-permute-start(bf16[24,2048]{1,0:T(8,128)(2,1)S(1)} %slice.40), channel_id=1, source_target_pairs={{0,256},{64,320},{128,384},{192,448},{256,0},{320,64},{384,128},{4... | collective-permute-start | bytes 294920 | tf_op jit(solution)/shard_map/ppermute | solution.py:54
  189.9 6.0 %collective-permute-done.10 = bf16[24,2048]{1,0:T(8,128)(2,1)S(1)} collective-permute-done((bf16[24,2048]{1,0:T(8,128)(2,1)S(1)}, bf16[24,2048]{1,0:T(8,128)(2,1)S(1)}, u32[]{:S(2)}, u32[]{:S(2)}) %collective-permute-start.10) | collective-permute-done | bytes 98336 | tf_op jit(solution)/shard_map/ppermute | solution.py:54
  (75 shorter events, 5.9 us)
Async XLA Ops:
  0.6 160.2 %copy-start = (bf16[24,2048]{1,0:T(8,128)(2,1)S(1)}, bf16[24,2048]{1,0:T(8,128)(2,1)}, u32[]{:S(2)}) copy-start(bf16[24,2048]{1,0:T(8,128)(2,1)} %param.17) | copy-start | bytes 294916
  2.5 15.3 %collective-permute-start.1 = (bf16[24,4224]{1,0:T(8,128)(2,1)S(1)}, bf16[24,4224]{1,0:T(8,128)(2,1)S(1)}, u32[]{:S(2)}, u32[]{:S(2)}) collective-permute-start(bf16[24,4224]{1,0:T(8,128)(2,1)S(1)} %fusion.15), channel_id=1, source_target_pairs={{0,256},{64,320},{128,384},{192,448},{256,0},{320,64},{384,128},{4... | collective-permute-start | bytes 608264 | tf_op jit(solution)/shard_map/ppermute | solution.py:54
  18.4 0.9 copy-start.6
  20.6 1.3 copy-start.1
  21.9 20.1 %copy-start.2 = (bf16[1,1024,512]{2,1,0:T(8,128)(2,1)S(1)}, bf16[1,1024,512]{2,1,0:T(8,128)(2,1)}, u32[]{:S(2)}) copy-start(bf16[1,1024,512]{2,1,0:T(8,128)(2,1)} %param.15) | copy-start | bytes 3145732
  21.9 93.2 %all-to-all-start = ((bf16[64,4,4096]{2,1,0:T(4,128)(2,1)}), bf16[64,4,4096]{2,1,0:T(4,128)(2,1)S(1)}, u32[]{:S(2)}, u32[]{:S(2)}) async-start(bf16[64,4,4096]{2,1,0:T(4,128)(2,1)} %copy-done.1), calls=%async_computation | async-start | bytes 4194304 | tf_op jit(solution)/shard_map/all_to_all | solution.py:185
  36.9 70.9 %collective-permute-start.2 = (bf16[4096,128]{1,0:T(8,128)(2,1)}, bf16[4096,128]{1,0:T(8,128)(2,1)}, u32[]{:S(2)}, u32[]{:S(2)}) collective-permute-start(bf16[4096,128]{1,0:T(8,128)(2,1)} %bitcast.69), channel_id=1, source_target_pairs={{0,128},{64,192},{128,0},{192,64},{256,384},{320,448},{384,256},{4... | collective-permute-start | bytes 3145736 | tf_op jit(solution)/shard_map/ppermute | solution.py:54
  42.1 70.0 %collective-permute-start.6 = (bf16[1024,512]{1,0:T(8,128)(2,1)S(1)}, bf16[1024,512]{1,0:T(8,128)(2,1)}, u32[]{:S(2)}, u32[]{:S(2)}) collective-permute-start(bf16[1024,512]{1,0:T(8,128)(2,1)S(1)} %bitcast.65), channel_id=1, source_target_pairs={{0,384},{64,448},{128,256},{192,320},{256,128},{320,192},{384,0},{... | collective-permute-start | bytes 3145736 | tf_op jit(solution)/shard_map/ppermute | solution.py:54
  47.7 66.3 %collective-permute-start.8 = (bf16[4096,128]{1,0:T(8,128)(2,1)}, bf16[4096,128]{1,0:T(8,128)(2,1)S(1)}, u32[]{:S(2)}, u32[]{:S(2)}) collective-permute-start(bf16[4096,128]{1,0:T(8,128)(2,1)} %bitcast.70), channel_id=1, source_target_pairs={{0,64},{64,0},{128,192},{192,128},{256,320},{320,256},{384,448},{4... | collective-permute-start | bytes 3145736 | tf_op jit(solution)/shard_map/ppermute | solution.py:54
  107.8 16.4 %collective-permute-start.3 = (bf16[4096,128]{1,0:T(8,128)(2,1)}, bf16[4096,128]{1,0:T(8,128)(2,1)}, u32[]{:S(2)}, u32[]{:S(2)}) collective-permute-start(bf16[4096,128]{1,0:T(8,128)(2,1)} %collective-permute-done.2.left_ref), channel_id=1, source_target_pairs={{0,64},{64,0},{128,192},{192,128},{256,320},{320,256},{384,448},{4... | collective-permute-start | bytes 3145736 | tf_op jit(solution)/shard_map/ppermute | solution.py:54
  109.7 20.7 %collective-permute-start.5 = (bf16[1024,512]{1,0:T(8,128)(2,1)S(1)}, bf16[1024,512]{1,0:T(8,128)(2,1)}, u32[]{:S(2)}, u32[]{:S(2)}) collective-permute-start(bf16[1024,512]{1,0:T(8,128)(2,1)S(1)} %bitcast.66), channel_id=1, source_target_pairs={{0,64},{64,0},{128,192},{192,128},{256,320},{320,256},{384,448},{4... | collective-permute-start | bytes 3145736 | tf_op jit(solution)/shard_map/ppermute | solution.py:54
  112.1 18.3 %collective-permute-start.7 = (bf16[1024,512]{1,0:T(8,128)(2,1)}, bf16[1024,512]{1,0:T(8,128)(2,1)}, u32[]{:S(2)}, u32[]{:S(2)}) collective-permute-start(bf16[1024,512]{1,0:T(8,128)(2,1)} %collective-permute-done.6.refs_2_), channel_id=1, source_target_pairs={{0,64},{64,0},{128,192},{192,128},{256,320},{320,256},{384,448},{4... | collective-permute-start | bytes 3145736 | tf_op jit(solution)/shard_map/ppermute | solution.py:54
  114.1 1.0 copy-start.4
  115.1 1.2 copy-start.3
  116.3 1.2 copy-start.5
  118.3 13.6 %collective-permute-start.9 = (bf16[256,256]{1,0:T(8,128)(2,1)S(1)}, bf16[256,256]{1,0:T(8,128)(2,1)S(1)}, u32[]{:S(2)}, u32[]{:S(2)}) collective-permute-start(bf16[256,256]{1,0:T(8,128)(2,1)S(1)} %shard_map.124.own_ref), channel_id=1, source_target_pairs={{0,256},{64,320},{128,384},{192,448},{256,0},{320,64},{384,128},{4... | collective-permute-start | bytes 393224 | tf_op jit(solution)/shard_map/ppermute | solution.py:54
  126.4 14.1 %collective-permute-start.4 = (bf16[256,256]{1,0:T(8,128)(2,1)S(1)}, bf16[256,256]{1,0:T(8,128)(2,1)S(1)}, u32[]{:S(2)}, u32[]{:S(2)}) collective-permute-start(bf16[256,256]{1,0:T(8,128)(2,1)S(1)} %shard_map.123.mate_ref), channel_id=1, source_target_pairs={{0,256},{64,320},{128,384},{192,448},{256,0},{320,64},{384,128},{4... | collective-permute-start | bytes 393224 | tf_op jit(solution)/shard_map/ppermute | solution.py:54
  143.9 11.8 %copy-start.11 = (s32[24,2]{0,1:T(2,128)S(1)}, s32[24,2]{0,1:T(2,128)}, u32[]{:S(2)}) copy-start(s32[24,2]{0,1:T(2,128)} %param.12) | copy-start | bytes 580
  143.9 11.8 %copy-start.10 = (f32[24,64]{1,0:T(8,128)S(1)}, f32[24,64]{1,0:T(8,128)}, u32[]{:S(2)}) copy-start(f32[24,64]{1,0:T(8,128)} %param.13) | copy-start | bytes 18436
  143.9 16.1 %copy-start.7 = (bf16[1,72,2048]{2,1,0:T(8,128)(2,1)S(1)}, bf16[1,72,2048]{2,1,0:T(8,128)(2,1)}, u32[]{:S(2)}) copy-start(bf16[1,72,2048]{2,1,0:T(8,128)(2,1)} %param.19) | copy-start | bytes 884740
  143.9 17.0 %copy-start.9 = (bf16[24,2048]{1,0:T(8,128)(2,1)S(1)}, bf16[24,2048]{1,0:T(8,128)(2,1)}, u32[]{:S(2)}) copy-start(bf16[24,2048]{1,0:T(8,128)(2,1)} %param.18) | copy-start | bytes 294916
  143.9 17.0 %copy-start.13 = (bf16[24,2048]{1,0:T(8,128)(2,1)S(1)}, bf16[24,2048]{1,0:T(8,128)(2,1)}, u32[]{:S(2)}) copy-start(bf16[24,2048]{1,0:T(8,128)(2,1)} %param.16) | copy-start | bytes 294916
  143.9 17.5 %copy-start.8 = (bf16[1,72,2048]{2,1,0:T(8,128)(2,1)S(1)}, bf16[1,72,2048]{2,1,0:T(8,128)(2,1)}, u32[]{:S(2)}) copy-start(bf16[1,72,2048]{2,1,0:T(8,128)(2,1)} %param.20) | copy-start | bytes 884740
  143.9 40.1 %all-to-all-start.1 = ((bf16[64,4,2048]{2,1,0:T(4,128)(2,1)}), bf16[64,4,2048]{2,1,0:T(4,128)(2,1)S(1)}, u32[]{:S(2)}, u32[]{:S(2)}) async-start(bf16[64,4,2048]{2,1,0:T(4,128)(2,1)} %shard_map.126), calls=%async_computation.1 | async-start | bytes 2097152 | tf_op jit(solution)/shard_map/all_to_all | solution.py:224
  155.9 13.1 %collective-permute-start = (f32[24,2]{0,1:T(2,128)S(1)}, f32[24,2]{0,1:T(2,128)S(1)}, u32[]{:S(2)}, u32[]{:S(2)}) collective-permute-start(f32[24,2]{0,1:T(2,128)S(1)} %broadcast_divide_fusion), channel_id=1, source_target_pairs={{0,256},{64,320},{128,384},{192,448},{256,0},{320,64},{384,128},{4... | collective-permute-start | bytes 584 | tf_op jit(solution)/shard_map/ppermute | solution.py:54
  184.9 10.9 %collective-permute-start.10 = (bf16[24,2048]{1,0:T(8,128)(2,1)S(1)}, bf16[24,2048]{1,0:T(8,128)(2,1)S(1)}, u32[]{:S(2)}, u32[]{:S(2)}) collective-permute-start(bf16[24,2048]{1,0:T(8,128)(2,1)S(1)} %slice.40), channel_id=1, source_target_pairs={{0,256},{64,320},{128,384},{192,448},{256,0},{320,64},{384,128},{4... | collective-permute-start | bytes 294920 | tf_op jit(solution)/shard_map/ppermute | solution.py:54
  196.1 0.7 copy-start.12

commit v6 on v4

--- a/solution.py
+++ b/solution.py
@@ -138,6 +138,20 @@
         out_ref[..., lanes] = total.astype(jnp.bfloat16).reshape(out_ref.shape[:-1] + (wide,))
 
 
+def combine_kernel(first_ref, second_ref, gates_ref, rows_ref, out_ref):
+    width, step = out_ref.shape[1], 512
+    for at in range(0, width, step):
+        lanes = slice(at, at + step)
+        rows = rows_ref[..., lanes].reshape(first_ref.shape[1], step)
+        mixed = gates_ref[:, :1] * jnp.dot(
+            first_ref[...], rows, preferred_element_type=jnp.float32
+        )
+        mixed += gates_ref[:, 1:] * jnp.dot(
+            second_ref[...], rows, preferred_element_type=jnp.float32
+        )
+        out_ref[:, lanes] = mixed.astype(jnp.bfloat16)
+
+
 def shards(
     hidden_in,
     expert_ids,
@@ -223,23 +237,29 @@
         to_hbm=True,
     )
     returned = lax.all_to_all(outputs, "ep", split_axis=0, concat_axis=0, tiled=True)
-    flat_back = returned.reshape(experts * 4, width)
 
     attended = attend(
         queries, span_keys, span_values, cache_keys[0], cache_values[0], valid_frames[0]
     )
 
-    running = jnp.zeros((2 * tokens, width), jnp.float32)
-    for column in range(2):
-        picked = jnp.dot(
-            picks[column].astype(jnp.bfloat16), flat_back, preferred_element_type=jnp.float32
-        )
-        running = running + both_gates[:, column : column + 1] * picked
-    halves = running.astype(jnp.bfloat16)
-    arrived = swap(halves[tokens:], ROW_FLIP)
+    halves = []
+    for at in (tokens, 0):
+        picked = [pick[at : at + tokens].astype(jnp.bfloat16) for pick in picks]
+        halves.append(
+            in_vmem(
+                combine_kernel,
+                (tokens, width),
+                jnp.bfloat16,
+                None,
+                *picked,
+                both_gates[at : at + tokens],
+                returned,
+            )
+        )
+    arrived = swap(halves[0], ROW_FLIP)
     flips = (0, CORE_FLIP, SECOND_FLIP, SECOND_FLIP ^ CORE_FLIP)
     blocks = [None] * 8
-    for half, flip in ((halves[:tokens], 0), (arrived, ROW_FLIP)):
+    for half, flip in ((halves[1], 0), (arrived, ROW_FLIP)):
         for index, block in enumerate(jnp.split(half, 4, axis=1)):
             blocks[flips[index] ^ flip] = block
     for bit in (1, 2, 4):

time: 201 us -> 200 us (level)
    pallas_call x5 -> x7, Pallas kernels: 10.2 us -> 11.2 us  [in_vmem(): pl.pallas_call(kernel, in_specs=specs, out_specs=pl.BlockSpec(memory_spac...]
where the time goes in v6:
time: 200 us; the launch traced here: 199 us
  waiting for transfers between devices  102 us (51%)
  starting transfers between devices  70.8 us (35%)
  Pallas kernels  11.2 us (6%)
  local copies, waits for them, and re-layouts  9.94 us (5%)
  other arithmetic  2.96 us (1%)
    ppermute x11, waiting for transfers between devices, swap(): lax.ppermute(block, 'dp', [(place, place ^ flip) for place in range(8)])  87.3 us
    ppermute x11, starting transfers between devices, swap(): lax.ppermute(block, 'dp', [(place, place ^ flip) for place in range(8)])  44.1 us
    all_to_all x1, starting transfers between devices, shards(): lax.all_to_all(dispatch, 'ep', split_axis=0, concat_axis=0, tiled=True)  14.9 us
    all_to_all x1, waiting for transfers between devices, shards(): lax.all_to_all(outputs, 'ep', split_axis=0, concat_axis=0, tiled=True)  14.5 us
    all_to_all x1, starting transfers between devices, shards(): lax.all_to_all(outputs, 'ep', split_axis=0, concat_axis=0, tiled=True)  11.8 us
    pallas_call x7, Pallas kernels, in_vmem(): pl.pallas_call(kernel, in_specs=specs, out_specs=pl.BlockSpec(memory_spac...  11.2 us
    unnamed x35, local copies, waits for them, and re-layouts  8.27 us
  transfers between devices with their start and end apart: 13, of which 6 were waited for; matrix products, arithmetic and copies ran while one was open for 2% of the time, Pallas kernels for 3%

profile of v6, /device:TPU:10, one launch (start us, length us, event | category | flops | bytes accessed | tf_op | source)
XLA Modules:
  0.0 199.3 jit_solution(10292499816793002930)
XLA Ops:
  0.7 0.8 multiply_add_fusion
  1.5 0.9 fusion.13
  2.5 6.8 %collective-permute-start = (bf16[24,4224]{1,0:T(8,128)(2,1)S(1)}, bf16[24,4224]{1,0:T(8,128)(2,1)S(1)}, u32[]{:S(2)}, u32[]{:S(2)}) collective-permute-start(bf16[24,4224]{1,0:T(8,128)(2,1)S(1)} %fusion.13), channel_id=1, source_target_pairs={{0,256},{64,320},{128,384},{192,448},{256,0},{320,64},{384,128},{4... | collective-permute-start | bytes 608264 | tf_op jit(solution)/shard_map/ppermute | solution.py:54
  9.3 0.8 copy.63
  10.6 7.1 %collective-permute-done.refs_1_ = bf16[24,4224]{1,0:T(8,128)(2,1)S(1)} collective-permute-done((bf16[24,4224]{1,0:T(8,128)(2,1)S(1)}, bf16[24,4224]{1,0:T(8,128)(2,1)S(1)}, u32[]{:S(2)}, u32[]{:S(2)}) %collective-permute-start) | collective-permute-done | bytes 202784 | tf_op jit(solution)/shard_map/ppermute | solution.py:54
  18.4 0.9 copy-done.8
  19.3 1.3 shard_map.122
  20.6 1.3 copy-done.1
  21.9 14.9 %all-to-all-start = ((bf16[64,4,4096]{2,1,0:T(4,128)(2,1)}), bf16[64,4,4096]{2,1,0:T(4,128)(2,1)S(1)}, u32[]{:S(2)}, u32[]{:S(2)}) async-start(bf16[64,4,4096]{2,1,0:T(4,128)(2,1)} %copy-done.1), calls=%async_computation | async-start | bytes 4194304 | tf_op jit(solution)/shard_map/all_to_all | solution.py:202
  36.9 5.2 %collective-permute-start.3 = (bf16[4096,128]{1,0:T(8,128)(2,1)}, bf16[4096,128]{1,0:T(8,128)(2,1)S(1)}, u32[]{:S(2)}, u32[]{:S(2)}) collective-permute-start(bf16[4096,128]{1,0:T(8,128)(2,1)} %bitcast.63), channel_id=1, source_target_pairs={{0,128},{64,192},{128,0},{192,64},{256,384},{320,448},{384,256},{4... | collective-permute-start | bytes 3145736 | tf_op jit(solution)/shard_map/ppermute | solution.py:54
  42.1 5.6 %collective-permute-start.7 = (bf16[1024,512]{1,0:T(8,128)(2,1)S(1)}, bf16[1024,512]{1,0:T(8,128)(2,1)}, u32[]{:S(2)}, u32[]{:S(2)}) collective-permute-start(bf16[1024,512]{1,0:T(8,128)(2,1)S(1)} %bitcast.59), channel_id=1, source_target_pairs={{0,384},{64,448},{128,256},{192,320},{256,128},{320,192},{384,0},{... | collective-permute-start | bytes 3145736 | tf_op jit(solution)/shard_map/ppermute | solution.py:54
  47.7 60.0 %collective-permute-done.3.left_ref = bf16[4096,128]{1,0:T(8,128)(2,1)S(1)} collective-permute-done((bf16[4096,128]{1,0:T(8,128)(2,1)}, bf16[4096,128]{1,0:T(8,128)(2,1)S(1)}, u32[]{:S(2)}, u32[]{:S(2)}) %collective-permute-start.3) | collective-permute-done | bytes 1048608 | tf_op jit(solution)/shard_map/ppermute | solution.py:54
  107.7 1.9 collective-permute-start.4
  109.6 1.0 copy-done.4
  110.6 2.4 %collective-permute-start.1 = (bf16[4096,128]{1,0:T(8,128)(2,1)}, bf16[4096,128]{1,0:T(8,128)(2,1)}, u32[]{:S(2)}, u32[]{:S(2)}) collective-permute-start(bf16[4096,128]{1,0:T(8,128)(2,1)} %bitcast.64), channel_id=1, source_target_pairs={{0,64},{64,0},{128,192},{192,128},{256,320},{320,256},{384,448},{4... | collective-permute-start | bytes 3145736 | tf_op jit(solution)/shard_map/ppermute | solution.py:54
  113.0 1.9 collective-permute-start.6
  114.9 2.4 %collective-permute-start.8 = (bf16[1024,512]{1,0:T(8,128)(2,1)}, bf16[1024,512]{1,0:T(8,128)(2,1)}, u32[]{:S(2)}, u32[]{:S(2)}) collective-permute-start(bf16[1024,512]{1,0:T(8,128)(2,1)} %collective-permute-done.7.refs_2_), channel_id=1, source_target_pairs={{0,64},{64,0},{128,192},{192,128},{256,320},{320,256},{384,448},{4... | collective-permute-start | bytes 3145736 | tf_op jit(solution)/shard_map/ppermute | solution.py:54
  117.3 1.0 copy-done.6
  118.4 1.2 copy-done.5
  119.6 1.2 copy-done.7
  121.6 5.8 %collective-permute-start.5 = (bf16[256,256]{1,0:T(8,128)(2,1)S(1)}, bf16[256,256]{1,0:T(8,128)(2,1)S(1)}, u32[]{:S(2)}, u32[]{:S(2)}) collective-permute-start(bf16[256,256]{1,0:T(8,128)(2,1)S(1)} %shard_map.124.odd_ref), channel_id=1, source_target_pairs={{0,256},{64,320},{128,384},{192,448},{256,0},{320,64},{384,128},{4... | collective-permute-start | bytes 393224 | tf_op jit(solution)/shard_map/ppermute | solution.py:54
  127.4 2.0 %shard_map.123.even_ref = bf16[256,256]{1,0:T(8,128)(2,1)S(1)} custom-call(s32[1]{0:T(128)} %bitcast.6.place_ref, bf16[64,4,4096]{2,1,0:T(4,128)(2,1)S(1)} %all-to-all-done.rows_ref, bf16[4096,128]{1,0:T(8,128)(2,1)S(1)} %bitcast.65, bf16[4096,128]{1,0:T(8,128)(2,1)} %collective-permute-done.1.right_ref), custom_call_target="tpu_custom_call" | custom-call | tf_op jit(solution)/shard_map/pallas_call | solution.py:70
  129.5 3.9 %collective-permute-start.2 = (bf16[256,256]{1,0:T(8,128)(2,1)S(1)}, bf16[256,256]{1,0:T(8,128)(2,1)S(1)}, u32[]{:S(2)}, u32[]{:S(2)}) collective-permute-start(bf16[256,256]{1,0:T(8,128)(2,1)S(1)} %shard_map.123.even_ref), channel_id=1, source_target_pairs={{0,256},{64,320},{128,384},{192,448},{256,0},{320,64},{384,128},{4... | collective-permute-start | bytes 393224 | tf_op jit(solution)/shard_map/ppermute | solution.py:54
  133.4 2.6 %shard_map.125.refs_4_ = f32[256,2048]{1,0:T(8,128)S(1)} custom-call(s32[1]{0:T(128)} %bitcast.6.place_ref, bf16[256,256]{1,0:T(8,128)(2,1)S(1)} %shard_map.123.even_ref, bf16[256,256]{1,0:T(8,128)(2,1)S(1)} %shard_map.124.odd_ref, bf16[1024,512]{1,0:T(8,128)(2,1)S(1)} %bitcast.61, bf16[1024,512]{1,0:T(8,128)(2,1)} %collective-permute-done.6.refs_1_, ...), custom_call_target="tpu_custom_call" | custom-call | tf_op jit(solution)/shard_map/pallas_call | solution.py:70
  136.0 7.1 %collective-permute-done.2.even_ref = bf16[256,256]{1,0:T(8,128)(2,1)S(1)} collective-permute-done((bf16[256,256]{1,0:T(8,128)(2,1)S(1)}, bf16[256,256]{1,0:T(8,128)(2,1)S(1)}, u32[]{:S(2)}, u32[]{:S(2)}) %collective-permute-start.2) | collective-permute-done | bytes 131104 | tf_op jit(solution)/shard_map/ppermute | solution.py:54
  143.1 3.6 %shard_map.126 = bf16[64,4,2048]{2,1,0:T(4,128)(2,1)} custom-call(s32[1]{0:T(128)} %bitcast.6.place_ref, bf16[256,256]{1,0:T(8,128)(2,1)S(1)} %collective-permute-done.2.even_ref, bf16[256,256]{1,0:T(8,128)(2,1)S(1)} %collective-permute-done.5.odd_ref, bf16[1024,512]{1,0:T(8,128)(2,1)S(1)} %bitcast.62, bf16[1024,512]{1,0:T(8,128)(2,1)} %collective-permute-done.6.refs_1_, ...), custom_call_target="tpu_custom_call" | custom-call | tf_op jit(solution)/shard_map/pallas_call | solution.py:70
  146.8 11.8 %all-to-all-start.1 = ((bf16[64,4,2048]{2,1,0:T(4,128)(2,1)}), bf16[64,4,2048]{2,1,0:T(4,128)(2,1)S(1)}, u32[]{:S(2)}, u32[]{:S(2)}) async-start(bf16[64,4,2048]{2,1,0:T(4,128)(2,1)} %shard_map.126), calls=%async_computation.1 | async-start | bytes 2097152 | tf_op jit(solution)/shard_map/all_to_all | solution.py:239
  159.1 4.0 %collective-permute-start.9 = (f32[24,2]{1,0:T(8,128)S(1)}, f32[24,2]{1,0:T(8,128)S(1)}, u32[]{:S(2)}, u32[]{:S(2)}) collective-permute-start(f32[24,2]{1,0:T(8,128)S(1)} %fusion.25.gates_ref), channel_id=1, source_target_pairs={{0,256},{64,320},{128,384},{192,448},{256,0},{320,64},{384,128},{4... | collective-permute-start | bytes 584 | tf_op jit(solution)/shard_map/ppermute | solution.py:54
  164.8 7.2 %collective-permute-done.9.gates_ref = f32[24,2]{1,0:T(8,128)S(1)} collective-permute-done((f32[24,2]{1,0:T(8,128)S(1)}, f32[24,2]{1,0:T(8,128)S(1)}, u32[]{:S(2)}, u32[]{:S(2)}) %collective-permute-start.9) | collective-permute-done | bytes 224 | tf_op jit(solution)/shard_map/ppermute | solution.py:54
  172.0 14.5 %all-to-all-done.1.rows_ref = bf16[64,4,2048]{2,1,0:T(4,128)(2,1)S(1)} async-done(((bf16[64,4,2048]{2,1,0:T(4,128)(2,1)}), bf16[64,4,2048]{2,1,0:T(4,128)(2,1)S(1)}, u32[]{:S(2)}, u32[]{:S(2)}) %all-to-all-start.1) | async-done | bytes 1048608 | tf_op jit(solution)/shard_map/all_to_all | solution.py:239
  187.0 4.0 %collective-permute-start.10 = (bf16[24,2048]{1,0:T(8,128)(2,1)S(1)}, bf16[24,2048]{1,0:T(8,128)(2,1)S(1)}, u32[]{:S(2)}, u32[]{:S(2)}) collective-permute-start(bf16[24,2048]{1,0:T(8,128)(2,1)S(1)} %shard_map.128), channel_id=1, source_target_pairs={{0,256},{64,320},{128,384},{192,448},{256,0},{320,64},{384,128},{4... | collective-permute-start | bytes 294920 | tf_op jit(solution)/shard_map/ppermute | solution.py:54
  192.4 5.9 %collective-permute-done.10 = bf16[24,2048]{1,0:T(8,128)(2,1)S(1)} collective-permute-done((bf16[24,2048]{1,0:T(8,128)(2,1)S(1)}, bf16[24,2048]{1,0:T(8,128)(2,1)S(1)}, u32[]{:S(2)}, u32[]{:S(2)}) %collective-permute-start.10) | collective-permute-done | bytes 98336 | tf_op jit(solution)/shard_map/ppermute | solution.py:54
  (80 shorter events, 6.2 us)
Async XLA Ops:
  0.6 163.5 %copy-start = (bf16[24,2048]{1,0:T(8,128)(2,1)S(1)}, bf16[24,2048]{1,0:T(8,128)(2,1)}, u32[]{:S(2)}) copy-start(bf16[24,2048]{1,0:T(8,128)(2,1)} %param.17) | copy-start | bytes 294916
  2.5 15.3 %collective-permute-start = (bf16[24,4224]{1,0:T(8,128)(2,1)S(1)}, bf16[24,4224]{1,0:T(8,128)(2,1)S(1)}, u32[]{:S(2)}, u32[]{:S(2)}) collective-permute-start(bf16[24,4224]{1,0:T(8,128)(2,1)S(1)} %fusion.13), channel_id=1, source_target_pairs={{0,256},{64,320},{128,384},{192,448},{256,0},{320,64},{384,128},{4... | collective-permute-start | bytes 608264 | tf_op jit(solution)/shard_map/ppermute | solution.py:54
  18.4 0.9 copy-start.8
  20.6 1.3 copy-start.1
  21.9 20.1 %copy-start.2 = (bf16[1,1024,512]{2,1,0:T(8,128)(2,1)S(1)}, bf16[1,1024,512]{2,1,0:T(8,128)(2,1)}, u32[]{:S(2)}) copy-start(bf16[1,1024,512]{2,1,0:T(8,128)(2,1)} %param.15) | copy-start | bytes 3145732
  21.9 96.5 %all-to-all-start = ((bf16[64,4,4096]{2,1,0:T(4,128)(2,1)}), bf16[64,4,4096]{2,1,0:T(4,128)(2,1)S(1)}, u32[]{:S(2)}, u32[]{:S(2)}) async-start(bf16[64,4,4096]{2,1,0:T(4,128)(2,1)} %copy-done.1), calls=%async_computation | async-start | bytes 4194304 | tf_op jit(solution)/shard_map/all_to_all | solution.py:202
  36.9 70.8 %collective-permute-start.3 = (bf16[4096,128]{1,0:T(8,128)(2,1)}, bf16[4096,128]{1,0:T(8,128)(2,1)S(1)}, u32[]{:S(2)}, u32[]{:S(2)}) collective-permute-start(bf16[4096,128]{1,0:T(8,128)(2,1)} %bitcast.63), channel_id=1, source_target_pairs={{0,128},{64,192},{128,0},{192,64},{256,384},{320,448},{384,256},{4... | collective-permute-start | bytes 3145736 | tf_op jit(solution)/shard_map/ppermute | solution.py:54
  42.1 72.8 %collective-permute-start.7 = (bf16[1024,512]{1,0:T(8,128)(2,1)S(1)}, bf16[1024,512]{1,0:T(8,128)(2,1)}, u32[]{:S(2)}, u32[]{:S(2)}) collective-permute-start(bf16[1024,512]{1,0:T(8,128)(2,1)S(1)} %bitcast.59), channel_id=1, source_target_pairs={{0,384},{64,448},{128,256},{192,320},{256,128},{320,192},{384,0},{... | collective-permute-start | bytes 3145736 | tf_op jit(solution)/shard_map/ppermute | solution.py:54
  107.7 9.7 %collective-permute-start.4 = (bf16[4096,128]{1,0:T(8,128)(2,1)S(1)}, bf16[4096,128]{1,0:T(8,128)(2,1)S(1)}, u32[]{:S(2)}, u32[]{:S(2)}) collective-permute-start(bf16[4096,128]{1,0:T(8,128)(2,1)S(1)} %collective-permute-done.3.left_ref), channel_id=1, source_target_pairs={{0,64},{64,0},{128,192},{192,128},{256,320},{320,256},{384,448},{4... | collective-permute-start | bytes 3145736 | tf_op jit(solution)/shard_map/ppermute | solution.py:54
  109.6 1.0 copy-start.4
  110.6 16.8 %collective-permute-start.1 = (bf16[4096,128]{1,0:T(8,128)(2,1)}, bf16[4096,128]{1,0:T(8,128)(2,1)}, u32[]{:S(2)}, u32[]{:S(2)}) collective-permute-start(bf16[4096,128]{1,0:T(8,128)(2,1)} %bitcast.64), channel_id=1, source_target_pairs={{0,64},{64,0},{128,192},{192,128},{256,320},{320,256},{384,448},{4... | collective-permute-start | bytes 3145736 | tf_op jit(solution)/shard_map/ppermute | solution.py:54
  113.0 20.5 %collective-permute-start.6 = (bf16[1024,512]{1,0:T(8,128)(2,1)S(1)}, bf16[1024,512]{1,0:T(8,128)(2,1)}, u32[]{:S(2)}, u32[]{:S(2)}) collective-permute-start(bf16[1024,512]{1,0:T(8,128)(2,1)S(1)} %bitcast.60), channel_id=1, source_target_pairs={{0,64},{64,0},{128,192},{192,128},{256,320},{320,256},{384,448},{4... | collective-permute-start | bytes 3145736 | tf_op jit(solution)/shard_map/ppermute | solution.py:54
  114.9 18.5 %collective-permute-start.8 = (bf16[1024,512]{1,0:T(8,128)(2,1)}, bf16[1024,512]{1,0:T(8,128)(2,1)}, u32[]{:S(2)}, u32[]{:S(2)}) collective-permute-start(bf16[1024,512]{1,0:T(8,128)(2,1)} %collective-permute-done.7.refs_2_), channel_id=1, source_target_pairs={{0,64},{64,0},{128,192},{192,128},{256,320},{320,256},{384,448},{4... | collective-permute-start | bytes 3145736 | tf_op jit(solution)/shard_map/ppermute | solution.py:54
  117.3 1.0 copy-start.6
  118.4 1.2 copy-start.5
  119.6 1.2 copy-start.7
  120.8 6.6 %copy-start.3 = (bf16[1,4096,128]{2,1,0:T(8,128)(2,1)S(1)}, bf16[1,4096,128]{2,1,0:T(8,128)(2,1)}, u32[]{:S(2)}) copy-start(bf16[1,4096,128]{2,1,0:T(8,128)(2,1)} %param.14) | copy-start | bytes 3145732
  121.6 14.4 %collective-permute-start.5 = (bf16[256,256]{1,0:T(8,128)(2,1)S(1)}, bf16[256,256]{1,0:T(8,128)(2,1)S(1)}, u32[]{:S(2)}, u32[]{:S(2)}) collective-permute-start(bf16[256,256]{1,0:T(8,128)(2,1)S(1)} %shard_map.124.odd_ref), channel_id=1, source_target_pairs={{0,256},{64,320},{128,384},{192,448},{256,0},{320,64},{384,128},{4... | collective-permute-start | bytes 393224 | tf_op jit(solution)/shard_map/ppermute | solution.py:54
  129.5 13.7 %collective-permute-start.2 = (bf16[256,256]{1,0:T(8,128)(2,1)S(1)}, bf16[256,256]{1,0:T(8,128)(2,1)S(1)}, u32[]{:S(2)}, u32[]{:S(2)}) collective-permute-start(bf16[256,256]{1,0:T(8,128)(2,1)S(1)} %shard_map.123.even_ref), channel_id=1, source_target_pairs={{0,256},{64,320},{128,384},{192,448},{256,0},{320,64},{384,128},{4... | collective-permute-start | bytes 393224 | tf_op jit(solution)/shard_map/ppermute | solution.py:54
  146.7 11.8 %copy-start.13 = (s32[24,2]{0,1:T(2,128)S(1)}, s32[24,2]{0,1:T(2,128)}, u32[]{:S(2)}) copy-start(s32[24,2]{0,1:T(2,128)} %param.12) | copy-start | bytes 580
  146.7 11.8 %copy-start.12 = (f32[24,64]{1,0:T(8,128)S(1)}, f32[24,64]{1,0:T(8,128)}, u32[]{:S(2)}) copy-start(f32[24,64]{1,0:T(8,128)} %param.13) | copy-start | bytes 18436
  146.7 16.5 %copy-start.9 = (bf16[1,72,2048]{2,1,0:T(8,128)(2,1)S(1)}, bf16[1,72,2048]{2,1,0:T(8,128)(2,1)}, u32[]{:S(2)}) copy-start(bf16[1,72,2048]{2,1,0:T(8,128)(2,1)} %param.19) | copy-start | bytes 884740
  146.7 17.2 %copy-start.10 = (bf16[1,72,2048]{2,1,0:T(8,128)(2,1)S(1)}, bf16[1,72,2048]{2,1,0:T(8,128)(2,1)}, u32[]{:S(2)}) copy-start(bf16[1,72,2048]{2,1,0:T(8,128)(2,1)} %param.20) | copy-start | bytes 884740
  146.7 17.4 %copy-start.11 = (bf16[24,2048]{1,0:T(8,128)(2,1)S(1)}, bf16[24,2048]{1,0:T(8,128)(2,1)}, u32[]{:S(2)}) copy-start(bf16[24,2048]{1,0:T(8,128)(2,1)} %param.18) | copy-start | bytes 294916
  146.8 17.5 %copy-start.15 = (bf16[24,2048]{1,0:T(8,128)(2,1)S(1)}, bf16[24,2048]{1,0:T(8,128)(2,1)}, u32[]{:S(2)}) copy-start(bf16[24,2048]{1,0:T(8,128)(2,1)} %param.16) | copy-start | bytes 294916
  146.8 39.7 %all-to-all-start.1 = ((bf16[64,4,2048]{2,1,0:T(4,128)(2,1)}), bf16[64,4,2048]{2,1,0:T(4,128)(2,1)S(1)}, u32[]{:S(2)}, u32[]{:S(2)}) async-start(bf16[64,4,2048]{2,1,0:T(4,128)(2,1)} %shard_map.126), calls=%async_computation.1 | async-start | bytes 2097152 | tf_op jit(solution)/shard_map/all_to_all | solution.py:239
  159.1 12.9 %collective-permute-start.9 = (f32[24,2]{1,0:T(8,128)S(1)}, f32[24,2]{1,0:T(8,128)S(1)}, u32[]{:S(2)}, u32[]{:S(2)}) collective-permute-start(f32[24,2]{1,0:T(8,128)S(1)} %fusion.25.gates_ref), channel_id=1, source_target_pairs={{0,256},{64,320},{128,384},{192,448},{256,0},{320,64},{384,128},{4... | collective-permute-start | bytes 584 | tf_op jit(solution)/shard_map/ppermute | solution.py:54
  187.0 11.4 %collective-permute-start.10 = (bf16[24,2048]{1,0:T(8,128)(2,1)S(1)}, bf16[24,2048]{1,0:T(8,128)(2,1)S(1)}, u32[]{:S(2)}, u32[]{:S(2)}) collective-permute-start(bf16[24,2048]{1,0:T(8,128)(2,1)S(1)} %shard_map.128), channel_id=1, source_target_pairs={{0,256},{64,320},{128,384},{192,448},{256,0},{320,64},{384,128},{4... | collective-permute-start | bytes 294920 | tf_op jit(solution)/shard_map/ppermute | solution.py:54
  198.6 0.7 copy-start.14
